TPU v7x, 32 devices: a whole 2x2x4 slice. The times are simulated.
32 devices in a mesh: rep: 4 (over x, core), ep: 4 (over z), grp: 2 (over y).
Axes of the slice: x: 2, y: 2, z: 4, core: 2. Of those that a mesh axis runs over, the one named last changes fastest.
Arguments:
- tokens: bfloat16 [4096, 2048], P(('rep', 'ep', 'grp')), may hold values from -6 to 6
- grad_out: bfloat16 [4096, 2048], P(('rep', 'ep', 'grp')), may hold values from -6 to 6
- expert_ids: int32 [4096, 2], P(('rep', 'ep', 'grp')), may hold values from 0 to 7, as said below
- combine: bfloat16 [4096, 2], P(('rep', 'ep', 'grp')), may hold values from 0.099609375 to 1
- weights: bfloat16 [2048, 3, 7168], P('grp', None, 'ep'), may hold values from -0.125 to 0.125
Outputs:
- grad_tokens: bfloat16 [4096, 2048], P(('rep', 'ep', 'grp'))
- grad_combine: float32 [4096, 2], P(('rep', 'ep', 'grp'))
- grad_weights: float32 [2048, 3, 7168], P(('rep', 'grp'), None, 'ep')
Inputs may be any that keep to these rules, and one draw needn't show every extreme that they name: `expert_ids`: each token names 2 different experts, at most one of them below 1. No expert below 1 is named by more than 4 tokens of one device, and each of them is named by exactly 4 tokens of some device.
All inputs are finite; a program needn't handle non-finite values.
Results may differ from a plain program's by a relative error of at most 0.0085.
Values may be sent and summed in bfloat16 or wider, within the bound.
No kernel may reach another device: no remote copies, remote signals or barrier semaphores. Data moves between devices by JAX's collectives and lax.ppermute only.
A program may use at most 128 MiB of HBM per device.

v0:
```python
import jax
import jax.numpy as jnp
from jax import lax
from jax.sharding import PartitionSpec as P

FLIGHT = 1
CAP = 4


def route_slots(routing, gate_vals, in_flight, capacity):
    experts = jnp.arange(in_flight, dtype=jnp.int32)
    matches = (routing[None, :, :] == experts[:, None, None]).astype(jnp.float32)
    assigned = jnp.sum(matches, axis=2)
    combined = jnp.sum(matches * gate_vals.astype(jnp.float32)[None, :, :], axis=2)
    before = jnp.cumsum(assigned, axis=1) - assigned
    slot_index = jnp.arange(capacity, dtype=jnp.float32)
    slot_map = (before[:, None, :] == slot_index[None, :, None]).astype(jnp.float32) * assigned[
        :, None, :
    ]
    return (matches, combined, slot_map)


def local(tokens, grad_out, expert_ids, combine, weights):
    ep_size = lax.axis_size("ep")
    rep_size = lax.axis_size("rep")
    grp_size = lax.axis_size("grp")
    quarter = ep_size // FLIGHT
    model_width = tokens.shape[1]
    slot_total = ep_size * CAP
    owner_rows = model_width // (rep_size * grp_size)
    highest = lax.Precision.HIGHEST
    matches, combined, slot_map = route_slots(expert_ids, combine, FLIGHT, CAP)
    slot_bf = slot_map.astype(jnp.bfloat16)
    sent_rows = jnp.einsum(
        "fct,td->fcd", slot_bf, tokens, preferred_element_type=jnp.float32
    ).astype(jnp.bfloat16)
    sent_grads = jnp.einsum(
        "fct,td->fcd", slot_bf, grad_out, preferred_element_type=jnp.float32
    ).astype(jnp.bfloat16)
    sent_scale = jnp.einsum("fct,ft->fc", slot_map, combined, precision=highest).astype(
        jnp.bfloat16
    )

    def spread(buffer):
        trailing = buffer.shape[1:]
        widened = jnp.broadcast_to(buffer[:, None], (FLIGHT, quarter) + trailing)
        return widened.reshape((ep_size,) + trailing)

    recv_rows, recv_grads, recv_scale = (
        lax.all_to_all(spread(sent_rows), "ep", split_axis=0, concat_axis=0, tiled=True),
        lax.all_to_all(spread(sent_grads), "ep", split_axis=0, concat_axis=0, tiled=True),
        lax.all_to_all(spread(sent_scale), "ep", split_axis=0, concat_axis=0, tiled=True),
    )
    token_rows = recv_rows.reshape(slot_total, model_width)
    grad_rows = recv_grads.reshape(slot_total, model_width)
    row_scale = recv_scale.reshape(slot_total, 1).astype(jnp.float32)

    def owner_layout(rows_now):
        shaped = rows_now.reshape(slot_total, rep_size, grp_size, owner_rows)
        return jnp.transpose(shaped, (2, 0, 1, 3))

    col_tokens, col_grads = (
        lax.all_to_all(owner_layout(token_rows), "grp", split_axis=0, concat_axis=0, tiled=True),
        lax.all_to_all(owner_layout(grad_rows), "grp", split_axis=0, concat_axis=0, tiled=True),
    )
    col_tokens = col_tokens.reshape(grp_size * slot_total, rep_size * owner_rows)
    col_grads = col_grads.reshape(grp_size * slot_total, rep_size * owner_rows)
    gathered = lax.all_gather(weights, "grp", axis=0, tiled=True)
    gate_up_pre = jnp.einsum(
        "rd,dkh->rkh", token_rows, gathered[:, :2], preferred_element_type=jnp.float32
    )
    down_back = jnp.dot(grad_rows, gathered[:, 2], preferred_element_type=jnp.float32)
    gate_pre = gate_up_pre[:, 0]
    up_pre = gate_up_pre[:, 1]
    sigmoid_gate = jax.nn.sigmoid(gate_pre)
    activated = gate_pre * sigmoid_gate
    hid_value = activated * up_pre
    hid_grad = row_scale * down_back
    grad_gate = (hid_grad * up_pre * sigmoid_gate * (1.0 + gate_pre * (1.0 - sigmoid_gate))).astype(
        jnp.bfloat16
    )
    grad_up = (hid_grad * activated).astype(jnp.bfloat16)
    scaled_hid = (row_scale * hid_value).astype(jnp.bfloat16)
    gate_up_grad = jnp.stack([grad_gate, grad_up], axis=1)
    hidden_all = jnp.stack([grad_gate, grad_up, scaled_hid], axis=1)
    partial_c = jnp.sum(hid_value * down_back, axis=1).astype(jnp.bfloat16)
    partial_x = jnp.einsum(
        "rkh,dkh->rd", gate_up_grad, gathered[:, :2], preferred_element_type=jnp.float32
    )
    back_x, back_c = (
        lax.all_to_all(
            partial_x.astype(jnp.bfloat16).reshape(ep_size, CAP, model_width),
            "ep",
            split_axis=0,
            concat_axis=0,
            tiled=True,
        ),
        lax.all_to_all(
            partial_c.reshape(ep_size, CAP), "ep", split_axis=0, concat_axis=0, tiled=True
        ),
    )
    summed_x = jnp.sum(
        back_x.astype(jnp.float32).reshape(FLIGHT, quarter, CAP, model_width), axis=1
    )
    summed_c = jnp.sum(back_c.astype(jnp.float32).reshape(FLIGHT, quarter, CAP), axis=1)
    grad_tokens = jnp.einsum("fct,fcd->td", slot_map, summed_x, precision=highest).astype(
        jnp.bfloat16
    )
    per_token = jnp.einsum("fct,fc->ft", slot_map, summed_c, precision=highest)
    grad_combine = jnp.sum(matches * per_token[:, :, None], axis=0)
    hidden_grads = lax.all_gather(hidden_all, "grp", axis=0, tiled=True)
    gate_up_term = jnp.einsum(
        "rc,rkh->ckh", col_tokens, hidden_grads[:, :2], preferred_element_type=jnp.float32
    )
    down_term = jnp.einsum(
        "rc,rh->ch", col_grads, hidden_grads[:, 2], preferred_element_type=jnp.float32
    )
    grad_weights = lax.psum_scatter(
        jnp.concatenate([gate_up_term, down_term[:, None, :]], axis=1).astype(jnp.bfloat16),
        "rep",
        scatter_dimension=0,
        tiled=True,
    ).astype(jnp.float32)
    return (grad_tokens, grad_combine, grad_weights)


def solution(mesh):
    in_specs = (
        P(("rep", "ep", "grp"), None),
        P(("rep", "ep", "grp"), None),
        P(("rep", "ep", "grp"), None),
        P(("rep", "ep", "grp"), None),
        P("grp", None, "ep"),
    )
    out_specs = (
        P(("rep", "ep", "grp"), None),
        P(("rep", "ep", "grp"), None),
        P(("rep", "grp"), None, "ep"),
    )
    return jax.shard_map(local, mesh=mesh, in_specs=in_specs, out_specs=out_specs, check_vma=False)
```

profile of v0, /device:TPU:0, one launch (start us, length us, event | category | flops | bytes accessed | tf_op | source)
XLA Modules:
  0.0 396.5 jit_solution(2041849928835757291)
XLA Ops:
  7.3 0.7 all-gather.2.cloned.1.call-update
  8.5 0.6 reshape.246
  9.1 6.3 %all-to-all-start = ((bf16[4,1,4]{2,1,0:T(2,128)(2,1)}), bf16[4,1,4]{2,1,0:T(2,128)(2,1)S(1)}, u32[]{:S(2)}, u32[]{:S(2)}) async-start(bf16[4,1,4]{2,1,0:T(2,128)(2,1)} %reshape.246), calls=%async_computation | async-start | bytes 4096 | tf_op jit(solution)/shard_map/all_to_all | solution.py:52
  15.7 5.3 %all-to-all-done = bf16[4,1,4]{2,1,0:T(2,128)(2,1)S(1)} async-done(((bf16[4,1,4]{2,1,0:T(2,128)(2,1)}), bf16[4,1,4]{2,1,0:T(2,128)(2,1)S(1)}, u32[]{:S(2)}, u32[]{:S(2)}) %all-to-all-start) | async-done | bytes 64 | tf_op jit(solution)/shard_map/all_to_all | solution.py:52
  21.0 0.6 reshape.247
  21.6 3.3 all-to-all-start.1
  25.1 5.5 %all-to-all-done.1 = bf16[4,4,2048]{2,1,0:T(4,128)(2,1)S(1)} async-done(((bf16[4,4,2048]{2,1,0:T(4,128)(2,1)}), bf16[4,4,2048]{2,1,0:T(4,128)(2,1)S(1)}, u32[]{:S(2)}, u32[]{:S(2)}) %all-to-all-start.1) | async-done | bytes 65568 | tf_op jit(solution)/shard_map/all_to_all | solution.py:51
  30.6 0.6 reshape.249
  31.3 3.3 all-to-all-start.2
  34.6 0.7 copy.18
  35.3 5.0 %all-to-all-done.2 = bf16[4,4,2048]{2,1,0:T(4,128)(2,1)S(1)} async-done(((bf16[4,4,2048]{2,1,0:T(4,128)(2,1)}), bf16[4,4,2048]{2,1,0:T(4,128)(2,1)S(1)}, u32[]{:S(2)}, u32[]{:S(2)}) %all-to-all-start.2) | async-done | bytes 65568 | tf_op jit(solution)/shard_map/all_to_all | solution.py:50
  40.3 3.3 all-to-all-start.6
  43.7 0.7 copy.21
  44.3 4.2 %all-to-all-done.6 = bf16[2,16,4,256]{3,2,1,0:T(4,128)(2,1)S(1)} async-done(((bf16[2,16,4,256]{3,2,1,0:T(4,128)(2,1)}), bf16[2,16,4,256]{3,2,1,0:T(4,128)(2,1)S(1)}, u32[]{:S(2)}, u32[]{:S(2)}) %all-to-all-start.6) | async-done | bytes 65568 | tf_op jit(solution)/shard_map/all_to_all | solution.py:64
  48.5 3.3 all-to-all-start.5
  52.1 4.7 %all-to-all-done.5 = bf16[2,16,4,256]{3,2,1,0:T(4,128)(2,1)S(1)} async-done(((bf16[2,16,4,256]{3,2,1,0:T(4,128)(2,1)}), bf16[2,16,4,256]{3,2,1,0:T(4,128)(2,1)S(1)}, u32[]{:S(2)}, u32[]{:S(2)}) %all-to-all-start.5) | async-done | bytes 65568 | tf_op jit(solution)/shard_map/all_to_all | solution.py:63
  56.8 215.1 %all-gather.2.cloned.1.call-done = bf16[2048,3,1792]{2,0,1:T(8,128)(2,1)} async-done(((bf16[1024,3,1792]{2,0,1:T(8,128)(2,1)}), bf16[2048,3,1792]{2,0,1:T(8,128)(2,1)}) %all-gather.2.cloned.1.call-update) | async-done | bytes 22020112 | tf_op jit(solution)/shard_map/all_gather | solution.py:68
  271.9 6.2 %fusion.2 = f32[16,2,1792]{2,0,1:T(8,128)S(1)} fusion(bf16[16,2048,1]{1,0,2:T(8,128)(2,1)S(1)} %reshape.257, bf16[2048,3,1792]{2,0,1:T(8,128)(2,1)} %all-gather.2.cloned.1.call-done), kind=kOutput, calls=%fused_computation.2 | convolution fusion | flops 234881024 | bytes 14974976 | tf_op jit(solution)/shard_map/rd,dkh->rkh/dot_general | solution.py:69
  278.2 4.3 %fusion.27 = (bf16[16,1,1792]{2,0,1:T(8,128)(2,1)S(1)}, bf16[16,1,1792]{2,0,1:T(8,128)(2,1)S(1)}, bf16[16]{0:T(256)(128)(2,1)S(1)}) fusion(f32[16,2,1792]{2,0,1:T(8,128)S(1)} %fusion.2, f32[16]{0:T(128)S(1)} %reshape.254, bf16[16,2048]{1,0:T(8,128)(2,1)S(1)} %reshape.248, bf16[2048,3,1792]{2,0,1:T(8,128)(2,1)} %all-gather.2.cloned.1.call-done), kind=kOutput, calls=%fused_computation.43 | convolution fusion | flops 117927920 | bytes 7749728 | tf_op jit(solution)/shard_map/dot_general | solution.py:72
  282.5 6.6 %all_gather.7 = bf16[32,3,1792]{2,0,1:T(8,128)(2,1)S(1)} all-gather(bf16[16,3,1792]{2,0,1:T(8,128)(2,1)S(1)} %pad_maximum_fusion.1), channel_id=1, replica_groups=mesh['rep'=4,'ep'=4,'grp'=2] {'grp'}, dimensions={0}, use_global_device_ids=true | all-gather | bytes 516096 | tf_op jit(solution)/shard_map/all_gather | solution.py:111
  289.1 1.1 fusion.5
  290.3 2.1 convolution_convert_fusion
  292.4 4.9 %pad_maximum_fusion = bf16[1024,3,1792]{2,0,1:T(8,128)(2,1)} fusion(bf16[1024,1,1792]{2,0,1:T(8,128)(2,1)S(1)} %fusion.5, bf16[1024,2,1792]{2,0,1:T(8,128)(2,1)S(1)} %convolution_convert_fusion), kind=kLoop, calls=%fused_computation.4 | loop fusion | flops 5505024 | bytes 22020096 | tf_op jit(solution)/shard_map/concatenate | solution.py:119
  297.3 7.2 %fusion.9 = bf16[16,2048]{1,0:T(8,128)(2,1)S(1)} fusion(bf16[2048,3,1792]{2,0,1:T(8,128)(2,1)} %all-gather.2.cloned.1.call-done, bf16[16,1,1792]{2,0,1:T(8,128)(2,1)S(1)} %get-tuple-element.6, bf16[16,1,1792]{2,0,1:T(8,128)(2,1)S(1)} %get-tuple-element.5), kind=kOutput, calls=%fused_computation.12 | convolution fusion | flops 234971136 | bytes 14860288 | tf_op jit(solution)/shard_map/rkh,dkh->rd/dot_general | solution.py:87
  304.6 0.7 reshape.251
  305.3 10.0 %all_to_all.37 = bf16[4,1,4]{2,1,0:T(2,128)(2,1)S(1)} all-to-all(bf16[4,1,4]{2,1,0:T(2,128)(2,1)S(1)} %convert_element_type.105), channel_id=1, replica_groups=mesh['rep'=4,'ep'=4,'grp'=2] {'ep'}, dimensions={0} | all-to-all | bytes 64 | tf_op jit(solution)/shard_map/all_to_all | solution.py:98
  315.3 3.3 all-to-all-start.3
  318.7 0.6 broadcast_select_fusion
  319.3 5.0 %all-to-all-done.3 = bf16[4,4,2048]{2,1,0:T(4,128)(2,1)S(1)} async-done(((bf16[4,4,2048]{2,1,0:T(4,128)(2,1)}), bf16[4,4,2048]{2,1,0:T(4,128)(2,1)S(1)}, u32[]{:S(2)}, u32[]{:S(2)}) %all-to-all-start.3) | async-done | bytes 65568 | tf_op jit(solution)/shard_map/all_to_all | solution.py:91
  324.3 1.8 convolution_convert_fusion.2
  326.2 58.8 %reduce-scatter.2.cloned.1.call-done = bf16[256,3,1792]{2,0,1:T(8,128)(2,1)} async-done(((bf16[1024,3,1792]{2,0,1:T(8,128)(2,1)}), bf16[256,3,1792]{2,0,1:T(8,128)(2,1)}) %reduce-scatter.2.cloned.1.call-update) | async-done | bytes 2752528 | tf_op jit(solution)/shard_map/reduce_scatter | solution.py:118
  385.0 4.7 %convert_element_type.103 = f32[256,3,1792]{2,0,1:T(8,128)} convert(bf16[256,3,1792]{2,0,1:T(8,128)(2,1)} %reduce-scatter.2.cloned.1.call-done) | non-fusion elementwise | flops 1376256 | bytes 8257536 | tf_op jit(solution)/shard_map/convert_element_type | solution.py:123
  (35 shorter events, 1.7 us)
Async XLA Ops:
  7.2 8.3 %copy-start = (bf16[128,2048]{1,0:T(8,128)(2,1)S(1)}, bf16[128,2048]{1,0:T(8,128)(2,1)}, u32[]{:S(2)}) copy-start(bf16[128,2048]{1,0:T(8,128)(2,1)} %param.6) | copy-start | bytes 1572868
  7.2 0.8 copy-start.3
  7.2 0.8 copy-start.4
  7.2 17.7 %copy-start.2 = (bf16[128,2048]{1,0:T(8,128)(2,1)S(1)}, bf16[128,2048]{1,0:T(8,128)(2,1)}, u32[]{:S(2)}) copy-start(bf16[128,2048]{1,0:T(8,128)(2,1)} %param.5) | copy-start | bytes 1572868
  7.2 264.7 %all-gather.2.cloned.1.call-start = ((), (), s32[]{:S(2)}) async-start(), calls=%async_computation.8 | async-start | bytes 33030144 | tf_op jit(solution)/shard_map/all_gather | solution.py:68
  9.1 11.8 %all-to-all-start = ((bf16[4,1,4]{2,1,0:T(2,128)(2,1)}), bf16[4,1,4]{2,1,0:T(2,128)(2,1)S(1)}, u32[]{:S(2)}, u32[]{:S(2)}) async-start(bf16[4,1,4]{2,1,0:T(2,128)(2,1)} %reshape.246), calls=%async_computation | async-start | bytes 4096 | tf_op jit(solution)/shard_map/all_to_all | solution.py:52
  21.6 9.0 %all-to-all-start.1 = ((bf16[4,4,2048]{2,1,0:T(4,128)(2,1)}), bf16[4,4,2048]{2,1,0:T(4,128)(2,1)S(1)}, u32[]{:S(2)}, u32[]{:S(2)}) async-start(bf16[4,4,2048]{2,1,0:T(4,128)(2,1)} %reshape.247), calls=%async_computation.1 | async-start | bytes 131072 | tf_op jit(solution)/shard_map/all_to_all | solution.py:51
  31.3 9.0 %all-to-all-start.2 = ((bf16[4,4,2048]{2,1,0:T(4,128)(2,1)}), bf16[4,4,2048]{2,1,0:T(4,128)(2,1)S(1)}, u32[]{:S(2)}, u32[]{:S(2)}) async-start(bf16[4,4,2048]{2,1,0:T(4,128)(2,1)} %reshape.249), calls=%async_computation.2 | async-start | bytes 131072 | tf_op jit(solution)/shard_map/all_to_all | solution.py:50
  40.3 8.2 %all-to-all-start.6 = ((bf16[2,16,4,256]{3,2,1,0:T(4,128)(2,1)}), bf16[2,16,4,256]{3,2,1,0:T(4,128)(2,1)S(1)}, u32[]{:S(2)}, u32[]{:S(2)}) async-start(bf16[2,16,4,256]{3,2,1,0:T(4,128)(2,1)} %copy.18), calls=%async_computation.6 | async-start | bytes 131072 | tf_op jit(solution)/shard_map/all_to_all | solution.py:64
  48.5 8.2 %all-to-all-start.5 = ((bf16[2,16,4,256]{3,2,1,0:T(4,128)(2,1)}), bf16[2,16,4,256]{3,2,1,0:T(4,128)(2,1)S(1)}, u32[]{:S(2)}, u32[]{:S(2)}) async-start(bf16[2,16,4,256]{3,2,1,0:T(4,128)(2,1)} %bitcast.83), calls=%async_computation.5 | async-start | bytes 131072 | tf_op jit(solution)/shard_map/all_to_all | solution.py:63
  51.8 333.1 %reduce-scatter.2.cloned.1.call-start = ((), (), s32[]{:S(2)}) async-start(), calls=%async_computation.9 | async-start | bytes 13762560 | tf_op jit(solution)/shard_map/reduce_scatter | solution.py:118
  297.3 92.4 %copy-start.1 = (bf16[128,2048]{1,0:T(8,128)(2,1)S(1)}, bf16[128,2048]{1,0:T(8,128)(2,1)}, u32[]{:S(2)}) copy-start(bf16[128,2048]{1,0:T(8,128)(2,1)} %param.6) | copy-start | bytes 1572868
  315.3 9.0 %all-to-all-start.3 = ((bf16[4,4,2048]{2,1,0:T(4,128)(2,1)}), bf16[4,4,2048]{2,1,0:T(4,128)(2,1)S(1)}, u32[]{:S(2)}, u32[]{:S(2)}) async-start(bf16[4,4,2048]{2,1,0:T(4,128)(2,1)} %reshape.251), calls=%async_computation.3 | async-start | bytes 131072 | tf_op jit(solution)/shard_map/all_to_all | solution.py:91
Sparse Core Ops, SparseCore 0:
  9.6 262.2 all-gather.1
  297.4 87.5 reduce-scatter.1
where the time goes:
time: 397 us
  waiting for transfers between devices  304 us (77%)
  matrix products  23.4 us (6%)
  starting transfers between devices  22.9 us (6%)
  blocking collectives  16.6 us (4%)
  between operations  14.2 us (4%)
  other arithmetic  10.7 us (3%)
  local copies, waits for them, and re-layouts  4.37 us (1%)
    all_gather x1, waiting for transfers between devices, local(): gathered = lax.all_gather(weights, 'grp', axis=0, tiled=True)  215 us
    reduce_scatter x1, waiting for transfers between devices, local(): lax.psum_scatter(jnp.concatenate([gate_up_term, down_term[:, None, :]], a...  58.8 us
    all_to_all x1, blocking collectives, local(): lax.all_to_all(partial_c.reshape(ep_size, CAP), 'ep', split_axis=0, conca...  9.96 us
  transfers between devices with their start and end apart: 8, of which 8 were waited for; matrix products, arithmetic and copies ran while one was open for 4% of the time, Pallas kernels for 0%

commit v1 on v0

v1 whole, which is shorter than its diff:
```python
import functools

import jax
import jax.numpy as jnp
from jax import lax
from jax.experimental import pallas as pl
from jax.experimental.pallas import tpu as pltpu
from jax.sharding import PartitionSpec as P

CAP = 4
PACK = 2 * CAP
LANES = 128
BF = jnp.bfloat16
F32 = jnp.float32


def tile_of(extent, most):
    for tile in range(most, 0, -LANES):
        if tile % LANES == 0 and extent % tile == 0:
            return tile
    return extent


def iota(shape, axis):
    return lax.broadcasted_iota(jnp.int32, shape, axis)


def slots(ids):
    tokens = ids.shape[1]
    named = jnp.sum((ids == 0).astype(F32), axis=0, keepdims=True)
    earlier = (iota((tokens, tokens), 0) < iota((tokens, tokens), 1)).astype(BF)
    wide = jnp.broadcast_to(named, (PACK, tokens))
    before = jnp.dot(wide.astype(BF), earlier, preferred_element_type=F32)
    slot = (iota((PACK, tokens), 0) % CAP).astype(F32)
    return jnp.where(before == slot, wide, 0.0)


def pack_kernel(ids_ref, comb_ref, tok_ref, out_ref, rows_ref, cols_ref, *, grp_size, owners):
    ids = ids_ref[...]
    both = slots(ids)
    model_width = tok_ref.shape[1]
    tokens = ids.shape[1]
    half = model_width // grp_size
    upper = iota((PACK, tokens), 0) < CAP
    first = jnp.where(upper, both, 0.0).astype(BF)
    second = jnp.where(upper, 0.0, both).astype(BF)
    packed = (
        jnp.dot(first, tok_ref[...], preferred_element_type=F32)
        + jnp.dot(second, out_ref[...], preferred_element_type=F32)
    ).astype(BF)
    chosen = jnp.sum(
        jnp.where(ids == 0, comb_ref[...].astype(F32), 0.0), axis=0, keepdims=True
    )
    scale = jnp.sum(both * chosen, axis=1, keepdims=True)
    scale = jnp.broadcast_to(scale, (PACK, LANES)).astype(BF)
    for peer in range(rows_ref.shape[0]):
        side = peer % grp_size
        rows_ref[peer, :, :half] = packed[:, side * half : (side + 1) * half]
        rows_ref[peer, :, half:] = scale
    width = model_width // owners
    spread = cols_ref.shape[0] // owners
    for owner in range(owners):
        rep, grp = owner // grp_size, owner % grp_size
        for at in range(spread):
            cols_ref[(rep * spread + at) * grp_size + grp] = packed[
                :, owner * width : (owner + 1) * width
            ]


def forward_kernel(recv_ref, w_ref, own_ref, send_ref, scale_ref, rows_ref):
    depth = w_ref.shape[1]

    @pl.when(pl.program_id(0) == 0)
    def _():
        peers = recv_ref.shape[0] // PACK
        block = 8 if peers % 8 == 0 else peers
        many = block * CAP
        row, col = iota((many, block * PACK), 0), iota((many, block * PACK), 1)
        source = row // CAP * PACK + row % CAP
        take_x = (col == source).astype(BF)
        take_y = (col == source + CAP).astype(BF)
        for at in range(peers // block):
            piece = recv_ref[at * block * PACK : (at + 1) * block * PACK, :]
            xr = jnp.dot(take_x, piece, preferred_element_type=F32)
            yr = jnp.dot(take_y, piece[:, :depth], preferred_element_type=F32)
            here = pl.ds(at * many, many)
            rows_ref[0, here, :] = xr[:, :depth].astype(BF)
            rows_ref[1, here, :] = yr.astype(BF)
            scale_ref[here, :] = xr[:, depth:]

    for k in range(3):
        part = jnp.dot(rows_ref[k // 2], w_ref[k], preferred_element_type=F32)
        own_ref[k] = part
        send_ref[k] = part.astype(BF)


def hidden_kernel(own_ref, other_ref, scale_ref, w_ref, hid_ref, back_ref, px_ref, pc_ref):
    step = pl.program_id(0)

    @pl.when(step == 0)
    def _():
        px_ref[...] = jnp.zeros_like(px_ref)
        pc_ref[...] = jnp.zeros_like(pc_ref)

    a = own_ref[0] + other_ref[0].astype(F32)
    b = own_ref[1] + other_ref[1].astype(F32)
    back = own_ref[2] + other_ref[2].astype(F32)
    cr = scale_ref[:, :1]
    sig = jax.nn.sigmoid(a)
    act = a * sig
    h = act * b
    dh = cr * back
    da = (dh * b * sig * (1.0 + a * (1.0 - sig))).astype(BF)
    db = (dh * act).astype(BF)
    hid_ref[0] = da
    hid_ref[1] = db
    hid_ref[2] = (cr * h).astype(BF)
    contract = (((1,), (1,)), ((), ()))
    px_ref[...] += lax.dot_general(
        da, w_ref[0], contract, preferred_element_type=F32
    ) + lax.dot_general(db, w_ref[1], contract, preferred_element_type=F32)
    pc_ref[...] += jnp.sum(h * back, axis=1, keepdims=True)

    @pl.when(step == pl.num_programs(0) - 1)
    def _():
        pairs = px_ref.shape[0] // PACK
        half = px_ref.shape[1] // 2
        low = px_ref[:, :half]
        high = px_ref[:, half:]
        many = px_ref.shape[0]
        upper = iota((many, half), 0) % PACK < CAP
        low_up = pltpu.roll(low, many - CAP, 0)
        high_down = pltpu.roll(high, CAP, 0)
        even = jnp.where(upper, low, high_down)
        odd = jnp.where(upper, low_up, high)
        pc = pc_ref[...]
        pc_up = pltpu.roll(pc, many - CAP, 0)
        for q in range(pairs):
            at = slice(q * PACK, (q + 1) * PACK)
            back_ref[2 * q, :, :half] = even[at].astype(BF)
            back_ref[2 * q, :, half:] = pc[at].astype(BF)
            back_ref[2 * q + 1, :, :half] = odd[at].astype(BF)
            back_ref[2 * q + 1, :, half:] = pc_up[at].astype(BF)


def weight_kernel(order_ref, cols_ref, *refs):
    hid_refs, out_ref, left_ref = refs[:-2], refs[-2], refs[-1]
    members = len(hid_refs)
    many = hid_refs[0].shape[1]

    @pl.when(pl.program_id(0) == 0)
    def _():
        sources = many // CAP
        block = 8 if sources % 8 == 0 else sources
        rows = block * CAP
        row, col = iota((rows, block * PACK), 0), iota((rows, block * PACK), 1)
        source = row // CAP * PACK + row % CAP
        take = [(col == source + k * CAP).astype(BF) for k in range(2)]
        for m in range(members):
            for at in range(sources // block):
                start = order_ref[m] * (sources * PACK) + at * block * PACK
                piece = cols_ref[pl.ds(pl.multiple_of(start, PACK), block * PACK), :]
                for k in range(2):
                    left_ref[k, pl.ds(m * many + at * rows, rows), :] = jnp.dot(
                        take[k], piece, preferred_element_type=F32
                    ).astype(BF)

    contract = (((0,), (0,)), ((), ()))
    for k in range(3):
        right = jnp.concatenate([ref[k] for ref in hid_refs], axis=0)
        out_ref[k] = lax.dot_general(
            left_ref[k // 2], right, contract, preferred_element_type=F32
        )


def token_kernel(ids_ref, recv_ref, tok_ref, comb_ref, *, grp_size):
    ids = ids_ref[...]
    both = slots(ids)
    peers = recv_ref.shape[0]
    tokens = ids.shape[1]
    half = tok_ref.shape[1] // (2 * grp_size)
    upper = iota((PACK, tokens), 0) < CAP
    contract = (((0,), (0,)), ((), ()))
    picks = [
        jnp.where(upper, both, 0.0).astype(BF),
        jnp.where(upper, 0.0, both).astype(BF),
    ]
    for side in range(grp_size):
        total = recv_ref[side].astype(F32)
        for at in range(side + grp_size, peers, grp_size):
            total = total + recv_ref[at].astype(F32)
        if side == 0:
            pc = total[:, half:]
            per = jnp.sum(
                jnp.where(upper, both, 0.0) * pc[:, :1], axis=0, keepdims=True
            )
            comb_ref[...] = jnp.where(ids == 0, per, 0.0)
        rounded = total[:, :half].astype(BF)
        for part in range(2):
            start = (2 * side + part) * half
            tok_ref[:, start : start + half] = lax.dot_general(
                picks[part], rounded, contract, preferred_element_type=F32
            ).astype(BF)


def local(tokens, grad_out, expert_ids, combine, weights):
    ep_size = lax.axis_size("ep")
    rep_size = lax.axis_size("rep")
    grp_size = lax.axis_size("grp")
    token_count, model_width = tokens.shape
    peers = ep_size * grp_size
    many = peers * CAP
    depth, _, hidden = weights.shape
    owners = rep_size * grp_size
    owner_rows = model_width // owners
    side_width = depth + LANES
    vmem = pl.BlockSpec(memory_space=pltpu.VMEM)
    ids = expert_ids.T
    w = jnp.transpose(weights, (1, 0, 2))

    rows, cols = pl.pallas_call(
        functools.partial(pack_kernel, grp_size=grp_size, owners=owners),
        out_shape=(
            jax.ShapeDtypeStruct((peers, PACK, side_width), BF),
            jax.ShapeDtypeStruct((rep_size * peers, PACK, owner_rows), BF),
        ),
        in_specs=[vmem] * 4,
        out_specs=(vmem, vmem),
        name="pack",
    )(ids, combine.T, tokens, grad_out)

    recv = lax.all_to_all(rows, ("ep", "grp"), 0, 0, tiled=True)
    recv = recv.reshape(peers * PACK, side_width)
    col_recv = lax.all_to_all(cols, ("rep", "ep", "grp"), 0, 0, tiled=True)
    col_recv = col_recv.reshape(rep_size * peers * PACK, owner_rows)

    tile = tile_of(hidden, 256)
    steps = hidden // tile
    own, send, scale = pl.pallas_call(
        forward_kernel,
        grid=(steps,),
        out_shape=(
            jax.ShapeDtypeStruct((3, many, hidden), F32),
            jax.ShapeDtypeStruct((3, many, hidden), BF),
            jax.ShapeDtypeStruct((many, LANES), F32),
        ),
        in_specs=[
            pl.BlockSpec((peers * PACK, side_width), lambda i: (0, 0)),
            pl.BlockSpec((3, depth, tile), lambda i: (0, 0, i)),
        ],
        out_specs=(
            pl.BlockSpec((3, many, tile), lambda i: (0, 0, i)),
            pl.BlockSpec((3, many, tile), lambda i: (0, 0, i)),
            pl.BlockSpec((many, LANES), lambda i: (0, 0)),
        ),
        scratch_shapes=[pltpu.VMEM((2, many, depth), BF)],
        name="forward",
    )(recv, w)

    if grp_size == 2:
        other = lax.ppermute(send, "grp", [(0, 1), (1, 0)])
    else:
        other = (lax.psum(send.astype(F32), "grp") - send.astype(F32)).astype(BF)

    hid, back = pl.pallas_call(
        hidden_kernel,
        grid=(steps,),
        out_shape=(
            jax.ShapeDtypeStruct((3, many, hidden), BF),
            jax.ShapeDtypeStruct((peers, PACK, depth // 2 + LANES), BF),
        ),
        in_specs=[
            pl.BlockSpec((3, many, tile), lambda i: (0, 0, i)),
            pl.BlockSpec((3, many, tile), lambda i: (0, 0, i)),
            pl.BlockSpec((many, LANES), lambda i: (0, 0)),
            pl.BlockSpec((2, depth, tile), lambda i: (0, 0, i)),
        ],
        out_specs=(
            pl.BlockSpec((3, many, tile), lambda i: (0, 0, i)),
            pl.BlockSpec((peers, PACK, depth // 2 + LANES), lambda i: (0, 0, 0)),
        ),
        scratch_shapes=[
            pltpu.VMEM((many, depth), F32),
            pltpu.VMEM((many, LANES), F32),
        ],
        name="hidden",
    )(own, other, scale, w)

    back_recv = lax.all_to_all(back, ("ep", "grp"), 0, 0, tiled=True)

    gathered = [hid]
    flips = [0]
    step = rep_size // 2
    while step:
        pairs = [(i, i ^ step) for i in range(rep_size)]
        gathered += [lax.ppermute(piece, "rep", pairs) for piece in gathered]
        flips += [flip ^ step for flip in flips]
        step //= 2
    order = jnp.bitwise_xor(lax.axis_index("rep"), jnp.array(flips, jnp.int32))

    grad_weights = pl.pallas_call(
        weight_kernel,
        grid=(steps,),
        out_shape=jax.ShapeDtypeStruct((3, owner_rows, hidden), F32),
        in_specs=[
            pl.BlockSpec(memory_space=pltpu.SMEM),
            pl.BlockSpec((rep_size * peers * PACK, owner_rows), lambda i: (0, 0)),
        ]
        + [pl.BlockSpec((3, many, tile), lambda i: (0, 0, i))] * rep_size,
        out_specs=pl.BlockSpec((3, owner_rows, tile), lambda i: (0, 0, i)),
        scratch_shapes=[pltpu.VMEM((2, rep_size * many, owner_rows), BF)],
        name="weight",
    )(order, col_recv, *gathered)

    grad_tokens, grad_combine = pl.pallas_call(
        functools.partial(token_kernel, grp_size=grp_size),
        out_shape=(
            jax.ShapeDtypeStruct((token_count, model_width), BF),
            jax.ShapeDtypeStruct((2, token_count), F32),
        ),
        in_specs=[vmem] * 2,
        out_specs=(vmem, vmem),
        name="token",
    )(ids, back_recv)

    return (grad_tokens, grad_combine.T, jnp.transpose(grad_weights, (1, 0, 2)))


def solution(mesh):
    in_specs = (
        P(("rep", "ep", "grp"), None),
        P(("rep", "ep", "grp"), None),
        P(("rep", "ep", "grp"), None),
        P(("rep", "ep", "grp"), None),
        P("grp", None, "ep"),
    )
    out_specs = (
        P(("rep", "ep", "grp"), None),
        P(("rep", "ep", "grp"), None),
        P(("rep", "grp"), None, "ep"),
    )
    return jax.shard_map(local, mesh=mesh, in_specs=in_specs, out_specs=out_specs, check_vma=False)
```

time: 397 us -> 74.3 us (0.19)
  waiting for transfers between devices: 304 us -> 20.4 us
  Pallas kernels: 0 us -> 27.3 us
  matrix products: 23.4 us -> 0 us
  starting transfers between devices: 22.9 us -> 7.87 us
  between operations: 14.2 us -> 0.69 us
  other arithmetic: 10.7 us -> 0.52 us
    all_gather x1 -> x0, waiting for transfers between devices: 215 us -> none  [local(): gathered = lax.all_gather(weights, 'grp', axis=0, tiled=True)]
    reduce_scatter x1 -> x0, waiting for transfers between devices: 58.8 us -> none  [local(): lax.psum_scatter(jnp.concatenate([gate_up_term, down_term[:, None, :]], a...]
    pallas_call x0 -> x5, Pallas kernels: none -> 27.3 us  [the longest x1 8.38 us: local(): pl.pallas_call(forward_kernel, grid=(steps,), out_shape=(jax.ShapeDtypeSt...]
    dot_general x10 -> x0, matrix products: 23.4 us -> none  [the longest x1 7.23 us: local(): jnp.einsum('rkh,dkh->rd', gate_up_grad, gathered[:, :2], preferred_elemen...]
    all_to_all x6 -> x2, waiting for transfers between devices: 29.7 us -> 9.36 us  [the longest x1 5.11 us: local(): col_recv = lax.all_to_all(cols, ('rep', 'ep', 'grp'), 0, 0, tiled=True)]
    all_to_all x6 -> x2, starting transfers between devices: 22.8 us -> 6.04 us  [the longest x1 3.48 us: local(): back_recv = lax.all_to_all(back, ('ep', 'grp'), 0, 0, tiled=True)]
    ppermute x0 -> x4, waiting for transfers between devices: none -> 11 us  [the longest x1 8.25 us: local(): other = lax.ppermute(send, 'grp', [(0, 1), (1, 0)])]
    all_gather x1 -> x0, blocking collectives: 6.61 us -> none  [local(): hidden_grads = lax.all_gather(hidden_all, 'grp', axis=0, tiled=True)]
  transfers between devices with their start and end apart: 8 -> 6, of which waited for: 8 -> 4; matrix products, arithmetic and copies ran while one was open for 4% -> 1% of each run, Pallas kernels for 0% -> 3%
where the time goes in v1:
time: 74.3 us; the launch traced here: 73.2 us
  Pallas kernels  27.3 us (37%)
  waiting for transfers between devices  20.4 us (27%)
  blocking collectives  14.9 us (20%)
  starting transfers between devices  7.87 us (11%)
  local copies, waits for them, and re-layouts  1.62 us (2%)
    all_to_all x1, blocking collectives, local(): recv = lax.all_to_all(rows, ('ep', 'grp'), 0, 0, tiled=True)  14.9 us
    pallas_call x1, Pallas kernels, local(): pl.pallas_call(forward_kernel, grid=(steps,), out_shape=(jax.ShapeDtypeSt...  8.38 us
    ppermute x1, waiting for transfers between devices, local(): other = lax.ppermute(send, 'grp', [(0, 1), (1, 0)])  8.25 us
    pallas_call x1, Pallas kernels, local(): pl.pallas_call(hidden_kernel, grid=(steps,), out_shape=(jax.ShapeDtypeStr...  7.71 us
    pallas_call x1, Pallas kernels, local(): pl.pallas_call(weight_kernel, grid=(steps,), out_shape=jax.ShapeDtypeStru...  6.76 us
    all_to_all x1, waiting for transfers between devices, local(): col_recv = lax.all_to_all(cols, ('rep', 'ep', 'grp'), 0, 0, tiled=True)  5.11 us
    all_to_all x1, waiting for transfers between devices, local(): back_recv = lax.all_to_all(back, ('ep', 'grp'), 0, 0, tiled=True)  4.25 us
    all_to_all x1, starting transfers between devices, local(): back_recv = lax.all_to_all(back, ('ep', 'grp'), 0, 0, tiled=True)  3.48 us
  transfers between devices with their start and end apart: 6, of which 4 were waited for; matrix products, arithmetic and copies ran while one was open for 1% of the time, Pallas kernels for 3%

profile of v1, /device:TPU:0, one launch (start us, length us, event | category | flops | bytes accessed | tf_op | source)
XLA Modules:
  0.0 73.2 jit_solution(11414513780243694936)
XLA Ops:
  0.6 2.3 %pack.1 = (bf16[8,8,1152]{2,1,0:T(8,128)(2,1)}, bf16[32,8,256]{2,1,0:T(8,128)(2,1)}) custom-call(s32[2,128]{1,0:T(2,128)} %bitcast.12, bf16[2,128]{1,0:T(2,128)(2,1)} %bitcast.14, bf16[128,2048]{1,0:T(8,128)(2,1)} %tok_ref.1, bf16[128,2048]{1,0:T(8,128)(2,1)} %out_ref.1), custom_call_target="tpu_custom_call" | custom-call | tf_op jit(solution)/shard_map/pack/pallas_call | solution.py:221
  2.9 14.9 %all_to_all.15 = bf16[8,8,1152]{2,1,0:T(8,128)(2,1)} all-to-all(bf16[8,8,1152]{2,1,0:T(8,128)(2,1)} %get-tuple-element.12), channel_id=1, replica_groups=mesh['rep'=4,'ep'=4,'grp'=2] {'ep','grp'}, dimensions={0} | all-to-all | bytes 294912 | tf_op jit(solution)/shard_map/all_to_all | solution.py:232
  17.8 0.0 copy-start.6
  17.8 8.4 %forward.1 = (f32[3,32,1792]{2,1,0:T(8,128)}, bf16[3,32,1792]{2,1,0:T(8,128)(2,1)}, f32[32,128]{1,0:T(8,128)}) custom-call(bf16[64,1152]{1,0:T(8,128)(2,1)} %bitcast.10, bf16[3,1024,1792]{2,1,0:T(8,128)(2,1)} %bitcast.7), custom_call_target="tpu_custom_call" | custom-call | tf_op jit(solution)/shard_map/forward/pallas_call | solution.py:239
  26.2 0.3 collective-permute-start
  26.5 8.2 %collective-permute-done.other_ref = bf16[3,32,1792]{2,1,0:T(8,128)(2,1)S(1)} collective-permute-done((bf16[3,32,1792]{2,1,0:T(8,128)(2,1)}, bf16[3,32,1792]{2,1,0:T(8,128)(2,1)S(1)}, u32[]{:S(2)}, u32[]{:S(2)}) %collective-permute-start) | collective-permute-done | bytes 344096 | tf_op jit(solution)/shard_map/ppermute | solution.py:261
  34.8 0.0 copy-start.1
  34.8 0.7 copy-done.1
  35.5 7.7 %hidden.1 = (bf16[3,32,1792]{2,1,0:T(8,128)(2,1)}, bf16[8,8,640]{2,1,0:T(8,128)(2,1)}) custom-call(f32[3,32,1792]{2,1,0:T(8,128)} %get-tuple-element.13.own_ref, bf16[3,32,1792]{2,1,0:T(8,128)(2,1)} %copy-done.1, f32[32,128]{1,0:T(8,128)} %get-tuple-element.15.scale_ref, bf16[3,1024,1792]{2,1,0:T(8,128)(2,1)} %bitcast.8), custom_call_target="tpu_custom_call" | custom-call | tf_op jit(solution)/shard_map/hidden/pallas_call | solution.py:265
  43.2 1.5 %collective-permute-start.1 = (bf16[3,32,1792]{2,1,0:T(8,128)(2,1)}, bf16[3,32,1792]{2,1,0:T(8,128)(2,1)S(1)}, u32[]{:S(2)}, u32[]{:S(2)}) collective-permute-start(bf16[3,32,1792]{2,1,0:T(8,128)(2,1)} %get-tuple-element.20.refs_0_), channel_id=1, source_target_pairs={{0,16},{8,24},{16,0},{24,8},{1,17},{9,25},{17,1},{25,9},{2,18},{10... | collective-permute-start | bytes 1032200 | tf_op jit(solution)/shard_map/ppermute | solution.py:296
  44.7 3.5 %all-to-all-start.1 = ((bf16[8,8,640]{2,1,0:T(8,128)(2,1)}), bf16[8,8,640]{2,1,0:T(8,128)(2,1)S(1)}, u32[]{:S(2)}, u32[]{:S(2)}) async-start(bf16[8,8,640]{2,1,0:T(8,128)(2,1)} %get-tuple-element.16), calls=%async_computation.1 | async-start | bytes 163840 | tf_op jit(solution)/shard_map/all_to_all | solution.py:289
  48.2 0.0 collective-permute-start.2
  48.2 2.7 %collective-permute-done.1.refs_1_ = bf16[3,32,1792]{2,1,0:T(8,128)(2,1)S(1)} collective-permute-done((bf16[3,32,1792]{2,1,0:T(8,128)(2,1)}, bf16[3,32,1792]{2,1,0:T(8,128)(2,1)S(1)}, u32[]{:S(2)}, u32[]{:S(2)}) %collective-permute-start.1) | collective-permute-done | bytes 344096 | tf_op jit(solution)/shard_map/ppermute | solution.py:296
  50.9 0.0 copy-start.2
  50.9 0.0 collective-permute-start.3
  50.9 4.3 %all-to-all-done.1.recv_ref = bf16[8,8,640]{2,1,0:T(8,128)(2,1)S(1)} async-done(((bf16[8,8,640]{2,1,0:T(8,128)(2,1)}), bf16[8,8,640]{2,1,0:T(8,128)(2,1)S(1)}, u32[]{:S(2)}, u32[]{:S(2)}) %all-to-all-start.1) | async-done | bytes 81952 | tf_op jit(solution)/shard_map/all_to_all | solution.py:289
  55.2 0.0 copy-start.5
  55.2 2.6 %all-to-all-start.2 = ((bf16[32,8,256]{2,1,0:T(8,128)(2,1)}), bf16[32,8,256]{2,1,0:T(8,128)(2,1)S(1)}, u32[]{:S(2)}, u32[]{:S(2)}) async-start(bf16[32,8,256]{2,1,0:T(8,128)(2,1)} %get-tuple-element.19), calls=%async_computation.2 | async-start | bytes 262144 | tf_op jit(solution)/shard_map/all_to_all | solution.py:234
  57.8 0.0 copy-done.6
  57.8 0.5 broadcast_xor_fusion.order_ref
  58.3 0.0 copy-done.5
  58.3 2.2 %token_.1 = (bf16[128,2048]{1,0:T(8,128)(2,1)}, f32[2,128]{1,0:T(2,128)}) custom-call(s32[2,128]{1,0:T(2,128)} %bitcast.13, bf16[8,8,640]{2,1,0:T(8,128)(2,1)} %copy-done.5), custom_call_target="tpu_custom_call" | custom-call | tf_op jit(solution)/shard_map/token/pallas_call | solution.py:315
  60.5 5.1 %all-to-all-done.2 = bf16[32,8,256]{2,1,0:T(8,128)(2,1)S(1)} async-done(((bf16[32,8,256]{2,1,0:T(8,128)(2,1)}), bf16[32,8,256]{2,1,0:T(8,128)(2,1)S(1)}, u32[]{:S(2)}, u32[]{:S(2)}) %all-to-all-start.2) | async-done | bytes 131104 | tf_op jit(solution)/shard_map/all_to_all | solution.py:234
  65.6 0.0 copy-start
  65.6 0.0 collective-permute-done.2.refs_2_
  65.6 0.0 collective-permute-done.3.refs_3_
  65.6 0.0 copy-start.4
  65.6 0.0 copy-done.2
  65.6 0.6 copy-done
  66.2 0.1 copy-done.3
  66.4 0.1 copy-done.4
  66.5 6.8 %weight.1 = f32[3,256,1792]{2,1,0:T(8,128)} custom-call(s32[4]{0:T(128)} %broadcast_xor_fusion.order_ref, bf16[256,256]{1,0:T(8,128)(2,1)} %bitcast.11, bf16[3,32,1792]{2,1,0:T(8,128)(2,1)} %get-tuple-element.20.refs_0_, bf16[3,32,1792]{2,1,0:T(8,128)(2,1)} %copy-done.2, bf16[3,32,1792]{2,1,0:T(8,128)(2,1)} %copy-done.3, bf16[3,32,1792]{2,1,0:T(8,128)(2,1)} %copy-done.4), custom_call_target="tpu_custom_call" | custom-call | tf_op jit(solution)/shard_map/weight/pallas_call | solution.py:301
  (1 shorter events, 0.0 us)
Async XLA Ops:
  17.8 40.0 %copy-start.6 = (s32[4]{0:T(128)S(1)}, s32[4]{0:T(128)}, u32[]{:S(2)}) copy-start(s32[4]{0:T(128)} %constant.7.clone) | copy-start | bytes 52
  26.2 8.6 %collective-permute-start = (bf16[3,32,1792]{2,1,0:T(8,128)(2,1)}, bf16[3,32,1792]{2,1,0:T(8,128)(2,1)S(1)}, u32[]{:S(2)}, u32[]{:S(2)}) collective-permute-start(bf16[3,32,1792]{2,1,0:T(8,128)(2,1)} %get-tuple-element.14), channel_id=1, source_target_pairs={{0,1},{1,0},{2,3},{3,2},{4,5},{5,4},{6,7},{7,6},{8,9},{9,8},{10,11... | collective-permute-start | bytes 1032200 | tf_op jit(solution)/shard_map/ppermute | solution.py:261
  34.8 0.7 copy-start.1
  43.2 7.7 %collective-permute-start.1 = (bf16[3,32,1792]{2,1,0:T(8,128)(2,1)}, bf16[3,32,1792]{2,1,0:T(8,128)(2,1)S(1)}, u32[]{:S(2)}, u32[]{:S(2)}) collective-permute-start(bf16[3,32,1792]{2,1,0:T(8,128)(2,1)} %get-tuple-element.20.refs_0_), channel_id=1, source_target_pairs={{0,16},{8,24},{16,0},{24,8},{1,17},{9,25},{17,1},{25,9},{2,18},{10... | collective-permute-start | bytes 1032200 | tf_op jit(solution)/shard_map/ppermute | solution.py:296
  44.7 10.5 %all-to-all-start.1 = ((bf16[8,8,640]{2,1,0:T(8,128)(2,1)}), bf16[8,8,640]{2,1,0:T(8,128)(2,1)S(1)}, u32[]{:S(2)}, u32[]{:S(2)}) async-start(bf16[8,8,640]{2,1,0:T(8,128)(2,1)} %get-tuple-element.16), calls=%async_computation.1 | async-start | bytes 163840 | tf_op jit(solution)/shard_map/all_to_all | solution.py:289
  48.2 17.4 %collective-permute-start.2 = (bf16[3,32,1792]{2,1,0:T(8,128)(2,1)}, bf16[3,32,1792]{2,1,0:T(8,128)(2,1)S(1)}, u32[]{:S(2)}, u32[]{:S(2)}) collective-permute-start(bf16[3,32,1792]{2,1,0:T(8,128)(2,1)} %get-tuple-element.20.refs_0_), channel_id=1, source_target_pairs={{0,8},{8,0},{16,24},{24,16},{1,9},{9,1},{17,25},{25,17},{2,10},{10... | collective-permute-start | bytes 1032200 | tf_op jit(solution)/shard_map/ppermute | solution.py:296
  50.9 14.7 %copy-start.2 = (bf16[3,32,1792]{2,1,0:T(8,128)(2,1)}, bf16[3,32,1792]{2,1,0:T(8,128)(2,1)S(1)}, u32[]{:S(2)}) copy-start(bf16[3,32,1792]{2,1,0:T(8,128)(2,1)S(1)} %collective-permute-done.1.refs_1_) | copy-start | bytes 1032196
  50.9 14.6 %collective-permute-start.3 = (bf16[3,32,1792]{2,1,0:T(8,128)(2,1)S(1)}, bf16[3,32,1792]{2,1,0:T(8,128)(2,1)S(1)}, u32[]{:S(2)}, u32[]{:S(2)}) collective-permute-start(bf16[3,32,1792]{2,1,0:T(8,128)(2,1)S(1)} %collective-permute-done.1.refs_1_), channel_id=1, source_target_pairs={{0,8},{8,0},{16,24},{24,16},{1,9},{9,1},{17,25},{25,17},{2,10},{10... | collective-permute-start | bytes 1032200 | tf_op jit(solution)/shard_map/ppermute | solution.py:296
  55.2 3.1 %copy-start.5 = (bf16[8,8,640]{2,1,0:T(8,128)(2,1)}, bf16[8,8,640]{2,1,0:T(8,128)(2,1)S(1)}, u32[]{:S(2)}) copy-start(bf16[8,8,640]{2,1,0:T(8,128)(2,1)S(1)} %all-to-all-done.1.recv_ref) | copy-start | bytes 245764
  55.2 10.4 %all-to-all-start.2 = ((bf16[32,8,256]{2,1,0:T(8,128)(2,1)}), bf16[32,8,256]{2,1,0:T(8,128)(2,1)S(1)}, u32[]{:S(2)}, u32[]{:S(2)}) async-start(bf16[32,8,256]{2,1,0:T(8,128)(2,1)} %get-tuple-element.19), calls=%async_computation.2 | async-start | bytes 262144 | tf_op jit(solution)/shard_map/all_to_all | solution.py:234
  65.6 0.7 copy-start
  65.6 0.8 %copy-start.3 = (bf16[3,32,1792]{2,1,0:T(8,128)(2,1)}, bf16[3,32,1792]{2,1,0:T(8,128)(2,1)S(1)}, u32[]{:S(2)}) copy-start(bf16[3,32,1792]{2,1,0:T(8,128)(2,1)S(1)} %collective-permute-done.2.refs_2_) | copy-start | bytes 1032196
  65.6 0.9 %copy-start.4 = (bf16[3,32,1792]{2,1,0:T(8,128)(2,1)}, bf16[3,32,1792]{2,1,0:T(8,128)(2,1)S(1)}, u32[]{:S(2)}) copy-start(bf16[3,32,1792]{2,1,0:T(8,128)(2,1)S(1)} %collective-permute-done.3.refs_3_) | copy-start | bytes 1032196

commit v2 on v1

v2 whole, which is shorter than its diff:
```python
import functools

import jax
import jax.numpy as jnp
from jax import lax
from jax.experimental import pallas as pl
from jax.experimental.pallas import tpu as pltpu
from jax.sharding import PartitionSpec as P


CAP = 4
PACK = 2 * CAP
LANES = 128
GRANT = 16 << 20
WHOLE = 60 * 1024 * 1024
BF = jnp.bfloat16
F32 = jnp.float32


def tile_of(extent, most):
    for tile in range(most, 0, -LANES):
        if tile % LANES == 0 and extent % tile == 0:
            return tile
    return extent


def cost(flops):
    return pl.CostEstimate(flops=flops, bytes_accessed=0, transcendentals=0)


def iota(shape, axis):
    return lax.broadcasted_iota(jnp.int32, shape, axis)


def slots(ids):
    tokens = ids.shape[1]
    named = jnp.sum((ids == 0).astype(F32), axis=0, keepdims=True)
    earlier = (iota((tokens, tokens), 0) < iota((tokens, tokens), 1)).astype(BF)
    wide = jnp.broadcast_to(named, (PACK, tokens))
    before = jnp.dot(wide.astype(BF), earlier, preferred_element_type=F32)
    slot = (iota((PACK, tokens), 0) % CAP).astype(F32)
    return jnp.where(before == slot, wide, 0.0)


def pack_kernel(*refs, grp_size, owners):
    sources, rows_ref = refs[:4], refs[4]
    held, done = refs[5:9], refs[9]
    loads = [
        pltpu.make_async_copy(source, target, done.at[n])
        for n, (source, target) in enumerate(zip(sources, held))
    ]
    for load in loads:
        load.start()
    for load in loads:
        load.wait()
    ids_ref, comb_ref, tok_ref, out_ref = held
    ids = ids_ref[...]
    both = slots(ids)
    model_width = tok_ref.shape[1]
    tokens = ids.shape[1]
    half = model_width // grp_size
    upper = iota((PACK, tokens), 0) < CAP
    first = jnp.where(upper, both, 0.0).astype(BF)
    second = jnp.where(upper, 0.0, both).astype(BF)
    packed = (
        jnp.dot(first, tok_ref[...], preferred_element_type=F32)
        + jnp.dot(second, out_ref[...], preferred_element_type=F32)
    ).astype(BF)
    chosen = jnp.sum(
        jnp.where(ids == 0, comb_ref[...].astype(F32), 0.0), axis=0, keepdims=True
    )
    scale = jnp.sum(both * chosen, axis=1, keepdims=True)
    scale = jnp.broadcast_to(scale, (PACK, LANES)).astype(BF)
    width = model_width // owners
    for peer in range(rows_ref.shape[0]):
        side = peer % grp_size
        rows_ref[peer, :, :half] = packed[:, side * half : (side + 1) * half]
        rows_ref[peer, :, half : half + LANES] = scale
        for rep in range(owners // grp_size):
            to = half + LANES + rep * width
            start = (rep * grp_size + side) * width
            rows_ref[peer, :, to : to + width] = packed[:, start : start + width]


def forward_kernel(
    recv_ref, far_ref, own_ref, send_ref, scale_ref, cols_ref, near_ref, down_ref, rows_ref, done, *, tile
):
    depth, hidden = far_ref.shape[1:]
    starts = range(0, hidden, tile)
    loads = []
    for n, start in enumerate(starts):
        here = pl.ds(start, tile)
        for k in range(3):
            loads.append(
                pltpu.make_async_copy(
                    far_ref.at[k, :, here],
                    down_ref.at[:, here] if k == 2 else near_ref.at[k, :, here],
                    done.at[3 * n + k],
                )
            )
    for load in loads:
        load.start()
    peers = recv_ref.shape[0] // PACK
    block = 8 if peers % 8 == 0 else peers
    many = block * CAP
    row, col = iota((many, block * PACK), 0), iota((many, block * PACK), 1)
    source = row // CAP * PACK + row % CAP
    take_x = (col == source).astype(BF)
    take_y = (col == source + CAP).astype(BF)
    for at in range(peers // block):
        piece = recv_ref[at * block * PACK : (at + 1) * block * PACK, : depth + LANES]
        xr = jnp.dot(take_x, piece, preferred_element_type=F32)
        yr = jnp.dot(take_y, piece[:, :depth], preferred_element_type=F32)
        here = pl.ds(at * many, many)
        rows_ref[0, here, :] = xr[:, :depth].astype(BF)
        rows_ref[1, here, :] = yr.astype(BF)
        scale_ref[here, :] = xr[:, depth:]
    cols_ref[...] = recv_ref[:, depth + LANES :]
    for n, start in enumerate(starts):
        here = slice(start, start + tile)
        for k in range(3):
            loads[3 * n + k].wait()
            right = down_ref[:, here] if k == 2 else near_ref[k, :, here]
            part = jnp.dot(rows_ref[k // 2], right, preferred_element_type=F32)
            own_ref[k, :, here] = part
            send_ref[k, :, here] = part.astype(BF)


def hidden_kernel(own_ref, other_ref, scale_ref, hid_ref, pc_ref, *, tile):
    cr = scale_ref[:, :1]
    pc = jnp.zeros((scale_ref.shape[0], 1), F32)
    for start in range(0, own_ref.shape[2], tile):
        here = slice(start, start + tile)
        a = own_ref[0, :, here] + other_ref[0, :, here].astype(F32)
        b = own_ref[1, :, here] + other_ref[1, :, here].astype(F32)
        back = own_ref[2, :, here] + other_ref[2, :, here].astype(F32)
        sig = jax.nn.sigmoid(a)
        act = a * sig
        h = act * b
        dh = cr * back
        hid_ref[0, :, here] = (dh * b * sig * (1.0 + a * (1.0 - sig))).astype(BF)
        hid_ref[1, :, here] = (dh * act).astype(BF)
        hid_ref[2, :, here] = (cr * h).astype(BF)
        pc = pc + jnp.sum(h * back, axis=1, keepdims=True)
    pc_ref[...] = jnp.broadcast_to(pc, pc_ref.shape)


def return_kernel(hid_ref, pc_ref, w_ref, back_ref):
    pc = pc_ref[...]
    contract = (((1,), (1,)), ((), ()))
    px = lax.dot_general(
        hid_ref[0], w_ref[0], contract, preferred_element_type=F32
    ) + lax.dot_general(hid_ref[1], w_ref[1], contract, preferred_element_type=F32)
    many = px.shape[0]
    half = px.shape[1] // 2
    low, high = px[:, :half], px[:, half:]
    upper = iota((many, half), 0) % PACK < CAP
    even = jnp.where(upper, low, pltpu.roll(high, CAP, 0))
    odd = jnp.where(upper, pltpu.roll(low, many - CAP, 0), high)
    pc_up = pltpu.roll(pc, many - CAP, 0)
    for q in range(many // PACK):
        at = slice(q * PACK, (q + 1) * PACK)
        back_ref[2 * q, :, :half] = even[at].astype(BF)
        back_ref[2 * q, :, half:] = pc[at].astype(BF)
        back_ref[2 * q + 1, :, :half] = odd[at].astype(BF)
        back_ref[2 * q + 1, :, half:] = pc_up[at].astype(BF)


def turn_kernel(rank_ref, *refs, many):
    cols_refs, (turned_ref, left_ref) = refs[:-2], refs[-2:]
    width = left_ref.shape[2]
    sources = many // CAP
    block = 8 if sources % 8 == 0 else sources
    rows = block * CAP
    row, col = iota((rows, block * PACK), 0), iota((rows, block * PACK), 1)
    source = row // CAP * PACK + row % CAP
    take = [(col == source + k * CAP).astype(BF) for k in range(2)]
    for m, cols_ref in enumerate(cols_refs):
        for at in range(sources // block):
            here = slice(at * block * PACK, (at + 1) * block * PACK)
            piece = cols_ref[here, :width]
            for rep in range(1, cols_ref.shape[1] // width):
                other = cols_ref[here, rep * width : (rep + 1) * width]
                piece = jnp.where(rank_ref[0] == rep, other, piece)
            for k in range(2):
                left_ref[k, pl.ds(m * many + at * rows, rows), :] = jnp.dot(
                    take[k], piece, preferred_element_type=F32
                )
    for k in range(2):
        turned_ref[k] = jnp.transpose(left_ref[k]).astype(BF)


def weight_kernel(turned_ref, *refs, tile):
    hid_refs, (out_ref, made_ref, done) = refs[:-3], refs[-3:]
    tiles = [
        (k, start) for start in range(0, hid_refs[0].shape[2], tile) for k in range(3)
    ]
    copies = [
        pltpu.make_async_copy(
            made_ref.at[k, :, pl.ds(start, tile)],
            out_ref.at[k, :, pl.ds(start, tile)],
            done.at[n],
        )
        for n, (k, start) in enumerate(tiles)
    ]
    for n, (k, start) in enumerate(tiles):
        here = slice(start, start + tile)
        right = jnp.concatenate([ref[k, :, here] for ref in hid_refs], axis=0)
        made_ref[k, :, here] = jnp.dot(
            turned_ref[k // 2], right, preferred_element_type=F32
        )
        if n:
            copies[n - 1].start()
    copies[-1].start()
    for copy in copies:
        copy.wait()


def token_kernel(ids_ref, recv_ref, tok_ref, comb_ref, *, grp_size):
    ids = ids_ref[...]
    both = slots(ids)
    peers = recv_ref.shape[0]
    tokens = ids.shape[1]
    half = tok_ref.shape[1] // (2 * grp_size)
    upper = iota((PACK, tokens), 0) < CAP
    contract = (((0,), (0,)), ((), ()))
    picks = [
        jnp.where(upper, both, 0.0).astype(BF),
        jnp.where(upper, 0.0, both).astype(BF),
    ]
    for side in range(grp_size):
        total = recv_ref[side].astype(F32)
        for at in range(side + grp_size, peers, grp_size):
            total = total + recv_ref[at].astype(F32)
        if side == 0:
            pc = total[:, half:]
            per = jnp.sum(
                jnp.where(upper, both, 0.0) * pc[:, :1], axis=0, keepdims=True
            )
            comb_ref[...] = jnp.where(ids == 0, per, 0.0)
        rounded = total[:, :half].astype(BF)
        for part in range(2):
            start = (2 * side + part) * half
            tok_ref[:, start : start + half] = lax.dot_general(
                picks[part], rounded, contract, preferred_element_type=F32
            ).astype(BF)


def gather(piece, rep_size):
    pieces = [piece]
    step = rep_size // 2
    while step:
        pairs = [(i, i ^ step) for i in range(rep_size)]
        pieces += [lax.ppermute(held, "rep", pairs) for held in pieces]
        step //= 2
    return pieces


def local(tokens, grad_out, expert_ids, combine, weights):
    ep_size = lax.axis_size("ep")
    rep_size = lax.axis_size("rep")
    grp_size = lax.axis_size("grp")
    token_count, model_width = tokens.shape
    peers = ep_size * grp_size
    many = peers * CAP
    depth, _, hidden = weights.shape
    owners = rep_size * grp_size
    owner_rows = model_width // owners
    side_width = depth + LANES + rep_size * owner_rows
    vmem = pl.BlockSpec(memory_space=pltpu.VMEM)
    hbm = pl.BlockSpec(memory_space=pltpu.HBM)
    ids = expert_ids.T
    w = jnp.transpose(weights, (1, 0, 2))

    rank = lax.axis_index("rep").astype(jnp.int32).reshape(1)
    ids, rank = lax.optimization_barrier((ids, rank))
    rows = pl.pallas_call(
        functools.partial(pack_kernel, grp_size=grp_size, owners=owners),
        out_shape=jax.ShapeDtypeStruct((peers, PACK, side_width), BF),
        in_specs=[hbm] * 4,
        out_specs=vmem,
        scratch_shapes=[
            pltpu.VMEM(ids.shape, ids.dtype),
            pltpu.VMEM(ids.shape, combine.dtype),
            pltpu.VMEM(tokens.shape, tokens.dtype),
            pltpu.VMEM(grad_out.shape, grad_out.dtype),
            pltpu.SemaphoreType.DMA((4,)),
        ],
        compiler_params=pltpu.CompilerParams(vmem_limit_bytes=WHOLE),
        cost_estimate=cost(2_000_000_000),
        name="pack",
    )(ids, combine.T, tokens, grad_out)

    recv = lax.all_to_all(rows, ("ep", "grp"), 0, 0, tiled=True)
    recv = recv.reshape(peers * PACK, side_width)

    tile = tile_of(hidden, 256)
    own, send, scale, cols, near = pl.pallas_call(
        functools.partial(forward_kernel, tile=tile),
        out_shape=(
            jax.ShapeDtypeStruct((3, many, hidden), F32),
            jax.ShapeDtypeStruct((3, many, hidden), BF),
            jax.ShapeDtypeStruct((many, LANES), F32),
            jax.ShapeDtypeStruct((peers * PACK, rep_size * owner_rows), BF),
            jax.ShapeDtypeStruct((2, depth, hidden), BF),
        ),
        in_specs=[vmem, hbm],
        out_specs=(vmem,) * 5,
        scratch_shapes=[
            pltpu.VMEM((depth, hidden), BF),
            pltpu.VMEM((2, many, depth), BF),
            pltpu.SemaphoreType.DMA((3 * (hidden // tile),)),
        ],
        compiler_params=pltpu.CompilerParams(vmem_limit_bytes=WHOLE - (20 << 20)),
        cost_estimate=cost(3_000_000_000),
        name="forward",
    )(recv, w)

    gathered_cols = gather(cols, rep_size)
    turned = pl.pallas_call(
        functools.partial(turn_kernel, many=many),
        out_shape=jax.ShapeDtypeStruct((2, owner_rows, rep_size * many), BF),
        in_specs=[pl.BlockSpec(memory_space=pltpu.SMEM)] + [vmem] * rep_size,
        out_specs=vmem,
        scratch_shapes=[pltpu.VMEM((2, rep_size * many, owner_rows), F32)],
        compiler_params=pltpu.CompilerParams(vmem_limit_bytes=GRANT),
        cost_estimate=cost(1_000_000_000),
        name="turn",
    )(rank, *gathered_cols)

    if grp_size == 2:
        other = lax.ppermute(send, "grp", [(0, 1), (1, 0)])
    else:
        other = (lax.psum(send.astype(F32), "grp") - send.astype(F32)).astype(BF)

    other, turned = lax.optimization_barrier((other, turned))

    hid, pc = pl.pallas_call(
        functools.partial(hidden_kernel, tile=tile),
        out_shape=(
            jax.ShapeDtypeStruct((3, many, hidden), BF),
            jax.ShapeDtypeStruct((many, LANES), F32),
        ),
        in_specs=[vmem] * 3,
        out_specs=(vmem,) * 2,
        compiler_params=pltpu.CompilerParams(vmem_limit_bytes=GRANT),
        cost_estimate=cost(1_000_000_000),
        name="hidden",
    )(own, other, scale)

    back = pl.pallas_call(
        return_kernel,
        out_shape=jax.ShapeDtypeStruct((peers, PACK, depth // 2 + LANES), BF),
        in_specs=[vmem] * 3,
        out_specs=vmem,
        compiler_params=pltpu.CompilerParams(vmem_limit_bytes=GRANT),
        cost_estimate=cost(3_000_000_000),
        name="back",
    )(hid, pc, near)

    back_recv = lax.all_to_all(back, ("ep", "grp"), 0, 0, tiled=True)

    gathered = gather(hid, rep_size)
    grad_weights = pl.pallas_call(
        functools.partial(weight_kernel, tile=tile),
        out_shape=jax.ShapeDtypeStruct((3, owner_rows, hidden), F32),
        in_specs=[vmem] * (1 + rep_size),
        out_specs=pl.BlockSpec(memory_space=pl.ANY),
        scratch_shapes=[
            pltpu.VMEM((3, owner_rows, hidden), F32),
            pltpu.SemaphoreType.DMA((3 * (hidden // tile),)),
        ],
        compiler_params=pltpu.CompilerParams(vmem_limit_bytes=GRANT),
        cost_estimate=cost(6_000_000_000),
        name="weight",
    )(turned, *gathered)

    grad_tokens, grad_combine = pl.pallas_call(
        functools.partial(token_kernel, grp_size=grp_size),
        out_shape=(
            jax.ShapeDtypeStruct((token_count, model_width), BF),
            jax.ShapeDtypeStruct((2, token_count), F32),
        ),
        in_specs=[vmem] * 2,
        out_specs=(vmem, vmem),
        compiler_params=pltpu.CompilerParams(vmem_limit_bytes=GRANT),
        cost_estimate=cost(2_000_000_000),
        name="token",
    )(ids, back_recv)

    return (grad_tokens, grad_combine.T, jnp.transpose(grad_weights, (1, 0, 2)))


def solution(mesh):
    in_specs = (
        P(("rep", "ep", "grp"), None),
        P(("rep", "ep", "grp"), None),
        P(("rep", "ep", "grp"), None),
        P(("rep", "ep", "grp"), None),
        P("grp", None, "ep"),
    )
    out_specs = (
        P(("rep", "ep", "grp"), None),
        P(("rep", "ep", "grp"), None),
        P(("rep", "grp"), None, "ep"),
    )
    return jax.shard_map(
        local, mesh=mesh, in_specs=in_specs, out_specs=out_specs, check_vma=False
    )
```

time: 74.3 us -> 63 us (0.85); the launches traced: 73.2 us -> 62.7 us
  blocking collectives: 14.9 us -> 29.7 us
  Pallas kernels: 27.3 us -> 15.7 us
  waiting for transfers between devices: 20.4 us -> 13.8 us
  starting transfers between devices: 7.87 us -> 2.82 us
  local copies, waits for them, and re-layouts: 1.62 us -> 0.01 us
    all_to_all x0 -> x1, blocking collectives: none -> 12.4 us  [local(): back_recv = lax.all_to_all(back, ('ep', 'grp'), 0, 0, tiled=True)]
    pallas_call x3 -> x5, Pallas kernels: 22.8 us -> 12.1 us  [the longest x1 6.58 us: local(): pl.pallas_call(functools.partial(forward_kernel, tile=tile), out_shape=(j...]
    all_to_all x2 -> x0, waiting for transfers between devices: 9.36 us -> none  [the longest x1 5.11 us: local(): col_recv = lax.all_to_all(cols, ('rep', 'ep', 'grp'), 0, 0, tiled=True)]
    ppermute x3 -> x6, waiting for transfers between devices: 2.74 us -> 11.3 us  [gather(): pieces += [lax.ppermute(held, 'rep', pairs) for held in pieces]]
    all_to_all x2 -> x0, starting transfers between devices: 6.04 us -> none  [the longest x1 3.48 us: local(): back_recv = lax.all_to_all(back, ('ep', 'grp'), 0, 0, tiled=True)]
    ppermute x1, waiting for transfers between devices: 8.25 us -> 2.45 us  [local(): other = lax.ppermute(send, 'grp', [(0, 1), (1, 0)])]
    all_to_all x1, blocking collectives: 14.9 us -> 17.4 us  [local(): recv = lax.all_to_all(rows, ('ep', 'grp'), 0, 0, tiled=True)]
    unnamed x14 -> x2, local copies, waits for them, and re-layouts: 1.62 us -> 0.01 us
  transfers between devices with their start and end apart: 6 -> 7, of which waited for: 4 -> 4; matrix products, arithmetic and copies ran while one was open for 1% -> 0% of each run, Pallas kernels for 3% -> 6%
where the time goes in v2:
time: 63 us; the launch traced here: 62.7 us
  blocking collectives  29.7 us (47%)
  Pallas kernels  15.7 us (25%)
  waiting for transfers between devices  13.8 us (22%)
  starting transfers between devices  2.82 us (4%)
  between operations  0.68 us (1%)
    all_to_all x1, blocking collectives, local(): recv = lax.all_to_all(rows, ('ep', 'grp'), 0, 0, tiled=True)  17.4 us
    all_to_all x1, blocking collectives, local(): back_recv = lax.all_to_all(back, ('ep', 'grp'), 0, 0, tiled=True)  12.4 us
    ppermute x6, waiting for transfers between devices, gather(): pieces += [lax.ppermute(held, 'rep', pairs) for held in pieces]  11.3 us
    pallas_call x1, Pallas kernels, local(): pl.pallas_call(functools.partial(forward_kernel, tile=tile), out_shape=(j...  6.58 us
    pallas_call x1, Pallas kernels, local(): pl.pallas_call(functools.partial(weight_kernel, tile=tile), out_shape=jax...  2.83 us
    ppermute x1, waiting for transfers between devices, local(): other = lax.ppermute(send, 'grp', [(0, 1), (1, 0)])  2.45 us
    pallas_call x1, Pallas kernels, local(): pl.pallas_call(functools.partial(pack_kernel, grp_size=grp_size, owners=o...  2.35 us
    pallas_call x1, Pallas kernels, local(): pl.pallas_call(return_kernel, out_shape=jax.ShapeDtypeStruct((peers, PACK...  2.23 us
  transfers between devices with their start and end apart: 7, of which 4 were waited for; matrix products, arithmetic and copies ran while one was open for 0% of the time, Pallas kernels for 6%

profile of v2, /device:TPU:0, one launch (start us, length us, event | category | flops | bytes accessed | tf_op | source)
XLA Modules:
  0.0 62.7 jit_solution(10408055094287350715)
XLA Ops:
  0.6 2.3 %pack.1 = bf16[8,8,2176]{2,1,0:T(8,128)(2,1)} custom-call(s32[2,128]{1,0:T(2,128)} %bitcast.8, bf16[2,128]{1,0:T(2,128)(2,1)} %bitcast.11, bf16[128,2048]{1,0:T(8,128)(2,1)} %refs_2_.1, bf16[128,2048]{1,0:T(8,128)(2,1)} %refs_3_.1), custom_call_target="tpu_custom_call" | custom-call | flops 2000000000 | tf_op jit(solution)/shard_map/pack/pallas_call | solution.py:277
  3.0 17.4 %all_to_all.10 = bf16[8,8,2176]{2,1,0:T(8,128)(2,1)S(1)} all-to-all(bf16[8,8,2176]{2,1,0:T(8,128)(2,1)} %pack.1), channel_id=1, replica_groups=mesh['rep'=4,'ep'=4,'grp'=2] {'ep','grp'}, dimensions={0} | all-to-all | bytes 557056 | tf_op jit(solution)/shard_map/all_to_all | solution.py:294
  20.4 6.6 %forward.1 = (f32[3,32,1792]{2,1,0:T(8,128)S(1)}, bf16[3,32,1792]{2,1,0:T(8,128)(2,1)S(1)}, f32[32,128]{1,0:T(8,128)S(1)}, bf16[64,1024]{1,0:T(8,128)(2,1)S(1)}, bf16[2,1024,1792]{2,1,0:T(8,128)(2,1)S(1)}) custom-call(bf16[64,2176]{1,0:T(8,128)(2,1)S(1)} %bitcast.7, bf16[3,1024,1792]{2,1,0:T(8,128)(2,1)} %bitcast.10), custom_call_target="tpu_custom_call" | custom-call | flops 3000000000 | tf_op jit(solution)/shard_map/forward/pallas_call | solution.py:298
  26.9 1.6 %collective-permute-start.1 = (bf16[64,1024]{1,0:T(8,128)(2,1)S(1)}, bf16[64,1024]{1,0:T(8,128)(2,1)S(1)}, u32[]{:S(2)}, u32[]{:S(2)}) collective-permute-start(bf16[64,1024]{1,0:T(8,128)(2,1)S(1)} %get-tuple-element.20.refs_0_), channel_id=1, source_target_pairs={{0,16},{8,24},{16,0},{24,8},{1,17},{9,25},{17,1},{25,9},{2,18},{10... | collective-permute-start | bytes 393224 | tf_op jit(solution)/shard_map/ppermute | solution.py:254
  28.5 0.6 %collective-permute-start = (bf16[3,32,1792]{2,1,0:T(8,128)(2,1)S(1)}, bf16[3,32,1792]{2,1,0:T(8,128)(2,1)S(1)}, u32[]{:S(2)}, u32[]{:S(2)}) collective-permute-start(bf16[3,32,1792]{2,1,0:T(8,128)(2,1)S(1)} %get-tuple-element.18), channel_id=1, source_target_pairs={{0,1},{1,0},{2,3},{3,2},{4,5},{5,4},{6,7},{7,6},{8,9},{9,8},{10,11... | collective-permute-start | bytes 1032200 | tf_op jit(solution)/shard_map/ppermute | solution.py:332
  29.2 0.0 collective-permute-start.2
  29.2 2.8 %collective-permute-done.1.refs_1_ = bf16[64,1024]{1,0:T(8,128)(2,1)S(1)} collective-permute-done((bf16[64,1024]{1,0:T(8,128)(2,1)S(1)}, bf16[64,1024]{1,0:T(8,128)(2,1)S(1)}, u32[]{:S(2)}, u32[]{:S(2)}) %collective-permute-start.1) | collective-permute-done | bytes 131104 | tf_op jit(solution)/shard_map/ppermute | solution.py:254
  32.0 0.0 collective-permute-start.3
  32.0 0.0 collective-permute-done.2.refs_2_
  32.0 1.3 %collective-permute-done.3.refs_3_ = bf16[64,1024]{1,0:T(8,128)(2,1)S(1)} collective-permute-done((bf16[64,1024]{1,0:T(8,128)(2,1)S(1)}, bf16[64,1024]{1,0:T(8,128)(2,1)S(1)}, u32[]{:S(2)}, u32[]{:S(2)}) %collective-permute-start.3) | collective-permute-done | bytes 131104 | tf_op jit(solution)/shard_map/ppermute | solution.py:254
  33.3 0.2 turn.1.turned_ref
  33.6 2.5 %collective-permute-done.other_ref = bf16[3,32,1792]{2,1,0:T(8,128)(2,1)S(1)} collective-permute-done((bf16[3,32,1792]{2,1,0:T(8,128)(2,1)S(1)}, bf16[3,32,1792]{2,1,0:T(8,128)(2,1)S(1)}, u32[]{:S(2)}, u32[]{:S(2)}) %collective-permute-start) | collective-permute-done | bytes 344096 | tf_op jit(solution)/shard_map/ppermute | solution.py:332
  36.0 0.0 copy-start
  36.0 0.3 hidden.1
  36.3 0.6 collective-permute-start.4
  36.9 0.0 collective-permute-start.5
  36.9 7.1 %collective-permute-done.4.refs_1_ = bf16[3,32,1792]{2,1,0:T(8,128)(2,1)S(1)} collective-permute-done((bf16[3,32,1792]{2,1,0:T(8,128)(2,1)S(1)}, bf16[3,32,1792]{2,1,0:T(8,128)(2,1)S(1)}, u32[]{:S(2)}, u32[]{:S(2)}) %collective-permute-start.4) | collective-permute-done | bytes 344096 | tf_op jit(solution)/shard_map/ppermute | solution.py:254
  44.0 0.0 collective-permute-start.6
  44.0 2.2 %back.1 = bf16[8,8,640]{2,1,0:T(8,128)(2,1)S(1)} custom-call(bf16[3,32,1792]{2,1,0:T(8,128)(2,1)S(1)} %get-tuple-element.23.hid_ref.refs_0_, f32[32,128]{1,0:T(8,128)S(1)} %get-tuple-element.24.pc_ref, bf16[2,1024,1792]{2,1,0:T(8,128)(2,1)S(1)} %get-tuple-element.25.w_ref), custom_call_target="tpu_custom_call" | custom-call | flops 3000000000 | tf_op jit(solution)/shard_map/back/pallas_call | solution.py:351
  46.3 12.4 %all_to_all.11.recv_ref = bf16[8,8,640]{2,1,0:T(8,128)(2,1)S(1)} all-to-all(bf16[8,8,640]{2,1,0:T(8,128)(2,1)S(1)} %back.1), channel_id=1, replica_groups=mesh['rep'=4,'ep'=4,'grp'=2] {'ep','grp'}, dimensions={0} | all-to-all | bytes 163840 | tf_op jit(solution)/shard_map/all_to_all | solution.py:361
  58.6 0.0 copy-done
  58.6 1.3 %token_.1 = (bf16[128,2048]{1,0:T(8,128)(2,1)}, f32[2,128]{1,0:T(2,128)}) custom-call(s32[2,128]{1,0:T(2,128)S(1)} %bitcast.9, bf16[8,8,640]{2,1,0:T(8,128)(2,1)S(1)} %all_to_all.11.recv_ref), custom_call_target="tpu_custom_call" | custom-call | flops 2000000000 | tf_op jit(solution)/shard_map/token/pallas_call | solution.py:378
  59.9 0.0 collective-permute-done.5.refs_2_
  59.9 0.0 collective-permute-done.6.refs_3_
  59.9 2.8 %weight.1 = f32[3,256,1792]{2,1,0:T(8,128)} custom-call(bf16[2,256,128]{2,1,0:T(8,128)(2,1)S(1)} %turn.1.turned_ref, bf16[3,32,1792]{2,1,0:T(8,128)(2,1)S(1)} %get-tuple-element.23.hid_ref.refs_0_, bf16[3,32,1792]{2,1,0:T(8,128)(2,1)S(1)} %collective-permute-done.4.refs_1_, bf16[3,32,1792]{2,1,0:T(8,128)(2,1)S(1)} %collective-permute-done.5.refs_2_, ...), custom_call_target="tpu_custom_call" | custom-call | flops 6000000000 | tf_op jit(solution)/shard_map/weight/pallas_call | solution.py:364
Async XLA Ops:
  26.9 5.0 %collective-permute-start.1 = (bf16[64,1024]{1,0:T(8,128)(2,1)S(1)}, bf16[64,1024]{1,0:T(8,128)(2,1)S(1)}, u32[]{:S(2)}, u32[]{:S(2)}) collective-permute-start(bf16[64,1024]{1,0:T(8,128)(2,1)S(1)} %get-tuple-element.20.refs_0_), channel_id=1, source_target_pairs={{0,16},{8,24},{16,0},{24,8},{1,17},{9,25},{17,1},{25,9},{2,18},{10... | collective-permute-start | bytes 393224 | tf_op jit(solution)/shard_map/ppermute | solution.py:254
  28.5 7.5 %collective-permute-start = (bf16[3,32,1792]{2,1,0:T(8,128)(2,1)S(1)}, bf16[3,32,1792]{2,1,0:T(8,128)(2,1)S(1)}, u32[]{:S(2)}, u32[]{:S(2)}) collective-permute-start(bf16[3,32,1792]{2,1,0:T(8,128)(2,1)S(1)} %get-tuple-element.18), channel_id=1, source_target_pairs={{0,1},{1,0},{2,3},{3,2},{4,5},{5,4},{6,7},{7,6},{8,9},{9,8},{10,11... | collective-permute-start | bytes 1032200 | tf_op jit(solution)/shard_map/ppermute | solution.py:332
  29.2 2.8 %collective-permute-start.2 = (bf16[64,1024]{1,0:T(8,128)(2,1)S(1)}, bf16[64,1024]{1,0:T(8,128)(2,1)S(1)}, u32[]{:S(2)}, u32[]{:S(2)}) collective-permute-start(bf16[64,1024]{1,0:T(8,128)(2,1)S(1)} %get-tuple-element.20.refs_0_), channel_id=1, source_target_pairs={{0,8},{8,0},{16,24},{24,16},{1,9},{9,1},{17,25},{25,17},{2,10},{10... | collective-permute-start | bytes 393224 | tf_op jit(solution)/shard_map/ppermute | solution.py:254
  32.0 1.3 %collective-permute-start.3 = (bf16[64,1024]{1,0:T(8,128)(2,1)S(1)}, bf16[64,1024]{1,0:T(8,128)(2,1)S(1)}, u32[]{:S(2)}, u32[]{:S(2)}) collective-permute-start(bf16[64,1024]{1,0:T(8,128)(2,1)S(1)} %collective-permute-done.1.refs_1_), channel_id=1, source_target_pairs={{0,8},{8,0},{16,24},{24,16},{1,9},{9,1},{17,25},{25,17},{2,10},{10... | collective-permute-start | bytes 393224 | tf_op jit(solution)/shard_map/ppermute | solution.py:254
  36.0 22.6 %copy-start = (s32[128,2]{0,1:T(2,128)S(1)}, s32[128,2]{0,1:T(2,128)}, u32[]{:S(2)}) copy-start(s32[128,2]{0,1:T(2,128)} %param.7) | copy-start | bytes 3076
  36.3 7.7 %collective-permute-start.4 = (bf16[3,32,1792]{2,1,0:T(8,128)(2,1)S(1)}, bf16[3,32,1792]{2,1,0:T(8,128)(2,1)S(1)}, u32[]{:S(2)}, u32[]{:S(2)}) collective-permute-start(bf16[3,32,1792]{2,1,0:T(8,128)(2,1)S(1)} %get-tuple-element.23.hid_ref.refs_0_), channel_id=1, source_target_pairs={{0,16},{8,24},{16,0},{24,8},{1,17},{9,25},{17,1},{25,9},{2,18},{10... | collective-permute-start | bytes 1032200 | tf_op jit(solution)/shard_map/ppermute | solution.py:254
  36.9 23.0 %collective-permute-start.5 = (bf16[3,32,1792]{2,1,0:T(8,128)(2,1)S(1)}, bf16[3,32,1792]{2,1,0:T(8,128)(2,1)S(1)}, u32[]{:S(2)}, u32[]{:S(2)}) collective-permute-start(bf16[3,32,1792]{2,1,0:T(8,128)(2,1)S(1)} %get-tuple-element.23.hid_ref.refs_0_), channel_id=1, source_target_pairs={{0,8},{8,0},{16,24},{24,16},{1,9},{9,1},{17,25},{25,17},{2,10},{10... | collective-permute-start | bytes 1032200 | tf_op jit(solution)/shard_map/ppermute | solution.py:254
  44.0 15.9 %collective-permute-start.6 = (bf16[3,32,1792]{2,1,0:T(8,128)(2,1)S(1)}, bf16[3,32,1792]{2,1,0:T(8,128)(2,1)S(1)}, u32[]{:S(2)}, u32[]{:S(2)}) collective-permute-start(bf16[3,32,1792]{2,1,0:T(8,128)(2,1)S(1)} %collective-permute-done.4.refs_1_), channel_id=1, source_target_pairs={{0,8},{8,0},{16,24},{24,16},{1,9},{9,1},{17,25},{25,17},{2,10},{10... | collective-permute-start | bytes 1032200 | tf_op jit(solution)/shard_map/ppermute | solution.py:254

commit v3 on v2

--- a/solution.py
+++ b/solution.py
@@ -76,64 +76,73 @@
         side = peer % grp_size
         rows_ref[peer, :, :half] = packed[:, side * half : (side + 1) * half]
         rows_ref[peer, :, half : half + LANES] = scale
-        for rep in range(owners // grp_size):
+        for rep in range(owners // grp_size if rows_ref.shape[2] > half + LANES else 0):
             to = half + LANES + rep * width
             start = (rep * grp_size + side) * width
             rows_ref[peer, :, to : to + width] = packed[:, start : start + width]
 
 
-def forward_kernel(
-    recv_ref, far_ref, own_ref, send_ref, scale_ref, cols_ref, near_ref, down_ref, rows_ref, done, *, tile
-):
-    depth, hidden = far_ref.shape[1:]
-    starts = range(0, hidden, tile)
+def select_rows(recv_ref, first, depth, pick):
+    peers = recv_ref.shape[0] // PACK
+    block = 8 if peers % 8 == 0 else peers
+    many = block * CAP
+    row, col = iota((many, block * PACK), 0), iota((many, block * PACK), 1)
+    take = (col == row // CAP * PACK + row % CAP + pick * CAP).astype(BF)
+    for at in range(peers // block):
+        piece = recv_ref[at * block * PACK : (at + 1) * block * PACK, first : first + depth]
+        yield pl.ds(at * many, many), jnp.dot(take, piece, preferred_element_type=F32)
+
+
+def forward_kernel(recv_ref, far_ref, *refs, cuts):
+    own_ref, scale_ref, near_ref = refs[:3]
+    send_refs = refs[3 : 3 + len(cuts)]
+    cols_refs, (down_ref, rows_ref, done) = refs[3 + len(cuts) : -3], refs[-3:]
+    depth = far_ref.shape[1]
+    piece = tile_of(depth, 256)
+    pieces = [slice(at, at + piece) for at in range(0, depth, piece)]
     loads = []
-    for n, start in enumerate(starts):
-        here = pl.ds(start, tile)
+    for n, here in enumerate(pieces):
         for k in range(3):
+            target = down_ref if k == 2 else near_ref.at[k]
             loads.append(
                 pltpu.make_async_copy(
-                    far_ref.at[k, :, here],
-                    down_ref.at[:, here] if k == 2 else near_ref.at[k, :, here],
-                    done.at[3 * n + k],
+                    far_ref.at[k, here], target.at[here], done.at[3 * n + k]
                 )
             )
     for load in loads:
         load.start()
-    peers = recv_ref.shape[0] // PACK
-    block = 8 if peers % 8 == 0 else peers
-    many = block * CAP
-    row, col = iota((many, block * PACK), 0), iota((many, block * PACK), 1)
-    source = row // CAP * PACK + row % CAP
-    take_x = (col == source).astype(BF)
-    take_y = (col == source + CAP).astype(BF)
-    for at in range(peers // block):
-        piece = recv_ref[at * block * PACK : (at + 1) * block * PACK, : depth + LANES]
-        xr = jnp.dot(take_x, piece, preferred_element_type=F32)
-        yr = jnp.dot(take_y, piece[:, :depth], preferred_element_type=F32)
-        here = pl.ds(at * many, many)
+    for here, xr in select_rows(recv_ref, 0, depth + LANES, 0):
         rows_ref[0, here, :] = xr[:, :depth].astype(BF)
+        scale_ref[here, :] = xr[:, depth:]
+    for here, yr in select_rows(recv_ref, 0, depth, 1):
         rows_ref[1, here, :] = yr.astype(BF)
-        scale_ref[here, :] = xr[:, depth:]
-    cols_ref[...] = recv_ref[:, depth + LANES :]
-    for n, start in enumerate(starts):
-        here = slice(start, start + tile)
+    for cols_ref in cols_refs:
+        cols_ref[...] = recv_ref[:, depth + LANES :]
+    for n, here in enumerate(pieces):
+        last = n == len(pieces) - 1
         for k in range(3):
             loads[3 * n + k].wait()
-            right = down_ref[:, here] if k == 2 else near_ref[k, :, here]
-            part = jnp.dot(rows_ref[k // 2], right, preferred_element_type=F32)
-            own_ref[k, :, here] = part
-            send_ref[k, :, here] = part.astype(BF)
-
-
-def hidden_kernel(own_ref, other_ref, scale_ref, hid_ref, pc_ref, *, tile):
+            right_ref = down_ref if k == 2 else near_ref.at[k]
+            for cut, send_ref in zip(cuts, send_refs):
+                part = jnp.dot(
+                    rows_ref[k // 2, :, here], right_ref[here, cut], preferred_element_type=F32
+                )
+                if n:
+                    part = part + own_ref[k, :, cut]
+                own_ref[k, :, cut] = part
+                if last:
+                    send_ref[k] = part.astype(BF)
+
+
+def hidden_kernel(own_ref, other_ref, scale_ref, hid_ref, pc_ref, *, cut, tile):
     cr = scale_ref[:, :1]
     pc = jnp.zeros((scale_ref.shape[0], 1), F32)
-    for start in range(0, own_ref.shape[2], tile):
+    for start in range(0, hid_ref.shape[2], tile):
         here = slice(start, start + tile)
-        a = own_ref[0, :, here] + other_ref[0, :, here].astype(F32)
-        b = own_ref[1, :, here] + other_ref[1, :, here].astype(F32)
-        back = own_ref[2, :, here] + other_ref[2, :, here].astype(F32)
+        mine = slice(cut.start + start, cut.start + start + tile)
+        a = own_ref[0, :, mine] + other_ref[0, :, here].astype(F32)
+        b = own_ref[1, :, mine] + other_ref[1, :, here].astype(F32)
+        back = own_ref[2, :, mine] + other_ref[2, :, here].astype(F32)
         sig = jax.nn.sigmoid(a)
         act = a * sig
         h = act * b
@@ -145,12 +154,20 @@
     pc_ref[...] = jnp.broadcast_to(pc, pc_ref.shape)
 
 
-def return_kernel(hid_ref, pc_ref, w_ref, back_ref):
-    pc = pc_ref[...]
+def return_kernel(hid_ref, pc_ref, near_ref, *refs, cut, last):
     contract = (((1,), (1,)), ((), ()))
     px = lax.dot_general(
-        hid_ref[0], w_ref[0], contract, preferred_element_type=F32
-    ) + lax.dot_general(hid_ref[1], w_ref[1], contract, preferred_element_type=F32)
+        hid_ref[0], near_ref[0, :, cut], contract, preferred_element_type=F32
+    ) + lax.dot_general(hid_ref[1], near_ref[1, :, cut], contract, preferred_element_type=F32)
+    pc = pc_ref[...]
+    if cut.start:
+        px = px + refs[0][...]
+        pc = pc + refs[1][...]
+    if not last:
+        refs[-2][...] = px
+        refs[-1][...] = pc
+        return
+    back_ref = refs[-1]
     many = px.shape[0]
     half = px.shape[1] // 2
     low, high = px[:, :half], px[:, half:]
@@ -166,6 +183,22 @@
         back_ref[2 * q + 1, :, half:] = pc_up[at].astype(BF)
 
 
+def split_kernel(rep_ref, grp_ref, near_ref, far_ref, keep_ref, give_ref, *, width):
+    blocks = keep_ref.shape[1] // width
+    rep_high, grp = rep_ref[0] // blocks, grp_ref[0]
+
+    def owned(ref, at, side):
+        start = (2 * at + side) * width
+        return ref[:, start : start + width]
+
+    for at in range(blocks):
+        mine = jnp.where(grp == 0, owned(near_ref, at, 0), owned(near_ref, at, 1))
+        theirs = jnp.where(grp == 0, owned(far_ref, at, 0), owned(far_ref, at, 1))
+        here = slice(at * width, (at + 1) * width)
+        keep_ref[:, here] = jnp.where(rep_high == grp, mine, theirs)
+        give_ref[:, here] = jnp.where(rep_high == grp, theirs, mine)
+
+
 def turn_kernel(rank_ref, *refs, many):
     cols_refs, (turned_ref, left_ref) = refs[:-2], refs[-2:]
     width = left_ref.shape[2]
@@ -179,9 +212,10 @@
         for at in range(sources // block):
             here = slice(at * block * PACK, (at + 1) * block * PACK)
             piece = cols_ref[here, :width]
-            for rep in range(1, cols_ref.shape[1] // width):
+            blocks = cols_ref.shape[1] // width
+            for rep in range(1, blocks):
                 other = cols_ref[here, rep * width : (rep + 1) * width]
-                piece = jnp.where(rank_ref[0] == rep, other, piece)
+                piece = jnp.where(rank_ref[0] % blocks == rep, other, piece)
             for k in range(2):
                 left_ref[k, pl.ds(m * many + at * rows, rows), :] = jnp.dot(
                     take[k], piece, preferred_element_type=F32
@@ -190,23 +224,24 @@
         turned_ref[k] = jnp.transpose(left_ref[k]).astype(BF)
 
 
-def weight_kernel(turned_ref, *refs, tile):
+def weight_kernel(turned_ref, *refs, cuts, tile):
     hid_refs, (out_ref, made_ref, done) = refs[:-3], refs[-3:]
-    tiles = [
-        (k, start) for start in range(0, hid_refs[0].shape[2], tile) for k in range(3)
-    ]
+    members = len(hid_refs) // len(cuts)
+    tiles = []
+    for c, cut in enumerate(cuts):
+        pieces = hid_refs[c * members : (c + 1) * members]
+        for start in range(0, cut.stop - cut.start, tile):
+            tiles += [(k, cut.start + start, start, pieces) for k in range(3)]
     copies = [
         pltpu.make_async_copy(
-            made_ref.at[k, :, pl.ds(start, tile)],
-            out_ref.at[k, :, pl.ds(start, tile)],
-            done.at[n],
+            made_ref.at[k, :, pl.ds(to, tile)], out_ref.at[k, :, pl.ds(to, tile)], done.at[n]
         )
-        for n, (k, start) in enumerate(tiles)
+        for n, (k, to, _, _) in enumerate(tiles)
     ]
-    for n, (k, start) in enumerate(tiles):
+    for n, (k, to, start, pieces) in enumerate(tiles):
         here = slice(start, start + tile)
-        right = jnp.concatenate([ref[k, :, here] for ref in hid_refs], axis=0)
-        made_ref[k, :, here] = jnp.dot(
+        right = jnp.concatenate([ref[k, :, here] for ref in pieces], axis=0)
+        made_ref[k, :, to : to + tile] = jnp.dot(
             turned_ref[k // 2], right, preferred_element_type=F32
         )
         if n:
@@ -246,12 +281,13 @@
             ).astype(BF)
 
 
-def gather(piece, rep_size):
+def gather(piece, rep_size, give=None):
     pieces = [piece]
     step = rep_size // 2
     while step:
         pairs = [(i, i ^ step) for i in range(rep_size)]
-        pieces += [lax.ppermute(held, "rep", pairs) for held in pieces]
+        sent = [give] if give is not None and len(pieces) == 1 else pieces
+        pieces = pieces + [lax.ppermute(held, "rep", pairs) for held in sent]
         step //= 2
     return pieces
 
@@ -266,14 +302,16 @@
     depth, _, hidden = weights.shape
     owners = rep_size * grp_size
     owner_rows = model_width // owners
-    side_width = depth + LANES + rep_size * owner_rows
+    paired = grp_size == 2 and rep_size % 4 == 0
+    side_width = depth + LANES + (0 if paired else rep_size * owner_rows)
     vmem = pl.BlockSpec(memory_space=pltpu.VMEM)
     hbm = pl.BlockSpec(memory_space=pltpu.HBM)
     ids = expert_ids.T
     w = jnp.transpose(weights, (1, 0, 2))
 
-    rank = lax.axis_index("rep").astype(jnp.int32).reshape(1)
-    ids, rank = lax.optimization_barrier((ids, rank))
+    rep = lax.axis_index("rep").astype(jnp.int32).reshape(1)
+    grp = lax.axis_index("grp").astype(jnp.int32).reshape(1)
+    ids, rep, grp = lax.optimization_barrier((ids, rep, grp))
     rows = pl.pallas_call(
         functools.partial(pack_kernel, grp_size=grp_size, owners=owners),
         out_shape=jax.ShapeDtypeStruct((peers, PACK, side_width), BF),
@@ -294,29 +332,62 @@
     recv = lax.all_to_all(rows, ("ep", "grp"), 0, 0, tiled=True)
     recv = recv.reshape(peers * PACK, side_width)
 
+    if paired:
+        far_recv = lax.ppermute(recv, "grp", [(0, 1), (1, 0)])
+
     tile = tile_of(hidden, 256)
-    own, send, scale, cols, near = pl.pallas_call(
-        functools.partial(forward_kernel, tile=tile),
+    middle = -(-hidden // (2 * tile)) * tile
+    cuts = [slice(0, hidden)]
+    if middle < hidden:
+        cuts = [slice(0, middle), slice(middle, hidden)]
+    widths = [cut.stop - cut.start for cut in cuts]
+    own, scale, near, *sends = pl.pallas_call(
+        functools.partial(forward_kernel, cuts=cuts),
         out_shape=(
             jax.ShapeDtypeStruct((3, many, hidden), F32),
-            jax.ShapeDtypeStruct((3, many, hidden), BF),
             jax.ShapeDtypeStruct((many, LANES), F32),
-            jax.ShapeDtypeStruct((peers * PACK, rep_size * owner_rows), BF),
             jax.ShapeDtypeStruct((2, depth, hidden), BF),
+            *(jax.ShapeDtypeStruct((3, many, width), BF) for width in widths),
+            *(
+                jax.ShapeDtypeStruct((peers * PACK, rep_size * owner_rows), BF)
+                for _ in range(0 if paired else 1)
+            ),
         ),
         in_specs=[vmem, hbm],
-        out_specs=(vmem,) * 5,
+        out_specs=(vmem,) * (3 + len(cuts) + (0 if paired else 1)),
         scratch_shapes=[
             pltpu.VMEM((depth, hidden), BF),
             pltpu.VMEM((2, many, depth), BF),
-            pltpu.SemaphoreType.DMA((3 * (hidden // tile),)),
+            pltpu.SemaphoreType.DMA((3 * (depth // tile_of(depth, 256)),)),
         ],
         compiler_params=pltpu.CompilerParams(vmem_limit_bytes=WHOLE - (20 << 20)),
         cost_estimate=cost(3_000_000_000),
         name="forward",
     )(recv, w)
 
-    gathered_cols = gather(cols, rep_size)
+    others = []
+    for c in range(len(cuts)):
+        send = sends[c]
+        if grp_size == 2:
+            others.append(lax.ppermute(send, "grp", [(0, 1), (1, 0)]))
+        else:
+            total = lax.psum(send.astype(F32), "grp")
+            others.append((total - send.astype(F32)).astype(BF))
+
+    if paired:
+        side = (rep_size // 2) * owner_rows
+        keep, give = pl.pallas_call(
+            functools.partial(split_kernel, width=owner_rows),
+            out_shape=(jax.ShapeDtypeStruct((peers * PACK, side), BF),) * 2,
+            in_specs=[pl.BlockSpec(memory_space=pltpu.SMEM)] * 2 + [vmem] * 2,
+            out_specs=(vmem,) * 2,
+            compiler_params=pltpu.CompilerParams(vmem_limit_bytes=GRANT),
+            cost_estimate=cost(500_000_000),
+            name="split",
+        )(rep, grp, recv, far_recv)
+        gathered_cols = gather(keep, rep_size, give)
+    else:
+        gathered_cols = gather(sends[-1], rep_size)
     turned = pl.pallas_call(
         functools.partial(turn_kernel, many=many),
         out_shape=jax.ShapeDtypeStruct((2, owner_rows, rep_size * many), BF),
@@ -324,47 +395,49 @@
         out_specs=vmem,
         scratch_shapes=[pltpu.VMEM((2, rep_size * many, owner_rows), F32)],
         compiler_params=pltpu.CompilerParams(vmem_limit_bytes=GRANT),
-        cost_estimate=cost(1_000_000_000),
+        cost_estimate=cost(500_000_000),
         name="turn",
-    )(rank, *gathered_cols)
-
-    if grp_size == 2:
-        other = lax.ppermute(send, "grp", [(0, 1), (1, 0)])
-    else:
-        other = (lax.psum(send.astype(F32), "grp") - send.astype(F32)).astype(BF)
-
-    other, turned = lax.optimization_barrier((other, turned))
-
-    hid, pc = pl.pallas_call(
-        functools.partial(hidden_kernel, tile=tile),
-        out_shape=(
-            jax.ShapeDtypeStruct((3, many, hidden), BF),
-            jax.ShapeDtypeStruct((many, LANES), F32),
-        ),
-        in_specs=[vmem] * 3,
-        out_specs=(vmem,) * 2,
-        compiler_params=pltpu.CompilerParams(vmem_limit_bytes=GRANT),
-        cost_estimate=cost(1_000_000_000),
-        name="hidden",
-    )(own, other, scale)
-
-    back = pl.pallas_call(
-        return_kernel,
-        out_shape=jax.ShapeDtypeStruct((peers, PACK, depth // 2 + LANES), BF),
-        in_specs=[vmem] * 3,
-        out_specs=vmem,
-        compiler_params=pltpu.CompilerParams(vmem_limit_bytes=GRANT),
-        cost_estimate=cost(3_000_000_000),
-        name="back",
-    )(hid, pc, near)
+    )(rep, *gathered_cols)
+    others[-1], turned = lax.optimization_barrier((others[-1], turned))
+
+    gathered = []
+    back = []
+    for c, cut in enumerate(cuts):
+        last = c == len(cuts) - 1
+        hid, pc = pl.pallas_call(
+            functools.partial(hidden_kernel, cut=cut, tile=tile),
+            out_shape=(
+                jax.ShapeDtypeStruct((3, many, widths[c]), BF),
+                jax.ShapeDtypeStruct((many, LANES), F32),
+            ),
+            in_specs=[vmem] * 3,
+            out_specs=(vmem,) * 2,
+            compiler_params=pltpu.CompilerParams(vmem_limit_bytes=GRANT),
+            cost_estimate=cost(1_000_000_000),
+        )(own, others[c], scale)
+        if last:
+            shapes = jax.ShapeDtypeStruct((peers, PACK, depth // 2 + LANES), BF)
+        else:
+            shapes = (
+                jax.ShapeDtypeStruct((many, depth), F32),
+                jax.ShapeDtypeStruct((many, LANES), F32),
+            )
+        back = pl.pallas_call(
+            functools.partial(return_kernel, cut=cut, last=last),
+            out_shape=shapes,
+            in_specs=[vmem] * (3 + len(back)),
+            out_specs=vmem if last else (vmem,) * 2,
+            compiler_params=pltpu.CompilerParams(vmem_limit_bytes=GRANT),
+            cost_estimate=cost(3_000_000_000),
+        )(hid, pc, near, *back)
+        gathered += gather(hid, rep_size)
 
     back_recv = lax.all_to_all(back, ("ep", "grp"), 0, 0, tiled=True)
 
-    gathered = gather(hid, rep_size)
     grad_weights = pl.pallas_call(
-        functools.partial(weight_kernel, tile=tile),
+        functools.partial(weight_kernel, cuts=cuts, tile=tile),
         out_shape=jax.ShapeDtypeStruct((3, owner_rows, hidden), F32),
-        in_specs=[vmem] * (1 + rep_size),
+        in_specs=[vmem] * (1 + len(gathered)),
         out_specs=pl.BlockSpec(memory_space=pl.ANY),
         scratch_shapes=[
             pltpu.VMEM((3, owner_rows, hidden), F32),

time: 63 us -> 57 us (0.905)
  blocking collectives: 29.7 us -> 14.8 us
  starting transfers between devices: 2.82 us -> 11 us
  waiting for transfers between devices: 13.8 us -> 15.6 us
  Pallas kernels: 15.7 us -> 14.5 us
    all_to_all x1 -> x0, blocking collectives: 12.4 us -> none  [local(): back_recv = lax.all_to_all(back, ('ep', 'grp'), 0, 0, tiled=True)]
    all_to_all x0 -> x1, waiting for transfers between devices: none -> 5.98 us  [local(): back_recv = lax.all_to_all(back, ('ep', 'grp'), 0, 0, tiled=True)]
    ppermute x7 -> x12, starting transfers between devices: 2.82 us -> 7.54 us  [the longest x9 5.12 us: gather(): pieces = pieces + [lax.ppermute(held, 'rep', pairs) for held in sent]]
    ppermute x7 -> x12, waiting for transfers between devices: 13.8 us -> 9.62 us  [the longest x1 7.59 us: local(): far_recv = lax.ppermute(recv, 'grp', [(0, 1), (1, 0)])]
    all_to_all x0 -> x1, starting transfers between devices: none -> 3.48 us  [local(): back_recv = lax.all_to_all(back, ('ep', 'grp'), 0, 0, tiled=True)]
    all_to_all x1, blocking collectives: 17.4 us -> 14.8 us  [local(): recv = lax.all_to_all(rows, ('ep', 'grp'), 0, 0, tiled=True)]
    pallas_call x4 -> x7, Pallas kernels: 11.9 us -> 10.7 us  [the longest x1 4.58 us: local(): pl.pallas_call(functools.partial(forward_kernel, cuts=cuts), out_shape=(j...]
  transfers between devices with their start and end apart: 7 -> 13, of which waited for: 4 -> 3; matrix products, arithmetic and copies ran while one was open for 0% -> 0% of each run, Pallas kernels for 6% -> 8%
where the time goes in v3:
time: 57 us; the launch traced here: 56.7 us
  waiting for transfers between devices  15.6 us (27%)
  blocking collectives  14.8 us (26%)
  Pallas kernels  14.5 us (25%)
  starting transfers between devices  11 us (19%)
  between operations  0.74 us (1%)
    all_to_all x1, blocking collectives, local(): recv = lax.all_to_all(rows, ('ep', 'grp'), 0, 0, tiled=True)  14.8 us
    ppermute x1, waiting for transfers between devices, local(): far_recv = lax.ppermute(recv, 'grp', [(0, 1), (1, 0)])  7.59 us
    all_to_all x1, waiting for transfers between devices, local(): back_recv = lax.all_to_all(back, ('ep', 'grp'), 0, 0, tiled=True)  5.98 us
    ppermute x9, starting transfers between devices, gather(): pieces = pieces + [lax.ppermute(held, 'rep', pairs) for held in sent]  5.12 us
    pallas_call x1, Pallas kernels, local(): pl.pallas_call(functools.partial(forward_kernel, cuts=cuts), out_shape=(j...  4.58 us
    all_to_all x1, starting transfers between devices, local(): back_recv = lax.all_to_all(back, ('ep', 'grp'), 0, 0, tiled=True)  3.48 us
    pallas_call x2, Pallas kernels, local(): pl.pallas_call(functools.partial(return_kernel, cut=cut, last=last), out_...  2.97 us
    pallas_call x1, Pallas kernels, local(): pl.pallas_call(functools.partial(weight_kernel, cuts=cuts, tile=tile), ou...  2.84 us
  transfers between devices with their start and end apart: 13, of which 3 were waited for; matrix products, arithmetic and copies ran while one was open for 0% of the time, Pallas kernels for 8%

profile of v3, /device:TPU:0, one launch (start us, length us, event | category | flops | bytes accessed | tf_op | source)
XLA Modules:
  0.0 56.7 jit_solution(14537222847807226165)
XLA Ops:
  0.6 2.3 %pack.1 = bf16[8,8,1152]{2,1,0:T(8,128)(2,1)} custom-call(s32[2,128]{1,0:T(2,128)} %bitcast.11, bf16[2,128]{1,0:T(2,128)(2,1)} %bitcast.14, bf16[128,2048]{1,0:T(8,128)(2,1)} %refs_2_.1, bf16[128,2048]{1,0:T(8,128)(2,1)} %refs_3_.1), custom_call_target="tpu_custom_call" | custom-call | flops 2000000000 | tf_op jit(solution)/shard_map/pack/pallas_call | solution.py:315
  2.9 14.8 %all_to_all.10 = bf16[8,8,1152]{2,1,0:T(8,128)(2,1)S(1)} all-to-all(bf16[8,8,1152]{2,1,0:T(8,128)(2,1)} %pack.1), channel_id=1, replica_groups=mesh['rep'=4,'ep'=4,'grp'=2] {'ep','grp'}, dimensions={0} | all-to-all | bytes 294912 | tf_op jit(solution)/shard_map/all_to_all | solution.py:332
  17.7 4.6 %forward.1 = (f32[3,32,1792]{2,1,0:T(8,128)S(1)}, f32[32,128]{1,0:T(8,128)S(1)}, bf16[2,1024,1792]{2,1,0:T(8,128)(2,1)S(1)}, bf16[3,32,1024]{2,1,0:T(8,128)(2,1)S(1)}, bf16[3,32,768]{2,1,0:T(8,128)(2,1)S(1)}) custom-call(bf16[64,1152]{1,0:T(8,128)(2,1)S(1)} %bitcast.8, bf16[3,1024,1792]{2,1,0:T(8,128)(2,1)} %bitcast.13), custom_call_target="tpu_custom_call" | custom-call | flops 3000000000 | tf_op jit(solution)/shard_map/forward/pallas_call | solution.py:344
  22.3 0.4 collective-permute-start.5
  22.7 1.7 %collective-permute-start.1 = (bf16[64,1152]{1,0:T(8,128)(2,1)S(1)}, bf16[64,1152]{1,0:T(8,128)(2,1)S(1)}, u32[]{:S(2)}, u32[]{:S(2)}) collective-permute-start(bf16[64,1152]{1,0:T(8,128)(2,1)S(1)} %bitcast.9), channel_id=1, source_target_pairs={{0,1},{1,0},{2,3},{3,2},{4,5},{5,4},{6,7},{7,6},{8,9},{9,8},{10,11... | collective-permute-start | bytes 442376 | tf_op jit(solution)/shard_map/ppermute | solution.py:336
  24.4 0.3 collective-permute-start
  24.7 7.6 %collective-permute-done.1.far_ref = bf16[64,1152]{1,0:T(8,128)(2,1)S(1)} collective-permute-done((bf16[64,1152]{1,0:T(8,128)(2,1)S(1)}, bf16[64,1152]{1,0:T(8,128)(2,1)S(1)}, u32[]{:S(2)}, u32[]{:S(2)}) %collective-permute-start.1) | collective-permute-done | bytes 147488 | tf_op jit(solution)/shard_map/ppermute | solution.py:336
  32.3 1.6 %collective-permute-start.2 = (bf16[64,512]{1,0:T(8,128)(2,1)S(1)}, bf16[64,512]{1,0:T(8,128)(2,1)S(1)}, u32[]{:S(2)}, u32[]{:S(2)}) collective-permute-start(bf16[64,512]{1,0:T(8,128)(2,1)S(1)} %get-tuple-element.29), channel_id=1, source_target_pairs={{0,16},{8,24},{16,0},{24,8},{1,17},{9,25},{17,1},{25,9},{2,18},{10... | collective-permute-start | bytes 196616 | tf_op jit(solution)/shard_map/ppermute | solution.py:290
  33.9 0.0 collective-permute-start.3
  33.9 0.2 shard_map.77
  34.1 0.6 %collective-permute-start.6 = (bf16[3,32,1024]{2,1,0:T(8,128)(2,1)S(1)}, bf16[3,32,1024]{2,1,0:T(8,128)(2,1)S(1)}, u32[]{:S(2)}, u32[]{:S(2)}) collective-permute-start(bf16[3,32,1024]{2,1,0:T(8,128)(2,1)S(1)} %get-tuple-element.36.hid_ref.refs_0_), channel_id=1, source_target_pairs={{0,16},{8,24},{16,0},{24,8},{1,17},{9,25},{17,1},{25,9},{2,18},{10... | collective-permute-start | bytes 589832 | tf_op jit(solution)/shard_map/ppermute | solution.py:290
  34.7 2.0 %collective-permute-done.2.refs_1_ = bf16[64,512]{1,0:T(8,128)(2,1)S(1)} collective-permute-done((bf16[64,512]{1,0:T(8,128)(2,1)S(1)}, bf16[64,512]{1,0:T(8,128)(2,1)S(1)}, u32[]{:S(2)}, u32[]{:S(2)}) %collective-permute-start.2) | collective-permute-done | bytes 65568 | tf_op jit(solution)/shard_map/ppermute | solution.py:290
  36.7 0.0 collective-permute-start.4
  36.7 1.3 %shard_map.78 = (f32[32,1024]{1,0:T(8,128)S(1)}, f32[32,128]{1,0:T(8,128)S(1)}) custom-call(bf16[3,32,1024]{2,1,0:T(8,128)(2,1)S(1)} %get-tuple-element.36.hid_ref.refs_0_, f32[32,128]{1,0:T(8,128)S(1)} %get-tuple-element.37.pc_ref, bf16[2,1024,1792]{2,1,0:T(8,128)(2,1)S(1)} %get-tuple-element.34.near_ref), custom_call_target="tpu_custom_call" | custom-call | flops 3000000000 | tf_op jit(solution)/shard_map/pallas_call | solution.py:425
  38.0 0.0 collective-permute-done.4.refs_3_
  38.0 0.2 turn.1.turned_ref
  38.3 0.0 copy-start
  38.3 0.1 shard_map.76
  38.4 1.9 %collective-permute-start.9 = (bf16[3,32,768]{2,1,0:T(8,128)(2,1)S(1)}, bf16[3,32,768]{2,1,0:T(8,128)(2,1)S(1)}, u32[]{:S(2)}, u32[]{:S(2)}) collective-permute-start(bf16[3,32,768]{2,1,0:T(8,128)(2,1)S(1)} %get-tuple-element.32.hid_ref.refs_4_), channel_id=1, source_target_pairs={{0,16},{8,24},{16,0},{24,8},{1,17},{9,25},{17,1},{25,9},{2,18},{10... | collective-permute-start | bytes 442376 | tf_op jit(solution)/shard_map/ppermute | solution.py:290
  40.4 1.7 %shard_map.79 = bf16[8,8,640]{2,1,0:T(8,128)(2,1)} custom-call(bf16[3,32,768]{2,1,0:T(8,128)(2,1)S(1)} %get-tuple-element.32.hid_ref.refs_4_, f32[32,128]{1,0:T(8,128)S(1)} %get-tuple-element.33.pc_ref, bf16[2,1024,1792]{2,1,0:T(8,128)(2,1)S(1)} %get-tuple-element.34.near_ref, f32[32,1024]{1,0:T(8,128)S(1)} %get-tuple-element.38.refs_0_, ...), custom_call_target="tpu_custom_call" | custom-call | flops 3000000000 | tf_op jit(solution)/shard_map/pallas_call | solution.py:425
  42.0 3.5 %all-to-all-start.1 = ((bf16[8,8,640]{2,1,0:T(8,128)(2,1)}), bf16[8,8,640]{2,1,0:T(8,128)(2,1)S(1)}, u32[]{:S(2)}, u32[]{:S(2)}) async-start(bf16[8,8,640]{2,1,0:T(8,128)(2,1)} %shard_map.79), calls=%async_computation.1 | async-start | bytes 163840 | tf_op jit(solution)/shard_map/all_to_all | solution.py:435
  45.5 0.2 collective-permute-start.7
  45.7 0.0 collective-permute-done.6.refs_1_
  45.7 0.3 collective-permute-start.8
  46.0 0.2 collective-permute-start.10
  46.2 0.0 collective-permute-done.9.refs_5_
  46.2 0.3 collective-permute-start.11
  46.5 6.0 %all-to-all-done.1.recv_ref = bf16[8,8,640]{2,1,0:T(8,128)(2,1)S(1)} async-done(((bf16[8,8,640]{2,1,0:T(8,128)(2,1)}), bf16[8,8,640]{2,1,0:T(8,128)(2,1)S(1)}, u32[]{:S(2)}, u32[]{:S(2)}) %all-to-all-start.1) | async-done | bytes 81952 | tf_op jit(solution)/shard_map/all_to_all | solution.py:435
  52.5 1.3 %token_.1 = (bf16[128,2048]{1,0:T(8,128)(2,1)}, f32[2,128]{1,0:T(2,128)}) custom-call(s32[2,128]{1,0:T(2,128)S(1)} %bitcast.12, bf16[8,8,640]{2,1,0:T(8,128)(2,1)S(1)} %all-to-all-done.1.recv_ref), custom_call_target="tpu_custom_call" | custom-call | flops 2000000000 | tf_op jit(solution)/shard_map/token/pallas_call | solution.py:451
  53.8 0.0 collective-permute-done.7.refs_2_
  53.8 0.0 collective-permute-done.10.refs_6_
  53.8 2.8 %weight.1 = f32[3,256,1792]{2,1,0:T(8,128)} custom-call(bf16[2,256,128]{2,1,0:T(8,128)(2,1)S(1)} %turn.1.turned_ref, bf16[3,32,1024]{2,1,0:T(8,128)(2,1)S(1)} %get-tuple-element.36.hid_ref.refs_0_, bf16[3,32,1024]{2,1,0:T(8,128)(2,1)S(1)} %collective-permute-done.6.refs_1_, bf16[3,32,1024]{2,1,0:T(8,128)(2,1)S(1)} %collective-permute-done.7.refs_2_, ...), custom_call_target="tpu_custom_call" | custom-call | flops 6000000000 | tf_op jit(solution)/shard_map/weight/pallas_call | solution.py:437
  (7 shorter events, 0.0 us)
Async XLA Ops:
  22.3 11.6 %collective-permute-start.5 = (bf16[3,32,1024]{2,1,0:T(8,128)(2,1)S(1)}, bf16[3,32,1024]{2,1,0:T(8,128)(2,1)S(1)}, u32[]{:S(2)}, u32[]{:S(2)}) collective-permute-start(bf16[3,32,1024]{2,1,0:T(8,128)(2,1)S(1)} %get-tuple-element.35), channel_id=1, source_target_pairs={{0,1},{1,0},{2,3},{3,2},{4,5},{5,4},{6,7},{7,6},{8,9},{9,8},{10,11... | collective-permute-start | bytes 589832 | tf_op jit(solution)/shard_map/ppermute | solution.py:372
  22.7 9.6 %collective-permute-start.1 = (bf16[64,1152]{1,0:T(8,128)(2,1)S(1)}, bf16[64,1152]{1,0:T(8,128)(2,1)S(1)}, u32[]{:S(2)}, u32[]{:S(2)}) collective-permute-start(bf16[64,1152]{1,0:T(8,128)(2,1)S(1)} %bitcast.9), channel_id=1, source_target_pairs={{0,1},{1,0},{2,3},{3,2},{4,5},{5,4},{6,7},{7,6},{8,9},{9,8},{10,11... | collective-permute-start | bytes 442376 | tf_op jit(solution)/shard_map/ppermute | solution.py:336
  24.4 13.9 %collective-permute-start = (bf16[3,32,768]{2,1,0:T(8,128)(2,1)S(1)}, bf16[3,32,768]{2,1,0:T(8,128)(2,1)S(1)}, u32[]{:S(2)}, u32[]{:S(2)}) collective-permute-start(bf16[3,32,768]{2,1,0:T(8,128)(2,1)S(1)} %get-tuple-element.25), channel_id=1, source_target_pairs={{0,1},{1,0},{2,3},{3,2},{4,5},{5,4},{6,7},{7,6},{8,9},{9,8},{10,11... | collective-permute-start | bytes 442376 | tf_op jit(solution)/shard_map/ppermute | solution.py:372
  32.3 4.3 %collective-permute-start.2 = (bf16[64,512]{1,0:T(8,128)(2,1)S(1)}, bf16[64,512]{1,0:T(8,128)(2,1)S(1)}, u32[]{:S(2)}, u32[]{:S(2)}) collective-permute-start(bf16[64,512]{1,0:T(8,128)(2,1)S(1)} %get-tuple-element.29), channel_id=1, source_target_pairs={{0,16},{8,24},{16,0},{24,8},{1,17},{9,25},{17,1},{25,9},{2,18},{10... | collective-permute-start | bytes 196616 | tf_op jit(solution)/shard_map/ppermute | solution.py:290
  33.9 4.1 %collective-permute-start.3 = (bf16[64,512]{1,0:T(8,128)(2,1)S(1)}, bf16[64,512]{1,0:T(8,128)(2,1)S(1)}, u32[]{:S(2)}, u32[]{:S(2)}) collective-permute-start(bf16[64,512]{1,0:T(8,128)(2,1)S(1)} %get-tuple-element.28.refs_0_), channel_id=1, source_target_pairs={{0,8},{8,0},{16,24},{24,16},{1,9},{9,1},{17,25},{25,17},{2,10},{10... | collective-permute-start | bytes 196616 | tf_op jit(solution)/shard_map/ppermute | solution.py:290
  34.1 11.6 %collective-permute-start.6 = (bf16[3,32,1024]{2,1,0:T(8,128)(2,1)S(1)}, bf16[3,32,1024]{2,1,0:T(8,128)(2,1)S(1)}, u32[]{:S(2)}, u32[]{:S(2)}) collective-permute-start(bf16[3,32,1024]{2,1,0:T(8,128)(2,1)S(1)} %get-tuple-element.36.hid_ref.refs_0_), channel_id=1, source_target_pairs={{0,16},{8,24},{16,0},{24,8},{1,17},{9,25},{17,1},{25,9},{2,18},{10... | collective-permute-start | bytes 589832 | tf_op jit(solution)/shard_map/ppermute | solution.py:290
  36.7 1.3 %collective-permute-start.4 = (bf16[64,512]{1,0:T(8,128)(2,1)S(1)}, bf16[64,512]{1,0:T(8,128)(2,1)S(1)}, u32[]{:S(2)}, u32[]{:S(2)}) collective-permute-start(bf16[64,512]{1,0:T(8,128)(2,1)S(1)} %collective-permute-done.2.refs_1_), channel_id=1, source_target_pairs={{0,8},{8,0},{16,24},{24,16},{1,9},{9,1},{17,25},{25,17},{2,10},{10... | collective-permute-start | bytes 196616 | tf_op jit(solution)/shard_map/ppermute | solution.py:290
  38.3 14.3 %copy-start = (s32[128,2]{0,1:T(2,128)S(1)}, s32[128,2]{0,1:T(2,128)}, u32[]{:S(2)}) copy-start(s32[128,2]{0,1:T(2,128)} %param.7) | copy-start | bytes 3076
  38.4 7.8 %collective-permute-start.9 = (bf16[3,32,768]{2,1,0:T(8,128)(2,1)S(1)}, bf16[3,32,768]{2,1,0:T(8,128)(2,1)S(1)}, u32[]{:S(2)}, u32[]{:S(2)}) collective-permute-start(bf16[3,32,768]{2,1,0:T(8,128)(2,1)S(1)} %get-tuple-element.32.hid_ref.refs_4_), channel_id=1, source_target_pairs={{0,16},{8,24},{16,0},{24,8},{1,17},{9,25},{17,1},{25,9},{2,18},{10... | collective-permute-start | bytes 442376 | tf_op jit(solution)/shard_map/ppermute | solution.py:290
  42.0 10.5 %all-to-all-start.1 = ((bf16[8,8,640]{2,1,0:T(8,128)(2,1)}), bf16[8,8,640]{2,1,0:T(8,128)(2,1)S(1)}, u32[]{:S(2)}, u32[]{:S(2)}) async-start(bf16[8,8,640]{2,1,0:T(8,128)(2,1)} %shard_map.79), calls=%async_computation.1 | async-start | bytes 163840 | tf_op jit(solution)/shard_map/all_to_all | solution.py:435
  45.5 8.3 %collective-permute-start.7 = (bf16[3,32,1024]{2,1,0:T(8,128)(2,1)S(1)}, bf16[3,32,1024]{2,1,0:T(8,128)(2,1)S(1)}, u32[]{:S(2)}, u32[]{:S(2)}) collective-permute-start(bf16[3,32,1024]{2,1,0:T(8,128)(2,1)S(1)} %get-tuple-element.36.hid_ref.refs_0_), channel_id=1, source_target_pairs={{0,8},{8,0},{16,24},{24,16},{1,9},{9,1},{17,25},{25,17},{2,10},{10... | collective-permute-start | bytes 589832 | tf_op jit(solution)/shard_map/ppermute | solution.py:290
  45.7 8.1 %collective-permute-start.8 = (bf16[3,32,1024]{2,1,0:T(8,128)(2,1)S(1)}, bf16[3,32,1024]{2,1,0:T(8,128)(2,1)S(1)}, u32[]{:S(2)}, u32[]{:S(2)}) collective-permute-start(bf16[3,32,1024]{2,1,0:T(8,128)(2,1)S(1)} %collective-permute-done.6.refs_1_), channel_id=1, source_target_pairs={{0,8},{8,0},{16,24},{24,16},{1,9},{9,1},{17,25},{25,17},{2,10},{10... | collective-permute-start | bytes 589832 | tf_op jit(solution)/shard_map/ppermute | solution.py:290
  46.0 7.8 %collective-permute-start.10 = (bf16[3,32,768]{2,1,0:T(8,128)(2,1)S(1)}, bf16[3,32,768]{2,1,0:T(8,128)(2,1)S(1)}, u32[]{:S(2)}, u32[]{:S(2)}) collective-permute-start(bf16[3,32,768]{2,1,0:T(8,128)(2,1)S(1)} %get-tuple-element.32.hid_ref.refs_4_), channel_id=1, source_target_pairs={{0,8},{8,0},{16,24},{24,16},{1,9},{9,1},{17,25},{25,17},{2,10},{10... | collective-permute-start | bytes 442376 | tf_op jit(solution)/shard_map/ppermute | solution.py:290
  46.2 7.6 %collective-permute-start.11 = (bf16[3,32,768]{2,1,0:T(8,128)(2,1)S(1)}, bf16[3,32,768]{2,1,0:T(8,128)(2,1)S(1)}, u32[]{:S(2)}, u32[]{:S(2)}) collective-permute-start(bf16[3,32,768]{2,1,0:T(8,128)(2,1)S(1)} %collective-permute-done.9.refs_5_), channel_id=1, source_target_pairs={{0,8},{8,0},{16,24},{24,16},{1,9},{9,1},{17,25},{25,17},{2,10},{10... | collective-permute-start | bytes 442376 | tf_op jit(solution)/shard_map/ppermute | solution.py:290

commit v4 on v3

v4 whole, which is shorter than its diff:
```python
import functools

import jax
import jax.numpy as jnp
from jax import lax
from jax.experimental import pallas as pl
from jax.experimental.pallas import tpu as pltpu
from jax.sharding import PartitionSpec as P


CAP = 4
PACK = 2 * CAP
LANES = 128
GRANT = 16 << 20
WHOLE = 60 * 1024 * 1024
BF = jnp.bfloat16
F32 = jnp.float32


def tile_of(extent, most):
    for tile in range(most, 0, -LANES):
        if tile % LANES == 0 and extent % tile == 0:
            return tile
    return extent


def cost(flops):
    return pl.CostEstimate(flops=flops, bytes_accessed=0, transcendentals=0)


def iota(shape, axis):
    return lax.broadcasted_iota(jnp.int32, shape, axis)


def slots(ids):
    tokens = ids.shape[1]
    named = jnp.sum((ids == 0).astype(F32), axis=0, keepdims=True)
    earlier = (iota((tokens, tokens), 0) < iota((tokens, tokens), 1)).astype(BF)
    wide = jnp.broadcast_to(named, (PACK, tokens))
    before = jnp.dot(wide.astype(BF), earlier, preferred_element_type=F32)
    slot = (iota((PACK, tokens), 0) % CAP).astype(F32)
    return jnp.where(before == slot, wide, 0.0)


def pack_kernel(*refs, grp_size, owners):
    sources, (rows_ref, slots_ref) = refs[:4], refs[4:6]
    held, done = refs[6:10], refs[10]
    loads = [
        pltpu.make_async_copy(source, target, done.at[n])
        for n, (source, target) in enumerate(zip(sources, held))
    ]
    for load in loads:
        load.start()
    for load in loads[:2]:
        load.wait()
    ids_ref, comb_ref, tok_ref, out_ref = held
    ids = ids_ref[...]
    both = slots(ids)
    slots_ref[...] = both
    model_width = tok_ref.shape[1]
    tokens = ids.shape[1]
    half = model_width // grp_size
    upper = iota((PACK, tokens), 0) < CAP
    first = jnp.where(upper, both, 0.0).astype(BF)
    second = jnp.where(upper, 0.0, both).astype(BF)
    chosen = jnp.sum(
        jnp.where(ids == 0, comb_ref[...].astype(F32), 0.0), axis=0, keepdims=True
    )
    scale = jnp.sum(both * chosen, axis=1, keepdims=True)
    scale = jnp.broadcast_to(scale, (PACK, LANES)).astype(BF)
    for load in loads[2:]:
        load.wait()
    packed = (
        jnp.dot(first, tok_ref[...], preferred_element_type=F32)
        + jnp.dot(second, out_ref[...], preferred_element_type=F32)
    ).astype(BF)
    width = model_width // owners
    for peer in range(rows_ref.shape[0]):
        side = peer % grp_size
        rows_ref[peer, :, :half] = packed[:, side * half : (side + 1) * half]
        rows_ref[peer, :, half : half + LANES] = scale
        for rep in range(owners // grp_size if rows_ref.shape[2] > half + LANES else 0):
            to = half + LANES + rep * width
            start = (rep * grp_size + side) * width
            rows_ref[peer, :, to : to + width] = packed[:, start : start + width]


def select_rows(recv_ref, first, depth, pick):
    peers = recv_ref.shape[0] // PACK
    block = 8 if peers % 8 == 0 else peers
    many = block * CAP
    row, col = iota((many, block * PACK), 0), iota((many, block * PACK), 1)
    take = (col == row // CAP * PACK + row % CAP + pick * CAP).astype(BF)
    for at in range(peers // block):
        piece = recv_ref[at * block * PACK : (at + 1) * block * PACK, first : first + depth]
        yield pl.ds(at * many, many), jnp.dot(take, piece, preferred_element_type=F32)


def forward_kernel(source_ref, far_ref, *refs, cut, first):
    own_ref, send_ref, near_ref = refs[:3]
    down_ref, done = refs[-2:]
    depth = far_ref.shape[1]
    piece = tile_of(depth, 256)
    pieces = [slice(at, at + piece) for at in range(0, depth, piece)]
    loads = []
    for n, here in enumerate(pieces):
        for k in range(3):
            target = down_ref if k == 2 else near_ref.at[k]
            loads.append(
                pltpu.make_async_copy(
                    far_ref.at[k, here, cut], target.at[here], done.at[3 * n + k]
                )
            )
    for load in loads:
        load.start()
    rows_ref = source_ref
    if first:
        rows_ref, scale_ref = refs[3:5]
        for here, xr in select_rows(source_ref, 0, depth + LANES, 0):
            rows_ref[0, here, :] = xr[:, :depth].astype(BF)
            scale_ref[here, :] = xr[:, depth:]
        for here, yr in select_rows(source_ref, 0, depth, 1):
            rows_ref[1, here, :] = yr.astype(BF)
        for cols_ref in refs[5:-2]:
            cols_ref[...] = source_ref[:, depth + LANES :]
    for n, here in enumerate(pieces):
        for k in range(3):
            loads[3 * n + k].wait()
            right_ref = down_ref if k == 2 else near_ref.at[k]
            part = jnp.dot(
                rows_ref[k // 2, :, here], right_ref[here], preferred_element_type=F32
            )
            if n:
                part = part + own_ref[k]
            own_ref[k] = part
            if n == len(pieces) - 1:
                send_ref[k] = part.astype(BF)


def hidden_kernel(own_ref, other_ref, scale_ref, *refs, tile, width):
    hid_ref, pc_ref = refs[-2 - bool(width) :][:2]
    if width:
        give_ref = refs[-1]
        keep, give = split_columns(*refs[:4], width)
        rows = hid_ref.shape[1]
        for held, target_ref in ((keep, hid_ref), (give, give_ref)):
            for at in range(len(held)):
                for part in range(2):
                    start = (part * len(held) + at) * width
                    piece = held[at][part * rows : (part + 1) * rows]
                    target_ref[3, :, start : start + width] = piece
    cr = scale_ref[:, :1]
    pc = jnp.zeros((scale_ref.shape[0], 1), F32)
    for start in range(0, hid_ref.shape[2], tile):
        here = slice(start, start + tile)
        a = own_ref[0, :, here] + other_ref[0, :, here].astype(F32)
        b = own_ref[1, :, here] + other_ref[1, :, here].astype(F32)
        back = own_ref[2, :, here] + other_ref[2, :, here].astype(F32)
        sig = jax.nn.sigmoid(a)
        act = a * sig
        h = act * b
        dh = cr * back
        made = (
            (dh * b * sig * (1.0 + a * (1.0 - sig))).astype(BF),
            (dh * act).astype(BF),
            (cr * h).astype(BF),
        )
        for k in range(3):
            hid_ref[k, :, here] = made[k]
            if width:
                give_ref[k, :, here] = made[k]
        pc = pc + jnp.sum(h * back, axis=1, keepdims=True)
    pc_ref[...] = jnp.broadcast_to(pc, pc_ref.shape)


def return_kernel(hid_ref, pc_ref, near_ref, *refs, first, last):
    contract = (((1,), (1,)), ((), ()))
    px = lax.dot_general(
        hid_ref[0], near_ref[0], contract, preferred_element_type=F32
    ) + lax.dot_general(hid_ref[1], near_ref[1], contract, preferred_element_type=F32)
    pc = pc_ref[...]
    if not first:
        px = px + refs[0][...]
        pc = pc + refs[1][...]
    if not last:
        refs[-2][...] = px
        refs[-1][...] = pc
        return
    back_ref = refs[-1]
    many = px.shape[0]
    half = px.shape[1] // 2
    low, high = px[:, :half], px[:, half:]
    upper = iota((many, half), 0) % PACK < CAP
    even = jnp.where(upper, low, pltpu.roll(high, CAP, 0))
    odd = jnp.where(upper, pltpu.roll(low, many - CAP, 0), high)
    pc_up = pltpu.roll(pc, many - CAP, 0)
    for q in range(many // PACK):
        at = slice(q * PACK, (q + 1) * PACK)
        back_ref[2 * q, :, :half] = even[at].astype(BF)
        back_ref[2 * q, :, half:] = pc[at].astype(BF)
        back_ref[2 * q + 1, :, :half] = odd[at].astype(BF)
        back_ref[2 * q + 1, :, half:] = pc_up[at].astype(BF)


def split_columns(rep_ref, grp_ref, near_ref, far_ref, width):
    blocks = near_ref.shape[1] // width // 2
    rep_high, grp = rep_ref[0] // blocks, grp_ref[0]
    keep, give = [], []

    def owned(ref, at, side):
        start = (2 * at + side) * width
        return ref[:, start : start + width]

    for at in range(blocks):
        mine = jnp.where(grp == 0, owned(near_ref, at, 0), owned(near_ref, at, 1))
        theirs = jnp.where(grp == 0, owned(far_ref, at, 0), owned(far_ref, at, 1))
        keep.append(jnp.where(rep_high == grp, mine, theirs))
        give.append(jnp.where(rep_high == grp, theirs, mine))
    return keep, give


def turn_kernel(rep_ref, *refs, many):
    cols_refs, (turned_ref, left_ref) = refs[:-2], refs[-2:]
    width = left_ref.shape[2]
    sources = many // CAP
    planes = len(cols_refs[0].shape) == 3
    if planes:
        block = sources // 2
        blocks = cols_refs[0].shape[2] // width // 2
    else:
        block = 8 if sources % 8 == 0 else sources
        blocks = cols_refs[0].shape[1] // width
    rows = block * CAP
    row, col = iota((rows, block * PACK), 0), iota((rows, block * PACK), 1)
    source = row // CAP * PACK + row % CAP
    take = [(col == source + k * CAP).astype(BF) for k in range(2)]

    def owned(ref, at, rep):
        if planes:
            start = (at * blocks + rep) * width
            return ref[3, :, start : start + width]
        here = slice(at * block * PACK, (at + 1) * block * PACK)
        return ref[here, rep * width : (rep + 1) * width]

    for m, cols_ref in enumerate(cols_refs):
        for at in range(sources // block):
            piece = owned(cols_ref, at, 0)
            for rep in range(1, blocks):
                piece = jnp.where(rep_ref[0] % blocks == rep, owned(cols_ref, at, rep), piece)
            for k in range(2):
                left_ref[k, pl.ds(m * many + at * rows, rows), :] = jnp.dot(
                    take[k], piece, preferred_element_type=F32
                )
    for k in range(2):
        turned_ref[k] = jnp.transpose(left_ref[k]).astype(BF)


def weight_kernel(turned_ref, *refs, cut, tile, members):
    hid_refs, (out_ref, made_ref, done) = refs[:members], refs[-3:]
    tiles = [
        (k, start) for start in range(0, cut.stop - cut.start, tile) for k in range(3)
    ]
    copies = [
        pltpu.make_async_copy(
            made_ref.at[k, :, pl.ds(start, tile)],
            out_ref.at[k, :, pl.ds(cut.start + start, tile)],
            done.at[n],
        )
        for n, (k, start) in enumerate(tiles)
    ]
    for n, (k, start) in enumerate(tiles):
        here = slice(start, start + tile)
        right = jnp.concatenate([ref[k, :, here] for ref in hid_refs], axis=0)
        made_ref[k, :, here] = jnp.dot(
            turned_ref[k // 2], right, preferred_element_type=F32
        )
        if n:
            copies[n - 1].start()
    copies[-1].start()
    for copy in copies:
        copy.wait()


def token_kernel(ids_ref, slots_ref, recv_ref, tok_ref, comb_ref, *, grp_size):
    both = slots_ref[...]
    peers = recv_ref.shape[0]
    tokens = both.shape[1]
    half = tok_ref.shape[1] // (2 * grp_size)
    upper = iota((PACK, tokens), 0) < CAP
    contract = (((0,), (0,)), ((), ()))
    picks = [
        jnp.where(upper, both, 0.0).astype(BF),
        jnp.where(upper, 0.0, both).astype(BF),
    ]
    for side in range(grp_size):
        total = recv_ref[side].astype(F32)
        for at in range(side + grp_size, peers, grp_size):
            total = total + recv_ref[at].astype(F32)
        if side == 0:
            pc = total[:, half:]
            per = jnp.sum(
                jnp.where(upper, both, 0.0) * pc[:, :1], axis=0, keepdims=True
            )
            comb_ref[...] = jnp.where(ids_ref[...] == 0, per, 0.0)
        rounded = total[:, :half].astype(BF)
        for part in range(2):
            start = (2 * side + part) * half
            tok_ref[:, start : start + half] = lax.dot_general(
                picks[part], rounded, contract, preferred_element_type=F32
            ).astype(BF)


def gather(piece, rep_size, give=None):
    pieces = [piece]
    step = rep_size // 2
    while step:
        pairs = [(i, i ^ step) for i in range(rep_size)]
        sent = [give] if give is not None and len(pieces) == 1 else pieces
        pieces = pieces + [lax.ppermute(held, "rep", pairs) for held in sent]
        step //= 2
    return pieces


def local(tokens, grad_out, expert_ids, combine, weights):
    ep_size = lax.axis_size("ep")
    rep_size = lax.axis_size("rep")
    grp_size = lax.axis_size("grp")
    token_count, model_width = tokens.shape
    peers = ep_size * grp_size
    many = peers * CAP
    depth, _, hidden = weights.shape
    owners = rep_size * grp_size
    owner_rows = model_width // owners
    tile = tile_of(hidden, 256)
    middle = -(-hidden // (2 * tile)) * tile
    cuts = [slice(0, hidden)]
    if middle < hidden:
        cuts = [slice(0, middle), slice(middle, hidden)]
    widths = [cut.stop - cut.start for cut in cuts]
    paired = grp_size == 2 and rep_size % 2 == 0 and widths[0] == rep_size * owner_rows
    side_width = depth + LANES + (0 if paired else rep_size * owner_rows)
    vmem = pl.BlockSpec(memory_space=pltpu.VMEM)
    hbm = pl.BlockSpec(memory_space=pltpu.HBM)
    ids = expert_ids.T
    w = jnp.transpose(weights, (1, 0, 2))

    rep = lax.axis_index("rep").astype(jnp.int32).reshape(1)
    grp = lax.axis_index("grp").astype(jnp.int32).reshape(1)
    ids, rep, grp = lax.optimization_barrier((ids, rep, grp))
    rows, slot_map = pl.pallas_call(
        functools.partial(pack_kernel, grp_size=grp_size, owners=owners),
        out_shape=(
            jax.ShapeDtypeStruct((peers, PACK, side_width), BF),
            jax.ShapeDtypeStruct((PACK, token_count), F32),
        ),
        in_specs=[hbm] * 4,
        out_specs=(vmem,) * 2,
        scratch_shapes=[
            pltpu.VMEM(ids.shape, ids.dtype),
            pltpu.VMEM(ids.shape, combine.dtype),
            pltpu.VMEM(tokens.shape, tokens.dtype),
            pltpu.VMEM(grad_out.shape, grad_out.dtype),
            pltpu.SemaphoreType.DMA((4,)),
        ],
        compiler_params=pltpu.CompilerParams(vmem_limit_bytes=WHOLE),
        cost_estimate=cost(2_000_000_000),
        name="pack",
    )(ids, combine.T, tokens, grad_out)

    recv = lax.all_to_all(rows, ("ep", "grp"), 0, 0, tiled=True)
    recv = recv.reshape(peers * PACK, side_width)

    far_recv = None
    if paired:
        far_recv = lax.ppermute(recv, "grp", [(0, 1), (1, 0)])

    source = recv
    owns, nears, others = [], [], []
    for c, width in enumerate(widths):
        first = c == 0
        extra = ()
        if first:
            extra = (
                jax.ShapeDtypeStruct((2, many, depth), BF),
                jax.ShapeDtypeStruct((many, LANES), F32),
            )
            if not paired:
                cols_shape = (peers * PACK, rep_size * owner_rows)
                extra += (jax.ShapeDtypeStruct(cols_shape, BF),)
        own, send, near, *more = pl.pallas_call(
            functools.partial(forward_kernel, cut=pl.ds(cuts[c].start, width), first=first),
            out_shape=(
                jax.ShapeDtypeStruct((3, many, width), F32),
                jax.ShapeDtypeStruct((3, many, width), BF),
                jax.ShapeDtypeStruct((2, depth, width), BF),
                *extra,
            ),
            in_specs=[vmem, hbm],
            out_specs=(vmem,) * (3 + len(extra)),
            scratch_shapes=[
                pltpu.VMEM((depth, width), BF),
                pltpu.SemaphoreType.DMA((3 * (depth // tile_of(depth, 256)),)),
            ],
            compiler_params=pltpu.CompilerParams(vmem_limit_bytes=WHOLE - (20 << 20)),
            cost_estimate=cost(3_000_000_000),
        )(source, w)
        if first:
            source, scale = more[:2]
            cols = more[2:]
        owns.append(own)
        nears.append(near)
        if grp_size == 2:
            others.append(lax.ppermute(send, "grp", [(0, 1), (1, 0)]))
        else:
            total = lax.psum(send.astype(F32), "grp")
            others.append((total - send.astype(F32)).astype(BF))

    gathered = []
    back = []
    for c, cut in enumerate(cuts):
        last = c == len(cuts) - 1
        fourth = paired and c == 0
        hid_shape = jax.ShapeDtypeStruct((3 + fourth, many, widths[c]), BF)
        smem = pl.BlockSpec(memory_space=pltpu.SMEM)
        hid, pc, *give = pl.pallas_call(
            functools.partial(hidden_kernel, tile=tile, width=owner_rows if fourth else 0),
            out_shape=(hid_shape, jax.ShapeDtypeStruct((many, LANES), F32))
            + (hid_shape,) * fourth,
            in_specs=[vmem] * 3 + [smem, smem, vmem, vmem] * fourth,
            out_specs=(vmem,) * (2 + fourth),
            compiler_params=pltpu.CompilerParams(vmem_limit_bytes=GRANT),
            cost_estimate=cost(1_000_000_000),
        )(owns[c], others[c], scale, *((rep, grp, recv, far_recv) * fourth))
        if last:
            shapes = jax.ShapeDtypeStruct((peers, PACK, depth // 2 + LANES), BF)
        else:
            shapes = (
                jax.ShapeDtypeStruct((many, depth), F32),
                jax.ShapeDtypeStruct((many, LANES), F32),
            )
        back = pl.pallas_call(
            functools.partial(return_kernel, first=c == 0, last=last),
            out_shape=shapes,
            in_specs=[vmem] * (3 + len(back)),
            out_specs=vmem if last else (vmem,) * 2,
            compiler_params=pltpu.CompilerParams(vmem_limit_bytes=GRANT),
            cost_estimate=cost(3_000_000_000),
        )(hid, pc, nears[c], *back)
        gathered.append(gather(hid, rep_size, *give))

    turned = pl.pallas_call(
        functools.partial(turn_kernel, many=many),
        out_shape=jax.ShapeDtypeStruct((2, owner_rows, rep_size * many), BF),
        in_specs=[smem] + [vmem] * rep_size,
        out_specs=vmem,
        scratch_shapes=[pltpu.VMEM((2, rep_size * many, owner_rows), F32)],
        compiler_params=pltpu.CompilerParams(vmem_limit_bytes=GRANT),
        cost_estimate=cost(500_000_000),
        name="turn",
    )(rep, *(gathered[0] if paired else gather(cols[0], rep_size)))

    back_recv = lax.all_to_all(back, ("ep", "grp"), 0, 0, tiled=True)

    grad_weights = []
    for c, cut in enumerate(cuts):
        grad_weights = [
            pl.pallas_call(
                functools.partial(weight_kernel, cut=cut, tile=tile, members=rep_size),
                out_shape=jax.ShapeDtypeStruct((3, owner_rows, hidden), F32),
                in_specs=[vmem] * (1 + rep_size)
                + [pl.BlockSpec(memory_space=pl.ANY)] * len(grad_weights),
                out_specs=pl.BlockSpec(memory_space=pl.ANY),
                scratch_shapes=[
                    pltpu.VMEM((3, owner_rows, widths[c]), F32),
                    pltpu.SemaphoreType.DMA((3 * (widths[c] // tile),)),
                ],
                input_output_aliases={1 + rep_size: 0} if grad_weights else {},
                compiler_params=pltpu.CompilerParams(vmem_limit_bytes=GRANT),
                cost_estimate=cost(3_000_000_000),
            )(turned, *gathered[c], *grad_weights)
        ]

    grad_tokens, grad_combine = pl.pallas_call(
        functools.partial(token_kernel, grp_size=grp_size),
        out_shape=(
            jax.ShapeDtypeStruct((token_count, model_width), BF),
            jax.ShapeDtypeStruct((2, token_count), F32),
        ),
        in_specs=[vmem] * 3,
        out_specs=(vmem,) * 2,
        compiler_params=pltpu.CompilerParams(vmem_limit_bytes=GRANT),
        cost_estimate=cost(2_000_000_000),
        name="token",
    )(ids, slot_map, back_recv)

    return (grad_tokens, grad_combine.T, jnp.transpose(grad_weights[0], (1, 0, 2)))


def solution(mesh):
    in_specs = (
        P(("rep", "ep", "grp"), None),
        P(("rep", "ep", "grp"), None),
        P(("rep", "ep", "grp"), None),
        P(("rep", "ep", "grp"), None),
        P("grp", None, "ep"),
    )
    out_specs = (
        P(("rep", "ep", "grp"), None),
        P(("rep", "ep", "grp"), None),
        P(("rep", "grp"), None, "ep"),
    )
    return jax.shard_map(
        local, mesh=mesh, in_specs=in_specs, out_specs=out_specs, check_vma=False
    )
```

time: 57 us -> 55.9 us (0.981)
  waiting for transfers between devices: 15.6 us -> 13.5 us
  Pallas kernels: 14.5 us -> 16.5 us
  starting transfers between devices: 11 us -> 10 us
    ppermute x1, waiting for transfers between devices: 7.59 us -> 3.11 us  [local(): far_recv = lax.ppermute(recv, 'grp', [(0, 1), (1, 0)])]
    ppermute x2, waiting for transfers between devices: 0.01 us -> 4.36 us  [local(): others.append(lax.ppermute(send, 'grp', [(0, 1), (1, 0)]))]
    pallas_call x7 -> x8, Pallas kernels: 10.7 us -> 13 us  [the longest x2 5.96 us: local(): pl.pallas_call(functools.partial(forward_kernel, cut=pl.ds(cuts[c].start,...]
    ppermute x9 -> x6, waiting for transfers between devices: 2.02 us -> 0.02 us  [gather(): pieces = pieces + [lax.ppermute(held, 'rep', pairs) for held in sent]]
    ppermute x2, starting transfers between devices: 0.73 us -> 2.09 us  [local(): others.append(lax.ppermute(send, 'grp', [(0, 1), (1, 0)]))]
    ppermute x1, starting transfers between devices: 1.69 us -> 0.33 us  [local(): far_recv = lax.ppermute(recv, 'grp', [(0, 1), (1, 0)])]
    ppermute x9 -> x6, starting transfers between devices: 5.12 us -> 4.12 us  [gather(): pieces = pieces + [lax.ppermute(held, 'rep', pairs) for held in sent]]
  transfers between devices with their start and end apart: 13 -> 10, of which waited for: 3 -> 3; matrix products, arithmetic and copies ran while one was open for 0% -> 0% of each run, Pallas kernels for 8% -> 12%
where the time goes in v4:
time: 55.9 us; the launch traced here: 55.5 us
  Pallas kernels  16.5 us (30%)
  blocking collectives  14.8 us (26%)
  waiting for transfers between devices  13.5 us (24%)
  starting transfers between devices  10 us (18%)
  between operations  0.75 us (1%)
    all_to_all x1, blocking collectives, local(): recv = lax.all_to_all(rows, ('ep', 'grp'), 0, 0, tiled=True)  14.8 us
    all_to_all x1, waiting for transfers between devices, local(): back_recv = lax.all_to_all(back, ('ep', 'grp'), 0, 0, tiled=True)  5.98 us
    pallas_call x2, Pallas kernels, local(): pl.pallas_call(functools.partial(forward_kernel, cut=pl.ds(cuts[c].start,...  5.96 us
    ppermute x2, waiting for transfers between devices, local(): others.append(lax.ppermute(send, 'grp', [(0, 1), (1, 0)]))  4.36 us
    ppermute x6, starting transfers between devices, gather(): pieces = pieces + [lax.ppermute(held, 'rep', pairs) for held in sent]  4.12 us
    pallas_call x2, Pallas kernels, local(): pl.pallas_call(functools.partial(weight_kernel, cut=cut, tile=tile, membe...  3.71 us
    all_to_all x1, starting transfers between devices, local(): back_recv = lax.all_to_all(back, ('ep', 'grp'), 0, 0, tiled=True)  3.48 us
    ppermute x1, waiting for transfers between devices, local(): far_recv = lax.ppermute(recv, 'grp', [(0, 1), (1, 0)])  3.11 us
  transfers between devices with their start and end apart: 10, of which 3 were waited for; matrix products, arithmetic and copies ran while one was open for 0% of the time, Pallas kernels for 12%

profile of v4, /device:TPU:0, one launch (start us, length us, event | category | flops | bytes accessed | tf_op | source)
XLA Modules:
  0.0 55.5 jit_solution(4565717080032177602)
XLA Ops:
  0.6 2.2 %pack.1 = (bf16[8,8,1152]{2,1,0:T(8,128)(2,1)}, f32[8,128]{1,0:T(8,128)}) custom-call(s32[2,128]{1,0:T(2,128)} %bitcast.11, bf16[2,128]{1,0:T(2,128)(2,1)} %bitcast.16, bf16[128,2048]{1,0:T(8,128)(2,1)} %refs_2_.1, bf16[128,2048]{1,0:T(8,128)(2,1)} %refs_3_.1), custom_call_target="tpu_custom_call" | custom-call | flops 2000000000 | tf_op jit(solution)/shard_map/pack/pallas_call | solution.py:350
  2.8 14.8 %all_to_all.10 = bf16[8,8,1152]{2,1,0:T(8,128)(2,1)S(1)} all-to-all(bf16[8,8,1152]{2,1,0:T(8,128)(2,1)} %get-tuple-element.27), channel_id=1, replica_groups=mesh['rep'=4,'ep'=4,'grp'=2] {'ep','grp'}, dimensions={0} | all-to-all | bytes 294912 | tf_op jit(solution)/shard_map/all_to_all | solution.py:370
  17.6 3.2 %shard_map.76 = (f32[3,32,1024]{2,1,0:T(8,128)S(1)}, bf16[3,32,1024]{2,1,0:T(8,128)(2,1)S(1)}, bf16[2,1024,1024]{2,1,0:T(8,128)(2,1)S(1)}, bf16[2,32,1024]{2,1,0:T(8,128)(2,1)S(1)}, f32[32,128]{1,0:T(8,128)S(1)}) custom-call(bf16[64,1152]{1,0:T(8,128)(2,1)S(1)} %bitcast.8, bf16[3,1024,1792]{2,1,0:T(8,128)(2,1)} %bitcast.13), custom_call_target="tpu_custom_call" | custom-call | flops 3000000000 | tf_op jit(solution)/shard_map/pallas_call | solution.py:390
  20.8 2.8 %shard_map.77 = (f32[3,32,768]{2,1,0:T(8,128)S(1)}, bf16[3,32,768]{2,1,0:T(8,128)(2,1)S(1)}, bf16[2,1024,768]{2,1,0:T(8,128)(2,1)S(1)}) custom-call(bf16[2,32,1024]{2,1,0:T(8,128)(2,1)S(1)} %get-tuple-element.28.source_ref, bf16[3,1024,1792]{2,1,0:T(8,128)(2,1)} %bitcast.14), custom_call_target="tpu_custom_call" | custom-call | flops 3000000000 | tf_op jit(solution)/shard_map/pallas_call | solution.py:390
  23.6 0.4 collective-permute-start
  24.0 1.7 %collective-permute-start.1 = (bf16[3,32,1024]{2,1,0:T(8,128)(2,1)S(1)}, bf16[3,32,1024]{2,1,0:T(8,128)(2,1)S(1)}, u32[]{:S(2)}, u32[]{:S(2)}) collective-permute-start(bf16[3,32,1024]{2,1,0:T(8,128)(2,1)S(1)} %get-tuple-element.36), channel_id=1, source_target_pairs={{0,1},{1,0},{2,3},{3,2},{4,5},{5,4},{6,7},{7,6},{8,9},{9,8},{10,11... | collective-permute-start | bytes 589832 | tf_op jit(solution)/shard_map/ppermute | solution.py:413
  25.7 0.3 collective-permute-start.2
  26.0 4.4 %collective-permute-done.other_ref = bf16[3,32,768]{2,1,0:T(8,128)(2,1)S(1)} collective-permute-done((bf16[3,32,768]{2,1,0:T(8,128)(2,1)S(1)}, bf16[3,32,768]{2,1,0:T(8,128)(2,1)S(1)}, u32[]{:S(2)}, u32[]{:S(2)}) %collective-permute-start) | collective-permute-done | bytes 147488 | tf_op jit(solution)/shard_map/ppermute | solution.py:413
  30.4 0.1 shard_map.78
  30.5 1.6 %collective-permute-start.6 = (bf16[3,32,768]{2,1,0:T(8,128)(2,1)S(1)}, bf16[3,32,768]{2,1,0:T(8,128)(2,1)S(1)}, u32[]{:S(2)}, u32[]{:S(2)}) collective-permute-start(bf16[3,32,768]{2,1,0:T(8,128)(2,1)S(1)} %get-tuple-element.32.hid_ref.refs_0_), channel_id=1, source_target_pairs={{0,16},{8,24},{16,0},{24,8},{1,17},{9,25},{17,1},{25,9},{2,18},{10... | collective-permute-start | bytes 442376 | tf_op jit(solution)/shard_map/ppermute | solution.py:319
  32.1 3.1 %collective-permute-done.2.refs_3_ = bf16[64,1152]{1,0:T(8,128)(2,1)S(1)} collective-permute-done((bf16[64,1152]{1,0:T(8,128)(2,1)S(1)}, bf16[64,1152]{1,0:T(8,128)(2,1)S(1)}, u32[]{:S(2)}, u32[]{:S(2)}) %collective-permute-start.2) | collective-permute-done | bytes 147488 | tf_op jit(solution)/shard_map/ppermute | solution.py:375
  35.2 0.0 collective-permute-done.1.other_ref
  35.2 0.2 shard_map.79
  35.4 1.6 %collective-permute-start.3 = (bf16[4,32,1024]{2,1,0:T(8,128)(2,1)S(1)}, bf16[4,32,1024]{2,1,0:T(8,128)(2,1)S(1)}, u32[]{:S(2)}, u32[]{:S(2)}) collective-permute-start(bf16[4,32,1024]{2,1,0:T(8,128)(2,1)S(1)} %get-tuple-element.46), channel_id=1, source_target_pairs={{0,16},{8,24},{16,0},{24,8},{1,17},{9,25},{17,1},{25,9},{2,18},{10... | collective-permute-start | bytes 786440 | tf_op jit(solution)/shard_map/ppermute | solution.py:319
  36.9 1.3 %shard_map.80 = (f32[32,1024]{1,0:T(8,128)S(1)}, f32[32,128]{1,0:T(8,128)S(1)}) custom-call(bf16[4,32,1024]{2,1,0:T(8,128)(2,1)S(1)} %get-tuple-element.39.hid_ref.refs_0_, f32[32,128]{1,0:T(8,128)S(1)} %get-tuple-element.40.pc_ref, bf16[2,1024,1024]{2,1,0:T(8,128)(2,1)S(1)} %get-tuple-element.41.near_ref), custom_call_target="tpu_custom_call" | custom-call | flops 3000000000 | tf_op jit(solution)/shard_map/pallas_call | solution.py:441
  38.2 0.0 copy-start.1
  38.3 1.7 %shard_map.81 = bf16[8,8,640]{2,1,0:T(8,128)(2,1)} custom-call(bf16[3,32,768]{2,1,0:T(8,128)(2,1)S(1)} %get-tuple-element.32.hid_ref.refs_0_, f32[32,128]{1,0:T(8,128)S(1)} %get-tuple-element.33.pc_ref, bf16[2,1024,768]{2,1,0:T(8,128)(2,1)S(1)} %get-tuple-element.34.near_ref, f32[32,1024]{1,0:T(8,128)S(1)} %get-tuple-element.42.refs_0_, ...), custom_call_target="tpu_custom_call" | custom-call | flops 3000000000 | tf_op jit(solution)/shard_map/pallas_call | solution.py:441
  39.9 3.5 %all-to-all-start.1 = ((bf16[8,8,640]{2,1,0:T(8,128)(2,1)}), bf16[8,8,640]{2,1,0:T(8,128)(2,1)S(1)}, u32[]{:S(2)}, u32[]{:S(2)}) async-start(bf16[8,8,640]{2,1,0:T(8,128)(2,1)} %shard_map.81), calls=%async_computation.1 | async-start | bytes 163840 | tf_op jit(solution)/shard_map/all_to_all | solution.py:462
  43.4 0.0 collective-permute-start.4
  43.4 0.0 collective-permute-done.3.refs_1_
  43.4 0.5 collective-permute-start.5
  43.9 0.1 collective-permute-start.7
  44.0 0.0 collective-permute-done.6.refs_1_
  44.0 0.4 collective-permute-start.8
  44.4 6.0 %all-to-all-done.1.recv_ref = bf16[8,8,640]{2,1,0:T(8,128)(2,1)S(1)} async-done(((bf16[8,8,640]{2,1,0:T(8,128)(2,1)}), bf16[8,8,640]{2,1,0:T(8,128)(2,1)S(1)}, u32[]{:S(2)}, u32[]{:S(2)}) %all-to-all-start.1) | async-done | bytes 81952 | tf_op jit(solution)/shard_map/all_to_all | solution.py:462
  50.4 1.1 %token_.1 = (bf16[128,2048]{1,0:T(8,128)(2,1)}, f32[2,128]{1,0:T(2,128)}) custom-call(s32[2,128]{1,0:T(2,128)S(1)} %bitcast.12, f32[8,128]{1,0:T(8,128)S(1)} %copy-done.1, bf16[8,8,640]{2,1,0:T(8,128)(2,1)S(1)} %all-to-all-done.1.recv_ref), custom_call_target="tpu_custom_call" | custom-call | flops 2000000000 | tf_op jit(solution)/shard_map/token/pallas_call | solution.py:483
  51.6 0.0 collective-permute-done.4.refs_2_
  51.6 0.0 collective-permute-done.5.refs_3_
  51.6 0.2 turn.1.turned_ref
  51.8 2.0 %shard_map.82.refs_4_ = f32[3,256,1792]{2,1,0:T(8,128)} custom-call(bf16[2,256,128]{2,1,0:T(8,128)(2,1)S(1)} %turn.1.turned_ref, bf16[4,32,1024]{2,1,0:T(8,128)(2,1)S(1)} %get-tuple-element.39.hid_ref.refs_0_, bf16[4,32,1024]{2,1,0:T(8,128)(2,1)S(1)} %collective-permute-done.3.refs_1_, bf16[4,32,1024]{2,1,0:T(8,128)(2,1)S(1)} %collective-permute-done.4.refs_2_, ...), custom_call_target="tpu_custom_call" | custom-call | flops 3000000000 | tf_op jit(solution)/shard_map/pallas_call | solution.py:467
  53.8 0.0 collective-permute-done.8.refs_3_
  53.8 1.7 %shard_map.83 = f32[3,256,1792]{2,1,0:T(8,128)} custom-call(bf16[2,256,128]{2,1,0:T(8,128)(2,1)S(1)} %turn.1.turned_ref, bf16[3,32,768]{2,1,0:T(8,128)(2,1)S(1)} %get-tuple-element.32.hid_ref.refs_0_, bf16[3,32,768]{2,1,0:T(8,128)(2,1)S(1)} %collective-permute-done.6.refs_1_, ...), custom_call_target="tpu_custom_call", output_to_operand_aliasing={{}: (5, {})} | custom-call | flops 3000000000 | tf_op jit(solution)/shard_map/pallas_call | solution.py:467
  (4 shorter events, 0.0 us)
Async XLA Ops:
  23.6 6.8 %collective-permute-start = (bf16[3,32,768]{2,1,0:T(8,128)(2,1)S(1)}, bf16[3,32,768]{2,1,0:T(8,128)(2,1)S(1)}, u32[]{:S(2)}, u32[]{:S(2)}) collective-permute-start(bf16[3,32,768]{2,1,0:T(8,128)(2,1)S(1)} %get-tuple-element.30), channel_id=1, source_target_pairs={{0,1},{1,0},{2,3},{3,2},{4,5},{5,4},{6,7},{7,6},{8,9},{9,8},{10,11... | collective-permute-start | bytes 442376 | tf_op jit(solution)/shard_map/ppermute | solution.py:413
  24.0 11.2 %collective-permute-start.1 = (bf16[3,32,1024]{2,1,0:T(8,128)(2,1)S(1)}, bf16[3,32,1024]{2,1,0:T(8,128)(2,1)S(1)}, u32[]{:S(2)}, u32[]{:S(2)}) collective-permute-start(bf16[3,32,1024]{2,1,0:T(8,128)(2,1)S(1)} %get-tuple-element.36), channel_id=1, source_target_pairs={{0,1},{1,0},{2,3},{3,2},{4,5},{5,4},{6,7},{7,6},{8,9},{9,8},{10,11... | collective-permute-start | bytes 589832 | tf_op jit(solution)/shard_map/ppermute | solution.py:413
  25.7 9.5 %collective-permute-start.2 = (bf16[64,1152]{1,0:T(8,128)(2,1)S(1)}, bf16[64,1152]{1,0:T(8,128)(2,1)S(1)}, u32[]{:S(2)}, u32[]{:S(2)}) collective-permute-start(bf16[64,1152]{1,0:T(8,128)(2,1)S(1)} %bitcast.9), channel_id=1, source_target_pairs={{0,1},{1,0},{2,3},{3,2},{4,5},{5,4},{6,7},{7,6},{8,9},{9,8},{10,11... | collective-permute-start | bytes 442376 | tf_op jit(solution)/shard_map/ppermute | solution.py:375
  30.5 13.5 %collective-permute-start.6 = (bf16[3,32,768]{2,1,0:T(8,128)(2,1)S(1)}, bf16[3,32,768]{2,1,0:T(8,128)(2,1)S(1)}, u32[]{:S(2)}, u32[]{:S(2)}) collective-permute-start(bf16[3,32,768]{2,1,0:T(8,128)(2,1)S(1)} %get-tuple-element.32.hid_ref.refs_0_), channel_id=1, source_target_pairs={{0,16},{8,24},{16,0},{24,8},{1,17},{9,25},{17,1},{25,9},{2,18},{10... | collective-permute-start | bytes 442376 | tf_op jit(solution)/shard_map/ppermute | solution.py:319
  35.4 8.1 %collective-permute-start.3 = (bf16[4,32,1024]{2,1,0:T(8,128)(2,1)S(1)}, bf16[4,32,1024]{2,1,0:T(8,128)(2,1)S(1)}, u32[]{:S(2)}, u32[]{:S(2)}) collective-permute-start(bf16[4,32,1024]{2,1,0:T(8,128)(2,1)S(1)} %get-tuple-element.46), channel_id=1, source_target_pairs={{0,16},{8,24},{16,0},{24,8},{1,17},{9,25},{17,1},{25,9},{2,18},{10... | collective-permute-start | bytes 786440 | tf_op jit(solution)/shard_map/ppermute | solution.py:319
  38.2 12.2 %copy-start = (s32[128,2]{0,1:T(2,128)S(1)}, s32[128,2]{0,1:T(2,128)}, u32[]{:S(2)}) copy-start(s32[128,2]{0,1:T(2,128)} %param.7) | copy-start | bytes 3076
  38.2 12.2 %copy-start.1 = (f32[8,128]{1,0:T(8,128)S(1)}, f32[8,128]{1,0:T(8,128)}, u32[]{:S(2)}) copy-start(f32[8,128]{1,0:T(8,128)} %get-tuple-element.26.slots_ref) | copy-start | bytes 12292
  39.9 10.5 %all-to-all-start.1 = ((bf16[8,8,640]{2,1,0:T(8,128)(2,1)}), bf16[8,8,640]{2,1,0:T(8,128)(2,1)S(1)}, u32[]{:S(2)}, u32[]{:S(2)}) async-start(bf16[8,8,640]{2,1,0:T(8,128)(2,1)} %shard_map.81), calls=%async_computation.1 | async-start | bytes 163840 | tf_op jit(solution)/shard_map/all_to_all | solution.py:462
  43.4 8.1 %collective-permute-start.4 = (bf16[4,32,1024]{2,1,0:T(8,128)(2,1)S(1)}, bf16[4,32,1024]{2,1,0:T(8,128)(2,1)S(1)}, u32[]{:S(2)}, u32[]{:S(2)}) collective-permute-start(bf16[4,32,1024]{2,1,0:T(8,128)(2,1)S(1)} %get-tuple-element.39.hid_ref.refs_0_), channel_id=1, source_target_pairs={{0,8},{8,0},{16,24},{24,16},{1,9},{9,1},{17,25},{25,17},{2,10},{10... | collective-permute-start | bytes 786440 | tf_op jit(solution)/shard_map/ppermute | solution.py:319
  43.4 8.1 %collective-permute-start.5 = (bf16[4,32,1024]{2,1,0:T(8,128)(2,1)S(1)}, bf16[4,32,1024]{2,1,0:T(8,128)(2,1)S(1)}, u32[]{:S(2)}, u32[]{:S(2)}) collective-permute-start(bf16[4,32,1024]{2,1,0:T(8,128)(2,1)S(1)} %collective-permute-done.3.refs_1_), channel_id=1, source_target_pairs={{0,8},{8,0},{16,24},{24,16},{1,9},{9,1},{17,25},{25,17},{2,10},{10... | collective-permute-start | bytes 786440 | tf_op jit(solution)/shard_map/ppermute | solution.py:319
  43.9 9.9 %collective-permute-start.7 = (bf16[3,32,768]{2,1,0:T(8,128)(2,1)S(1)}, bf16[3,32,768]{2,1,0:T(8,128)(2,1)S(1)}, u32[]{:S(2)}, u32[]{:S(2)}) collective-permute-start(bf16[3,32,768]{2,1,0:T(8,128)(2,1)S(1)} %get-tuple-element.32.hid_ref.refs_0_), channel_id=1, source_target_pairs={{0,8},{8,0},{16,24},{24,16},{1,9},{9,1},{17,25},{25,17},{2,10},{10... | collective-permute-start | bytes 442376 | tf_op jit(solution)/shard_map/ppermute | solution.py:319
  44.0 9.8 %collective-permute-start.8 = (bf16[3,32,768]{2,1,0:T(8,128)(2,1)S(1)}, bf16[3,32,768]{2,1,0:T(8,128)(2,1)S(1)}, u32[]{:S(2)}, u32[]{:S(2)}) collective-permute-start(bf16[3,32,768]{2,1,0:T(8,128)(2,1)S(1)} %collective-permute-done.6.refs_1_), channel_id=1, source_target_pairs={{0,8},{8,0},{16,24},{24,16},{1,9},{9,1},{17,25},{25,17},{2,10},{10... | collective-permute-start | bytes 442376 | tf_op jit(solution)/shard_map/ppermute | solution.py:319

commit v5 on v4

--- a/solution.py
+++ b/solution.py
@@ -42,9 +42,10 @@
     return jnp.where(before == slot, wide, 0.0)
 
 
-def pack_kernel(*refs, grp_size, owners):
-    sources, (rows_ref, slots_ref) = refs[:4], refs[4:6]
-    held, done = refs[6:10], refs[10]
+def pack_kernel(*refs, grp_size, owners, paired):
+    grp_ref, *sources = refs[:5]
+    made = 3 if paired else 2
+    outs, (held, done) = refs[5 : 5 + made], (refs[5 + made : -1], refs[-1])
     loads = [
         pltpu.make_async_copy(source, target, done.at[n])
         for n, (source, target) in enumerate(zip(sources, held))
@@ -56,10 +57,12 @@
     ids_ref, comb_ref, tok_ref, out_ref = held
     ids = ids_ref[...]
     both = slots(ids)
-    slots_ref[...] = both
+    outs[0][...] = both
     model_width = tok_ref.shape[1]
     tokens = ids.shape[1]
     half = model_width // grp_size
+    width = model_width // owners
+    reps = owners // grp_size
     upper = iota((PACK, tokens), 0) < CAP
     first = jnp.where(upper, both, 0.0).astype(BF)
     second = jnp.where(upper, 0.0, both).astype(BF)
@@ -74,15 +77,38 @@
         jnp.dot(first, tok_ref[...], preferred_element_type=F32)
         + jnp.dot(second, out_ref[...], preferred_element_type=F32)
     ).astype(BF)
-    width = model_width // owners
-    for peer in range(rows_ref.shape[0]):
-        side = peer % grp_size
-        rows_ref[peer, :, :half] = packed[:, side * half : (side + 1) * half]
-        rows_ref[peer, :, half : half + LANES] = scale
-        for rep in range(owners // grp_size if rows_ref.shape[2] > half + LANES else 0):
-            to = half + LANES + rep * width
-            start = (rep * grp_size + side) * width
-            rows_ref[peer, :, to : to + width] = packed[:, start : start + width]
+
+    def owned(side, rep):
+        start = (rep * grp_size + side) * width
+        return packed[:, start : start + width]
+
+    if not paired:
+        rows_ref = outs[1]
+        for peer in range(rows_ref.shape[0]):
+            side = peer % grp_size
+            rows_ref[peer, :, :half] = packed[:, side * half : (side + 1) * half]
+            rows_ref[peer, :, half : half + LANES] = scale
+            for rep in range(reps):
+                to = half + LANES + rep * width
+                rows_ref[peer, :, to : to + width] = owned(side, rep)
+        return
+    for to_ref, near, far in ((outs[1], 0, 1), (outs[2], 1, 0)):
+        low = grp_ref[0] == 0
+        to_ref[:, :half] = jnp.where(
+            low, packed[:, near * half : (near + 1) * half], packed[:, far * half : (far + 1) * half]
+        )
+        to_ref[:, half : half + LANES] = scale
+        for at in range(reps // 2):
+            to = half + LANES + at * width
+            to_ref[:, to : to + width] = jnp.where(
+                low, owned(near, far * reps // 2 + at), owned(far, near * reps // 2 + at)
+            )
+
+
+def join_kernel(grp_ref, mine_ref, got_ref, out_ref):
+    low = grp_ref[0] == 0
+    out_ref[:PACK] = jnp.where(low, mine_ref[...], got_ref[...])
+    out_ref[PACK:] = jnp.where(low, got_ref[...], mine_ref[...])
 
 
 def select_rows(recv_ref, first, depth, pick):
@@ -96,52 +122,31 @@
         yield pl.ds(at * many, many), jnp.dot(take, piece, preferred_element_type=F32)
 
 
-def forward_kernel(source_ref, far_ref, *refs, cut, first):
-    own_ref, send_ref, near_ref = refs[:3]
-    down_ref, done = refs[-2:]
-    depth = far_ref.shape[1]
-    piece = tile_of(depth, 256)
-    pieces = [slice(at, at + piece) for at in range(0, depth, piece)]
-    loads = []
-    for n, here in enumerate(pieces):
-        for k in range(3):
-            target = down_ref if k == 2 else near_ref.at[k]
-            loads.append(
-                pltpu.make_async_copy(
-                    far_ref.at[k, here, cut], target.at[here], done.at[3 * n + k]
-                )
-            )
-    for load in loads:
-        load.start()
-    rows_ref = source_ref
+def forward_kernel(*refs, inputs, cut, first):
+    source_refs, w_ref, (own_ref, send_ref) = refs[:inputs], refs[inputs], refs[inputs + 1 :][:2]
+    depth = w_ref.shape[1]
+    rows_ref = source_refs[0]
     if first:
-        rows_ref, scale_ref = refs[3:5]
-        for here, xr in select_rows(source_ref, 0, depth + LANES, 0):
+        rows_ref, scale_ref, recv_ref = refs[inputs + 3 :]
+        many = recv_ref.shape[0] // inputs
+        for m, source_ref in enumerate(source_refs):
+            recv_ref[m * many : (m + 1) * many] = source_ref[...]
+        for here, xr in select_rows(recv_ref, 0, depth + LANES, 0):
             rows_ref[0, here, :] = xr[:, :depth].astype(BF)
             scale_ref[here, :] = xr[:, depth:]
-        for here, yr in select_rows(source_ref, 0, depth, 1):
+        for here, yr in select_rows(recv_ref, 0, depth, 1):
             rows_ref[1, here, :] = yr.astype(BF)
-        for cols_ref in refs[5:-2]:
-            cols_ref[...] = source_ref[:, depth + LANES :]
-    for n, here in enumerate(pieces):
-        for k in range(3):
-            loads[3 * n + k].wait()
-            right_ref = down_ref if k == 2 else near_ref.at[k]
-            part = jnp.dot(
-                rows_ref[k // 2, :, here], right_ref[here], preferred_element_type=F32
-            )
-            if n:
-                part = part + own_ref[k]
-            own_ref[k] = part
-            if n == len(pieces) - 1:
-                send_ref[k] = part.astype(BF)
+    for k in range(3):
+        part = jnp.dot(rows_ref[k // 2], w_ref[k, :, cut], preferred_element_type=F32)
+        own_ref[k] = part
+        send_ref[k] = part.astype(BF)
 
 
 def hidden_kernel(own_ref, other_ref, scale_ref, *refs, tile, width):
     hid_ref, pc_ref = refs[-2 - bool(width) :][:2]
     if width:
         give_ref = refs[-1]
-        keep, give = split_columns(*refs[:4], width)
+        keep, give = split_columns(*refs[:3], width)
         rows = hid_ref.shape[1]
         for held, target_ref in ((keep, hid_ref), (give, give_ref)):
             for at in range(len(held)):
@@ -173,11 +178,11 @@
     pc_ref[...] = jnp.broadcast_to(pc, pc_ref.shape)
 
 
-def return_kernel(hid_ref, pc_ref, near_ref, *refs, first, last):
+def return_kernel(ep_ref, hid_ref, pc_ref, w_ref, *refs, cut, first, last, near):
     contract = (((1,), (1,)), ((), ()))
     px = lax.dot_general(
-        hid_ref[0], near_ref[0], contract, preferred_element_type=F32
-    ) + lax.dot_general(hid_ref[1], near_ref[1], contract, preferred_element_type=F32)
+        hid_ref[0], w_ref[0, :, cut], contract, preferred_element_type=F32
+    ) + lax.dot_general(hid_ref[1], w_ref[1, :, cut], contract, preferred_element_type=F32)
     pc = pc_ref[...]
     if not first:
         px = px + refs[0][...]
@@ -196,26 +201,29 @@
     pc_up = pltpu.roll(pc, many - CAP, 0)
     for q in range(many // PACK):
         at = slice(q * PACK, (q + 1) * PACK)
-        back_ref[2 * q, :, :half] = even[at].astype(BF)
-        back_ref[2 * q, :, half:] = pc[at].astype(BF)
-        back_ref[2 * q + 1, :, :half] = odd[at].astype(BF)
-        back_ref[2 * q + 1, :, half:] = pc_up[at].astype(BF)
-
-
-def split_columns(rep_ref, grp_ref, near_ref, far_ref, width):
-    blocks = near_ref.shape[1] // width // 2
+        to = 2 * (ep_ref[0] ^ q if near else q)
+        back_ref[to, :, :half] = even[at].astype(BF)
+        back_ref[to, :, half:] = pc[at].astype(BF)
+        back_ref[to + 1, :, :half] = odd[at].astype(BF)
+        back_ref[to + 1, :, half:] = pc_up[at].astype(BF)
+
+
+def split_columns(rep_ref, grp_ref, recv_ref, width):
+    blocks = (recv_ref.shape[1] - LANES) // 3 // width
+    depth = 2 * blocks * width
     rep_high, grp = rep_ref[0] // blocks, grp_ref[0]
     keep, give = [], []
-
-    def owned(ref, at, side):
-        start = (2 * at + side) * width
-        return ref[:, start : start + width]
-
     for at in range(blocks):
-        mine = jnp.where(grp == 0, owned(near_ref, at, 0), owned(near_ref, at, 1))
-        theirs = jnp.where(grp == 0, owned(far_ref, at, 0), owned(far_ref, at, 1))
-        keep.append(jnp.where(rep_high == grp, mine, theirs))
-        give.append(jnp.where(rep_high == grp, theirs, mine))
+        start = 2 * at * width
+        near = jnp.where(
+            grp == 0,
+            recv_ref[:, start : start + width],
+            recv_ref[:, start + width : start + 2 * width],
+        )
+        start = depth + LANES + at * width
+        far = recv_ref[:, start : start + width]
+        keep.append(jnp.where(rep_high == grp, near, far))
+        give.append(jnp.where(rep_high == grp, far, near))
     return keep, give
 
 
@@ -337,24 +345,28 @@
     if middle < hidden:
         cuts = [slice(0, middle), slice(middle, hidden)]
     widths = [cut.stop - cut.start for cut in cuts]
-    paired = grp_size == 2 and rep_size % 2 == 0 and widths[0] == rep_size * owner_rows
-    side_width = depth + LANES + (0 if paired else rep_size * owner_rows)
+    paired = grp_size == 2 and ep_size == 4 and rep_size % 2 == 0
+    paired = paired and widths[0] == rep_size * owner_rows == depth
+    side_width = depth + LANES + rep_size * owner_rows // (2 if paired else 1)
     vmem = pl.BlockSpec(memory_space=pltpu.VMEM)
     hbm = pl.BlockSpec(memory_space=pltpu.HBM)
     ids = expert_ids.T
     w = jnp.transpose(weights, (1, 0, 2))
 
+    smem = pl.BlockSpec(memory_space=pltpu.SMEM)
     rep = lax.axis_index("rep").astype(jnp.int32).reshape(1)
+    ep = lax.axis_index("ep").astype(jnp.int32).reshape(1)
     grp = lax.axis_index("grp").astype(jnp.int32).reshape(1)
-    ids, rep, grp = lax.optimization_barrier((ids, rep, grp))
-    rows, slot_map = pl.pallas_call(
-        functools.partial(pack_kernel, grp_size=grp_size, owners=owners),
-        out_shape=(
-            jax.ShapeDtypeStruct((peers, PACK, side_width), BF),
-            jax.ShapeDtypeStruct((PACK, token_count), F32),
-        ),
-        in_specs=[hbm] * 4,
-        out_specs=(vmem,) * 2,
+    ids, rep, ep, grp = lax.optimization_barrier((ids, rep, ep, grp))
+    if paired:
+        row_shapes = (jax.ShapeDtypeStruct((PACK, side_width), BF),) * 2
+    else:
+        row_shapes = (jax.ShapeDtypeStruct((peers, PACK, side_width), BF),)
+    slot_map, *rows = pl.pallas_call(
+        functools.partial(pack_kernel, grp_size=grp_size, owners=owners, paired=paired),
+        out_shape=(jax.ShapeDtypeStruct((PACK, token_count), F32), *row_shapes),
+        in_specs=[smem] + [hbm] * 4,
+        out_specs=(vmem,) * (1 + len(row_shapes)),
         scratch_shapes=[
             pltpu.VMEM(ids.shape, ids.dtype),
             pltpu.VMEM(ids.shape, combine.dtype),
@@ -365,17 +377,28 @@
         compiler_params=pltpu.CompilerParams(vmem_limit_bytes=WHOLE),
         cost_estimate=cost(2_000_000_000),
         name="pack",
-    )(ids, combine.T, tokens, grad_out)
-
-    recv = lax.all_to_all(rows, ("ep", "grp"), 0, 0, tiled=True)
-    recv = recv.reshape(peers * PACK, side_width)
-
-    far_recv = None
+    )(grp, ids, combine.T, tokens, grad_out)
+
     if paired:
-        far_recv = lax.ppermute(recv, "grp", [(0, 1), (1, 0)])
-
-    source = recv
-    owns, nears, others = [], [], []
+        got = lax.ppermute(rows[1], "grp", [(0, 1), (1, 0)])
+        joined = pl.pallas_call(
+            join_kernel,
+            out_shape=jax.ShapeDtypeStruct((grp_size * PACK, side_width), BF),
+            in_specs=[smem] + [vmem] * 2,
+            out_specs=vmem,
+            compiler_params=pltpu.CompilerParams(vmem_limit_bytes=GRANT),
+            cost_estimate=cost(3_000_000_000),
+            name="join",
+        )(grp, rows[0], got)
+        sources = [joined]
+        for flip in range(1, ep_size):
+            pairs = [(i, i ^ flip) for i in range(ep_size)]
+            sources.append(lax.ppermute(joined, "ep", pairs))
+    else:
+        recv = lax.all_to_all(rows[0], ("ep", "grp"), 0, 0, tiled=True)
+        sources = [recv.reshape(peers * PACK, side_width)]
+
+    owns, others = [], []
     for c, width in enumerate(widths):
         first = c == 0
         extra = ()
@@ -383,32 +406,24 @@
             extra = (
                 jax.ShapeDtypeStruct((2, many, depth), BF),
                 jax.ShapeDtypeStruct((many, LANES), F32),
+                jax.ShapeDtypeStruct((peers * PACK, side_width), BF),
             )
-            if not paired:
-                cols_shape = (peers * PACK, rep_size * owner_rows)
-                extra += (jax.ShapeDtypeStruct(cols_shape, BF),)
-        own, send, near, *more = pl.pallas_call(
-            functools.partial(forward_kernel, cut=pl.ds(cuts[c].start, width), first=first),
+        own, send, *more = pl.pallas_call(
+            functools.partial(forward_kernel, inputs=len(sources), cut=cuts[c], first=first),
             out_shape=(
                 jax.ShapeDtypeStruct((3, many, width), F32),
                 jax.ShapeDtypeStruct((3, many, width), BF),
-                jax.ShapeDtypeStruct((2, depth, width), BF),
                 *extra,
             ),
-            in_specs=[vmem, hbm],
-            out_specs=(vmem,) * (3 + len(extra)),
-            scratch_shapes=[
-                pltpu.VMEM((depth, width), BF),
-                pltpu.SemaphoreType.DMA((3 * (depth // tile_of(depth, 256)),)),
-            ],
-            compiler_params=pltpu.CompilerParams(vmem_limit_bytes=WHOLE - (20 << 20)),
+            in_specs=[vmem] * (len(sources) + 1),
+            out_specs=(vmem,) * (2 + len(extra)),
+            compiler_params=pltpu.CompilerParams(vmem_limit_bytes=GRANT),
             cost_estimate=cost(3_000_000_000),
-        )(source, w)
+        )(*sources, w)
         if first:
-            source, scale = more[:2]
-            cols = more[2:]
+            source, scale, recv = more
+            sources = [source]
         owns.append(own)
-        nears.append(near)
         if grp_size == 2:
             others.append(lax.ppermute(send, "grp", [(0, 1), (1, 0)]))
         else:
@@ -421,16 +436,15 @@
         last = c == len(cuts) - 1
         fourth = paired and c == 0
         hid_shape = jax.ShapeDtypeStruct((3 + fourth, many, widths[c]), BF)
-        smem = pl.BlockSpec(memory_space=pltpu.SMEM)
         hid, pc, *give = pl.pallas_call(
             functools.partial(hidden_kernel, tile=tile, width=owner_rows if fourth else 0),
             out_shape=(hid_shape, jax.ShapeDtypeStruct((many, LANES), F32))
             + (hid_shape,) * fourth,
-            in_specs=[vmem] * 3 + [smem, smem, vmem, vmem] * fourth,
+            in_specs=[vmem] * 3 + [smem, smem, vmem] * fourth,
             out_specs=(vmem,) * (2 + fourth),
             compiler_params=pltpu.CompilerParams(vmem_limit_bytes=GRANT),
             cost_estimate=cost(1_000_000_000),
-        )(owns[c], others[c], scale, *((rep, grp, recv, far_recv) * fourth))
+        )(owns[c], others[c], scale, *((rep, grp, recv) * fourth))
         if last:
             shapes = jax.ShapeDtypeStruct((peers, PACK, depth // 2 + LANES), BF)
         else:
@@ -439,13 +453,15 @@
                 jax.ShapeDtypeStruct((many, LANES), F32),
             )
         back = pl.pallas_call(
-            functools.partial(return_kernel, first=c == 0, last=last),
+            functools.partial(
+                return_kernel, cut=cut, first=c == 0, last=last, near=paired
+            ),
             out_shape=shapes,
-            in_specs=[vmem] * (3 + len(back)),
+            in_specs=[smem] + [vmem] * (3 + len(back)),
             out_specs=vmem if last else (vmem,) * 2,
             compiler_params=pltpu.CompilerParams(vmem_limit_bytes=GRANT),
             cost_estimate=cost(3_000_000_000),
-        )(hid, pc, nears[c], *back)
+        )(ep, hid, pc, w, *back)
         gathered.append(gather(hid, rep_size, *give))
 
     turned = pl.pallas_call(
@@ -457,7 +473,7 @@
         compiler_params=pltpu.CompilerParams(vmem_limit_bytes=GRANT),
         cost_estimate=cost(500_000_000),
         name="turn",
-    )(rep, *(gathered[0] if paired else gather(cols[0], rep_size)))
+    )(rep, *(gathered[0] if paired else gather(recv[:, depth + LANES :], rep_size)))
 
     back_recv = lax.all_to_all(back, ("ep", "grp"), 0, 0, tiled=True)
 
@@ -509,6 +525,4 @@
         P(("rep", "ep", "grp"), None),
         P(("rep", "grp"), None, "ep"),
     )
-    return jax.shard_map(
-        local, mesh=mesh, in_specs=in_specs, out_specs=out_specs, check_vma=False
-    )
+    return jax.shard_map(local, mesh=mesh, in_specs=in_specs, out_specs=out_specs, check_vma=False)

time: 55.9 us -> 49.3 us (0.88)
  blocking collectives: 14.8 us -> 0 us
  starting transfers between devices: 10 us -> 17.4 us
  waiting for transfers between devices: 13.5 us -> 17.4 us
  Pallas kernels: 16.5 us -> 12.7 us
  local copies, waits for them, and re-layouts: 0.01 us -> 0.77 us
    all_to_all x1 -> x0, blocking collectives: 14.8 us -> none  [local(): recv = lax.all_to_all(rows, ('ep', 'grp'), 0, 0, tiled=True)]
    ppermute x1 -> x4, starting transfers between devices: 0.33 us -> 7.79 us  [the longest x3 4.73 us: local(): sources.append(lax.ppermute(joined, 'ep', pairs))]
    ppermute x1 -> x4, waiting for transfers between devices: 3.11 us -> 7.97 us  [the longest x3 5.93 us: local(): sources.append(lax.ppermute(joined, 'ep', pairs))]
    pallas_call x4 -> x5, Pallas kernels: 8.95 us -> 5.19 us  [the longest x2 2.98 us: local(): pl.pallas_call(functools.partial(return_kernel, cut=cut, first=c == 0, la...]
    ppermute x2, waiting for transfers between devices: 4.36 us -> 3.51 us  [local(): others.append(lax.ppermute(send, 'grp', [(0, 1), (1, 0)]))]
    unnamed x4 -> x8, local copies, waits for them, and re-layouts: 0.01 us -> 0.77 us
  transfers between devices with their start and end apart: 10 -> 13, of which waited for: 3 -> 6; matrix products, arithmetic and copies ran while one was open for 0% -> 0% of each run, Pallas kernels for 12% -> 14%
where the time goes in v5:
time: 49.3 us; the launch traced here: 49 us
  starting transfers between devices  17.4 us (35%)
  waiting for transfers between devices  17.4 us (35%)
  Pallas kernels  12.7 us (26%)
  local copies, waits for them, and re-layouts  0.77 us (2%)
  between operations  0.74 us (2%)
    ppermute x3, waiting for transfers between devices, local(): sources.append(lax.ppermute(joined, 'ep', pairs))  5.93 us
    all_to_all x1, waiting for transfers between devices, local(): back_recv = lax.all_to_all(back, ('ep', 'grp'), 0, 0, tiled=True)  5.89 us
    ppermute x3, starting transfers between devices, local(): sources.append(lax.ppermute(joined, 'ep', pairs))  4.73 us
    ppermute x6, starting transfers between devices, gather(): pieces = pieces + [lax.ppermute(held, 'rep', pairs) for held in sent]  4.18 us
    pallas_call x2, Pallas kernels, local(): pl.pallas_call(functools.partial(weight_kernel, cut=cut, tile=tile, membe...  3.7 us
    ppermute x2, waiting for transfers between devices, local(): others.append(lax.ppermute(send, 'grp', [(0, 1), (1, 0)]))  3.51 us
    all_to_all x1, starting transfers between devices, local(): back_recv = lax.all_to_all(back, ('ep', 'grp'), 0, 0, tiled=True)  3.36 us
    ppermute x1, starting transfers between devices, local(): got = lax.ppermute(rows[1], 'grp', [(0, 1), (1, 0)])  3.06 us
  transfers between devices with their start and end apart: 13, of which 6 were waited for; matrix products, arithmetic and copies ran while one was open for 0% of the time, Pallas kernels for 14%

profile of v5, /device:TPU:0, one launch (start us, length us, event | category | flops | bytes accessed | tf_op | source)
XLA Modules:
  0.0 49.0 jit_solution(15383758147106689968)
XLA Ops:
  0.6 2.1 %pack.1 = (f32[8,128]{1,0:T(8,128)}, bf16[8,1664]{1,0:T(8,128)(2,1)}, bf16[8,1664]{1,0:T(8,128)(2,1)}) custom-call(s32[1]{0:T(128)} %bitcast.3.refs_0_.grp_ref.refs_1_, s32[2,128]{1,0:T(2,128)} %bitcast.12, bf16[2,128]{1,0:T(2,128)(2,1)} %bitcast.15, bf16[128,2048]{1,0:T(8,128)(2,1)} %refs_3_.1, bf16[128,2048]{1,0:T(8,128)(2,1)} %refs_4_.1), custom_call_target="tpu_custom_call" | custom-call | flops 2000000000 | tf_op jit(solution)/shard_map/pack/pallas_call | solution.py:365
  2.8 3.1 %collective-permute-start = (bf16[8,1664]{1,0:T(8,128)(2,1)}, bf16[8,1664]{1,0:T(8,128)(2,1)S(1)}, u32[]{:S(2)}, u32[]{:S(2)}) collective-permute-start(bf16[8,1664]{1,0:T(8,128)(2,1)} %get-tuple-element.31), channel_id=1, source_target_pairs={{0,1},{1,0},{2,3},{3,2},{4,5},{5,4},{6,7},{7,6},{8,9},{9,8},{10,11... | collective-permute-start | bytes 79880 | tf_op jit(solution)/shard_map/ppermute | solution.py:383
  5.8 2.0 %collective-permute-done.got_ref = bf16[8,1664]{1,0:T(8,128)(2,1)S(1)} collective-permute-done((bf16[8,1664]{1,0:T(8,128)(2,1)}, bf16[8,1664]{1,0:T(8,128)(2,1)S(1)}, u32[]{:S(2)}, u32[]{:S(2)}) %collective-permute-start) | collective-permute-done | bytes 26656 | tf_op jit(solution)/shard_map/ppermute | solution.py:383
  7.9 0.7 %copy-done.2 = bf16[8,1664]{1,0:T(8,128)(2,1)S(1)} copy-done((bf16[8,1664]{1,0:T(8,128)(2,1)S(1)}, bf16[8,1664]{1,0:T(8,128)(2,1)}, u32[]{:S(2)}) %copy-start.2) | copy-done | bytes 26648
  8.6 2.1 %collective-permute-start.1 = (bf16[16,1664]{1,0:T(8,128)(2,1)S(1)}, bf16[16,1664]{1,0:T(8,128)(2,1)S(1)}, u32[]{:S(2)}, u32[]{:S(2)}) collective-permute-start(bf16[16,1664]{1,0:T(8,128)(2,1)S(1)} %join.1.refs_0_), channel_id=1, source_target_pairs={{0,2},{2,0},{4,6},{6,4},{1,3},{3,1},{5,7},{7,5},{8,10},{10,8},{12,... | collective-permute-start | bytes 159752 | tf_op jit(solution)/shard_map/ppermute | solution.py:396
  10.8 2.6 %collective-permute-start.2 = (bf16[16,1664]{1,0:T(8,128)(2,1)S(1)}, bf16[16,1664]{1,0:T(8,128)(2,1)S(1)}, u32[]{:S(2)}, u32[]{:S(2)}) collective-permute-start(bf16[16,1664]{1,0:T(8,128)(2,1)S(1)} %join.1.refs_0_), channel_id=1, source_target_pairs={{0,4},{2,6},{4,0},{6,2},{1,5},{3,7},{5,1},{7,3},{8,12},{10,14},{12... | collective-permute-start | bytes 159752 | tf_op jit(solution)/shard_map/ppermute | solution.py:396
  13.4 0.0 collective-permute-done.1.refs_1_
  13.4 3.6 %collective-permute-done.2.refs_2_ = bf16[16,1664]{1,0:T(8,128)(2,1)S(1)} collective-permute-done((bf16[16,1664]{1,0:T(8,128)(2,1)S(1)}, bf16[16,1664]{1,0:T(8,128)(2,1)S(1)}, u32[]{:S(2)}, u32[]{:S(2)}) %collective-permute-start.2) | collective-permute-done | bytes 53280 | tf_op jit(solution)/shard_map/ppermute | solution.py:396
  17.0 2.3 %collective-permute-done.3.refs_3_ = bf16[16,1664]{1,0:T(8,128)(2,1)S(1)} collective-permute-done((bf16[16,1664]{1,0:T(8,128)(2,1)S(1)}, bf16[16,1664]{1,0:T(8,128)(2,1)S(1)}, u32[]{:S(2)}, u32[]{:S(2)}) %collective-permute-start.3) | collective-permute-done | bytes 53280 | tf_op jit(solution)/shard_map/ppermute | solution.py:396
  19.3 1.3 %shard_map.76 = (f32[3,32,1024]{2,1,0:T(8,128)S(1)}, bf16[3,32,1024]{2,1,0:T(8,128)(2,1)S(1)}, bf16[2,32,1024]{2,1,0:T(8,128)(2,1)S(1)}, f32[32,128]{1,0:T(8,128)S(1)}, bf16[64,1664]{1,0:T(8,128)(2,1)S(1)}) custom-call(bf16[16,1664]{1,0:T(8,128)(2,1)S(1)} %join.1.refs_0_, bf16[16,1664]{1,0:T(8,128)(2,1)S(1)} %collective-permute-done.1.refs_1_, ...), custom_call_target="tpu_custom_call" | custom-call | flops 3000000000 | tf_op jit(solution)/shard_map/pallas_call | solution.py:411
  20.6 0.9 %shard_map.77 = (f32[3,32,768]{2,1,0:T(8,128)S(1)}, bf16[3,32,768]{2,1,0:T(8,128)(2,1)S(1)}) custom-call(bf16[2,32,1024]{2,1,0:T(8,128)(2,1)S(1)} %get-tuple-element.32.refs_0_, bf16[3,1024,1792]{2,1,0:T(8,128)(2,1)S(1)} %bitcast.9), custom_call_target="tpu_custom_call" | custom-call | flops 3000000000 | tf_op jit(solution)/shard_map/pallas_call | solution.py:411
  21.5 1.5 %collective-permute-start.4 = (bf16[3,32,768]{2,1,0:T(8,128)(2,1)S(1)}, bf16[3,32,768]{2,1,0:T(8,128)(2,1)S(1)}, u32[]{:S(2)}, u32[]{:S(2)}) collective-permute-start(bf16[3,32,768]{2,1,0:T(8,128)(2,1)S(1)} %get-tuple-element.34), channel_id=1, source_target_pairs={{0,1},{1,0},{2,3},{3,2},{4,5},{5,4},{6,7},{7,6},{8,9},{9,8},{10,11... | collective-permute-start | bytes 442376 | tf_op jit(solution)/shard_map/ppermute | solution.py:428
  23.0 0.5 %collective-permute-start.5 = (bf16[3,32,1024]{2,1,0:T(8,128)(2,1)S(1)}, bf16[3,32,1024]{2,1,0:T(8,128)(2,1)S(1)}, u32[]{:S(2)}, u32[]{:S(2)}) collective-permute-start(bf16[3,32,1024]{2,1,0:T(8,128)(2,1)S(1)} %get-tuple-element.39), channel_id=1, source_target_pairs={{0,1},{1,0},{2,3},{3,2},{4,5},{5,4},{6,7},{7,6},{8,9},{9,8},{10,11... | collective-permute-start | bytes 589832 | tf_op jit(solution)/shard_map/ppermute | solution.py:428
  23.6 3.1 %collective-permute-done.4.other_ref = bf16[3,32,768]{2,1,0:T(8,128)(2,1)S(1)} collective-permute-done((bf16[3,32,768]{2,1,0:T(8,128)(2,1)S(1)}, bf16[3,32,768]{2,1,0:T(8,128)(2,1)S(1)}, u32[]{:S(2)}, u32[]{:S(2)}) %collective-permute-start.4) | collective-permute-done | bytes 147488 | tf_op jit(solution)/shard_map/ppermute | solution.py:428
  26.7 0.1 shard_map.78
  26.8 1.6 %collective-permute-start.9 = (bf16[3,32,768]{2,1,0:T(8,128)(2,1)S(1)}, bf16[3,32,768]{2,1,0:T(8,128)(2,1)S(1)}, u32[]{:S(2)}, u32[]{:S(2)}) collective-permute-start(bf16[3,32,768]{2,1,0:T(8,128)(2,1)S(1)} %get-tuple-element.36.hid_ref.refs_0_), channel_id=1, source_target_pairs={{0,16},{8,24},{16,0},{24,8},{1,17},{9,25},{17,1},{25,9},{2,18},{10... | collective-permute-start | bytes 442376 | tf_op jit(solution)/shard_map/ppermute | solution.py:327
  28.4 0.4 collective-permute-done.5.other_ref
  28.8 0.2 shard_map.79
  29.0 1.6 %collective-permute-start.6 = (bf16[4,32,1024]{2,1,0:T(8,128)(2,1)S(1)}, bf16[4,32,1024]{2,1,0:T(8,128)(2,1)S(1)}, u32[]{:S(2)}, u32[]{:S(2)}) collective-permute-start(bf16[4,32,1024]{2,1,0:T(8,128)(2,1)S(1)} %get-tuple-element.48), channel_id=1, source_target_pairs={{0,16},{8,24},{16,0},{24,8},{1,17},{9,25},{17,1},{25,9},{2,18},{10... | collective-permute-start | bytes 786440 | tf_op jit(solution)/shard_map/ppermute | solution.py:327
  30.5 1.3 %shard_map.80 = (f32[32,1024]{1,0:T(8,128)S(1)}, f32[32,128]{1,0:T(8,128)S(1)}) custom-call(s32[1]{0:T(128)} %bitcast.2.ep_ref, bf16[4,32,1024]{2,1,0:T(8,128)(2,1)S(1)} %get-tuple-element.42.hid_ref.refs_0_, f32[32,128]{1,0:T(8,128)S(1)} %get-tuple-element.43.pc_ref, bf16[3,1024,1792]{2,1,0:T(8,128)(2,1)S(1)} %bitcast.10), custom_call_target="tpu_custom_call" | custom-call | flops 3000000000 | tf_op jit(solution)/shard_map/pallas_call | solution.py:455
  31.8 0.0 copy-start.3
  31.8 1.7 %shard_map.81 = bf16[8,8,640]{2,1,0:T(8,128)(2,1)} custom-call(s32[1]{0:T(128)} %bitcast.2.ep_ref, bf16[3,32,768]{2,1,0:T(8,128)(2,1)S(1)} %get-tuple-element.36.hid_ref.refs_0_, f32[32,128]{1,0:T(8,128)S(1)} %get-tuple-element.37.pc_ref, bf16[3,1024,1792]{2,1,0:T(8,128)(2,1)S(1)} %bitcast.11, f32[32,1024]{1,0:T(8,128)S(1)} %get-tuple-element.44.refs_0_, ...), custom_call_target="tpu_custom_call" | custom-call | flops 3000000000 | tf_op jit(solution)/shard_map/pallas_call | solution.py:455
  33.5 3.4 %all-to-all-start = ((bf16[8,8,640]{2,1,0:T(8,128)(2,1)}), bf16[8,8,640]{2,1,0:T(8,128)(2,1)S(1)}, u32[]{:S(2)}, u32[]{:S(2)}) async-start(bf16[8,8,640]{2,1,0:T(8,128)(2,1)} %shard_map.81), calls=%async_computation | async-start | bytes 163840 | tf_op jit(solution)/shard_map/all_to_all | solution.py:478
  36.9 0.1 collective-permute-start.7
  37.0 0.5 %collective-permute-start.8 = (bf16[4,32,1024]{2,1,0:T(8,128)(2,1)S(1)}, bf16[4,32,1024]{2,1,0:T(8,128)(2,1)S(1)}, u32[]{:S(2)}, u32[]{:S(2)}) collective-permute-start(bf16[4,32,1024]{2,1,0:T(8,128)(2,1)S(1)} %collective-permute-done.6.refs_1_), channel_id=1, source_target_pairs={{0,8},{8,0},{16,24},{24,16},{1,9},{9,1},{17,25},{25,17},{2,10},{10... | collective-permute-start | bytes 786440 | tf_op jit(solution)/shard_map/ppermute | solution.py:327
  37.5 0.1 collective-permute-start.10
  37.6 0.4 collective-permute-start.11
  38.0 5.9 %all-to-all-done.recv_ref = bf16[8,8,640]{2,1,0:T(8,128)(2,1)S(1)} async-done(((bf16[8,8,640]{2,1,0:T(8,128)(2,1)}), bf16[8,8,640]{2,1,0:T(8,128)(2,1)S(1)}, u32[]{:S(2)}, u32[]{:S(2)}) %all-to-all-start) | async-done | bytes 81952 | tf_op jit(solution)/shard_map/all_to_all | solution.py:478
  43.9 1.1 %token_.1 = (bf16[128,2048]{1,0:T(8,128)(2,1)}, f32[2,128]{1,0:T(2,128)}) custom-call(s32[2,128]{1,0:T(2,128)S(1)} %bitcast.13, f32[8,128]{1,0:T(8,128)S(1)} %copy-done.3, bf16[8,8,640]{2,1,0:T(8,128)(2,1)S(1)} %all-to-all-done.recv_ref), custom_call_target="tpu_custom_call" | custom-call | flops 2000000000 | tf_op jit(solution)/shard_map/token/pallas_call | solution.py:499
  45.0 0.2 turn.1.turned_ref
  45.2 2.0 %shard_map.82.refs_4_ = f32[3,256,1792]{2,1,0:T(8,128)} custom-call(bf16[2,256,128]{2,1,0:T(8,128)(2,1)S(1)} %turn.1.turned_ref, bf16[4,32,1024]{2,1,0:T(8,128)(2,1)S(1)} %get-tuple-element.42.hid_ref.refs_0_, bf16[4,32,1024]{2,1,0:T(8,128)(2,1)S(1)} %collective-permute-done.6.refs_1_, bf16[4,32,1024]{2,1,0:T(8,128)(2,1)S(1)} %collective-permute-done.7.refs_2_, ...), custom_call_target="tpu_custom_call" | custom-call | flops 3000000000 | tf_op jit(solution)/shard_map/pallas_call | solution.py:483
  47.2 1.7 %shard_map.83 = f32[3,256,1792]{2,1,0:T(8,128)} custom-call(bf16[2,256,128]{2,1,0:T(8,128)(2,1)S(1)} %turn.1.turned_ref, bf16[3,32,768]{2,1,0:T(8,128)(2,1)S(1)} %get-tuple-element.36.hid_ref.refs_0_, bf16[3,32,768]{2,1,0:T(8,128)(2,1)S(1)} %collective-permute-done.9.refs_1_, ...), custom_call_target="tpu_custom_call", output_to_operand_aliasing={{}: (5, {})} | custom-call | flops 3000000000 | tf_op jit(solution)/shard_map/pallas_call | solution.py:483
  (14 shorter events, 0.0 us)
Async XLA Ops:
  2.8 5.1 %collective-permute-start = (bf16[8,1664]{1,0:T(8,128)(2,1)}, bf16[8,1664]{1,0:T(8,128)(2,1)S(1)}, u32[]{:S(2)}, u32[]{:S(2)}) collective-permute-start(bf16[8,1664]{1,0:T(8,128)(2,1)} %get-tuple-element.31), channel_id=1, source_target_pairs={{0,1},{1,0},{2,3},{3,2},{4,5},{5,4},{6,7},{7,6},{8,9},{9,8},{10,11... | collective-permute-start | bytes 79880 | tf_op jit(solution)/shard_map/ppermute | solution.py:383
  7.9 0.7 %copy-start.2 = (bf16[8,1664]{1,0:T(8,128)(2,1)S(1)}, bf16[8,1664]{1,0:T(8,128)(2,1)}, u32[]{:S(2)}) copy-start(bf16[8,1664]{1,0:T(8,128)(2,1)} %get-tuple-element.30.mine_ref) | copy-start | bytes 79876
  8.6 10.7 %copy-start = (bf16[1024,3,1792]{2,0,1:T(8,128)(2,1)S(1)}, bf16[1024,3,1792]{2,0,1:T(8,128)(2,1)}, u32[]{:S(2)}) copy-start(bf16[1024,3,1792]{2,0,1:T(8,128)(2,1)} %param.9) | copy-start | bytes 33030148
  8.6 4.8 %collective-permute-start.1 = (bf16[16,1664]{1,0:T(8,128)(2,1)S(1)}, bf16[16,1664]{1,0:T(8,128)(2,1)S(1)}, u32[]{:S(2)}, u32[]{:S(2)}) collective-permute-start(bf16[16,1664]{1,0:T(8,128)(2,1)S(1)} %join.1.refs_0_), channel_id=1, source_target_pairs={{0,2},{2,0},{4,6},{6,4},{1,3},{3,1},{5,7},{7,5},{8,10},{10,8},{12,... | collective-permute-start | bytes 159752 | tf_op jit(solution)/shard_map/ppermute | solution.py:396
  10.8 6.2 %collective-permute-start.2 = (bf16[16,1664]{1,0:T(8,128)(2,1)S(1)}, bf16[16,1664]{1,0:T(8,128)(2,1)S(1)}, u32[]{:S(2)}, u32[]{:S(2)}) collective-permute-start(bf16[16,1664]{1,0:T(8,128)(2,1)S(1)} %join.1.refs_0_), channel_id=1, source_target_pairs={{0,4},{2,6},{4,0},{6,2},{1,5},{3,7},{5,1},{7,3},{8,12},{10,14},{12... | collective-permute-start | bytes 159752 | tf_op jit(solution)/shard_map/ppermute | solution.py:396
  13.4 5.9 %collective-permute-start.3 = (bf16[16,1664]{1,0:T(8,128)(2,1)S(1)}, bf16[16,1664]{1,0:T(8,128)(2,1)S(1)}, u32[]{:S(2)}, u32[]{:S(2)}) collective-permute-start(bf16[16,1664]{1,0:T(8,128)(2,1)S(1)} %join.1.refs_0_), channel_id=1, source_target_pairs={{0,6},{2,4},{4,2},{6,0},{1,7},{3,5},{5,3},{7,1},{8,14},{10,12},{12... | collective-permute-start | bytes 159752 | tf_op jit(solution)/shard_map/ppermute | solution.py:396
  21.5 5.2 %collective-permute-start.4 = (bf16[3,32,768]{2,1,0:T(8,128)(2,1)S(1)}, bf16[3,32,768]{2,1,0:T(8,128)(2,1)S(1)}, u32[]{:S(2)}, u32[]{:S(2)}) collective-permute-start(bf16[3,32,768]{2,1,0:T(8,128)(2,1)S(1)} %get-tuple-element.34), channel_id=1, source_target_pairs={{0,1},{1,0},{2,3},{3,2},{4,5},{5,4},{6,7},{7,6},{8,9},{9,8},{10,11... | collective-permute-start | bytes 442376 | tf_op jit(solution)/shard_map/ppermute | solution.py:428
  23.0 5.7 %collective-permute-start.5 = (bf16[3,32,1024]{2,1,0:T(8,128)(2,1)S(1)}, bf16[3,32,1024]{2,1,0:T(8,128)(2,1)S(1)}, u32[]{:S(2)}, u32[]{:S(2)}) collective-permute-start(bf16[3,32,1024]{2,1,0:T(8,128)(2,1)S(1)} %get-tuple-element.39), channel_id=1, source_target_pairs={{0,1},{1,0},{2,3},{3,2},{4,5},{5,4},{6,7},{7,6},{8,9},{9,8},{10,11... | collective-permute-start | bytes 589832 | tf_op jit(solution)/shard_map/ppermute | solution.py:428
  26.8 10.7 %collective-permute-start.9 = (bf16[3,32,768]{2,1,0:T(8,128)(2,1)S(1)}, bf16[3,32,768]{2,1,0:T(8,128)(2,1)S(1)}, u32[]{:S(2)}, u32[]{:S(2)}) collective-permute-start(bf16[3,32,768]{2,1,0:T(8,128)(2,1)S(1)} %get-tuple-element.36.hid_ref.refs_0_), channel_id=1, source_target_pairs={{0,16},{8,24},{16,0},{24,8},{1,17},{9,25},{17,1},{25,9},{2,18},{10... | collective-permute-start | bytes 442376 | tf_op jit(solution)/shard_map/ppermute | solution.py:327
  29.0 8.0 %collective-permute-start.6 = (bf16[4,32,1024]{2,1,0:T(8,128)(2,1)S(1)}, bf16[4,32,1024]{2,1,0:T(8,128)(2,1)S(1)}, u32[]{:S(2)}, u32[]{:S(2)}) collective-permute-start(bf16[4,32,1024]{2,1,0:T(8,128)(2,1)S(1)} %get-tuple-element.48), channel_id=1, source_target_pairs={{0,16},{8,24},{16,0},{24,8},{1,17},{9,25},{17,1},{25,9},{2,18},{10... | collective-permute-start | bytes 786440 | tf_op jit(solution)/shard_map/ppermute | solution.py:327
  31.8 12.0 %copy-start.1 = (s32[128,2]{0,1:T(2,128)S(1)}, s32[128,2]{0,1:T(2,128)}, u32[]{:S(2)}) copy-start(s32[128,2]{0,1:T(2,128)} %param.7) | copy-start | bytes 3076
  31.8 12.0 %copy-start.3 = (f32[8,128]{1,0:T(8,128)S(1)}, f32[8,128]{1,0:T(8,128)}, u32[]{:S(2)}) copy-start(f32[8,128]{1,0:T(8,128)} %get-tuple-element.28.slots_ref) | copy-start | bytes 12292
  33.5 10.3 %all-to-all-start = ((bf16[8,8,640]{2,1,0:T(8,128)(2,1)}), bf16[8,8,640]{2,1,0:T(8,128)(2,1)S(1)}, u32[]{:S(2)}, u32[]{:S(2)}) async-start(bf16[8,8,640]{2,1,0:T(8,128)(2,1)} %shard_map.81), calls=%async_computation | async-start | bytes 163840 | tf_op jit(solution)/shard_map/all_to_all | solution.py:478
  36.9 8.1 %collective-permute-start.7 = (bf16[4,32,1024]{2,1,0:T(8,128)(2,1)S(1)}, bf16[4,32,1024]{2,1,0:T(8,128)(2,1)S(1)}, u32[]{:S(2)}, u32[]{:S(2)}) collective-permute-start(bf16[4,32,1024]{2,1,0:T(8,128)(2,1)S(1)} %get-tuple-element.42.hid_ref.refs_0_), channel_id=1, source_target_pairs={{0,8},{8,0},{16,24},{24,16},{1,9},{9,1},{17,25},{25,17},{2,10},{10... | collective-permute-start | bytes 786440 | tf_op jit(solution)/shard_map/ppermute | solution.py:327
  37.0 8.0 %collective-permute-start.8 = (bf16[4,32,1024]{2,1,0:T(8,128)(2,1)S(1)}, bf16[4,32,1024]{2,1,0:T(8,128)(2,1)S(1)}, u32[]{:S(2)}, u32[]{:S(2)}) collective-permute-start(bf16[4,32,1024]{2,1,0:T(8,128)(2,1)S(1)} %collective-permute-done.6.refs_1_), channel_id=1, source_target_pairs={{0,8},{8,0},{16,24},{24,16},{1,9},{9,1},{17,25},{25,17},{2,10},{10... | collective-permute-start | bytes 786440 | tf_op jit(solution)/shard_map/ppermute | solution.py:327
  37.5 9.8 %collective-permute-start.10 = (bf16[3,32,768]{2,1,0:T(8,128)(2,1)S(1)}, bf16[3,32,768]{2,1,0:T(8,128)(2,1)S(1)}, u32[]{:S(2)}, u32[]{:S(2)}) collective-permute-start(bf16[3,32,768]{2,1,0:T(8,128)(2,1)S(1)} %get-tuple-element.36.hid_ref.refs_0_), channel_id=1, source_target_pairs={{0,8},{8,0},{16,24},{24,16},{1,9},{9,1},{17,25},{25,17},{2,10},{10... | collective-permute-start | bytes 442376 | tf_op jit(solution)/shard_map/ppermute | solution.py:327
  37.6 9.7 %collective-permute-start.11 = (bf16[3,32,768]{2,1,0:T(8,128)(2,1)S(1)}, bf16[3,32,768]{2,1,0:T(8,128)(2,1)S(1)}, u32[]{:S(2)}, u32[]{:S(2)}) collective-permute-start(bf16[3,32,768]{2,1,0:T(8,128)(2,1)S(1)} %collective-permute-done.9.refs_1_), channel_id=1, source_target_pairs={{0,8},{8,0},{16,24},{24,16},{1,9},{9,1},{17,25},{25,17},{2,10},{10... | collective-permute-start | bytes 442376 | tf_op jit(solution)/shard_map/ppermute | solution.py:327
